TPU v7x, 32 devices: a whole 2x2x4 slice. The times are simulated.
32 devices in a mesh: patch: 4 (over z), seq: 4 (over y, x), req: 2 (over core).
Axes of the slice: x: 2, y: 2, z: 4, core: 2. Of those that a mesh axis runs over, the one named last changes fastest.
Arguments:
- query: bfloat16 [4, 8, 3584], P(None, ('patch', 'req')), may hold values from -20 to 20
- text_cache: bfloat16 [4, 8, 3072, 1024], P(None, ('patch', 'req'), 'seq'), may hold values from -6 to 6
- text_len: int32 [8], P(('patch', 'req')), may hold values from 0 to 3072
- image_rows: bfloat16 [4, 8192, 1024], P(None, ('patch', 'seq', 'req')), may hold values from -6 to 6
- patch_map: int32 [8192], P(('patch', 'seq', 'req')), may hold values from 0 to 7, as said below
- image_places: int32 [8192], P(('patch', 'seq', 'req')), may hold values from 0 to 1023, as said below
Outputs:
- attended: bfloat16 [4, 8, 3584], P(None, ('patch', 'req'), 'seq')
- image_cache: bfloat16 [4, 8, 1024, 1024], P(None, ('patch', 'req'), 'seq')
Inputs may be any that keep to these rules, and one draw needn't show every extreme that they name: `patch_map`: each aligned block of 256 rows (the rows of one prefill device) holds exactly 32 rows of every request. `image_places`: together with patch_map every pair of request and position occurs exactly once. The rows of a device whose seq index is s have positions from s * 256 to (s + 1) * 256 - 1.
All inputs are finite; a program needn't handle non-finite values.
Results may differ from a plain program's by a relative error of at most 0.0026.
Values may be sent and summed in bfloat16 or wider, within the bound.
No kernel may reach another device: no remote copies, remote signals or barrier semaphores. Data moves between devices by JAX's collectives and lax.ppermute only.
A program may use at most 64 MiB of HBM per device.

v0:
```python
import functools
import math

import jax
import jax.numpy as jnp
from jax import lax
from jax.experimental import pallas as pl
from jax.experimental.pallas import tpu as pltpu
from jax.sharding import PartitionSpec as P


HEADS = 28
KV_HEADS = 4
HEAD_DIM = 128
LANES = 128
SUBLANES = 8
MASKED = -1e30

MOST_GROUPS = 16
VMEM_LIMIT = 16 * 1024 * 1024
WIDE_VMEM_LIMIT = 62 * 1024 * 1024


def gray(index):
    return index ^ (index >> 1)


def step_of(source, target, count):
    if count & (count - 1) == 0:
        return (gray(target) - gray(source) + count - 1) & (count - 1)
    return (target - source + count - 1) % count


def slot_choice(patch_count, req_count, owner, place):
    src_rows = owner.shape[1]
    per = src_rows // (patch_count * req_count)
    me = lax.axis_index("patch")
    mine = lax.axis_index("req")
    shape = (src_rows, src_rows)
    down = lax.broadcasted_iota(jnp.int32, shape, 0)
    across = lax.broadcasted_iota(jnp.int32, shape, 1)
    owner_row = jnp.broadcast_to(owner, shape)
    owner_col = jnp.sum(
        jnp.where(down == across, owner_row.astype(jnp.float32), 0.0), axis=1, keepdims=True
    ).astype(jnp.int32)
    ahead = (owner_row == owner_col) & (down < across)
    rank = jnp.sum(jnp.where(ahead, 1.0, 0.0), axis=0, keepdims=True).astype(jnp.int32)
    step = step_of(me, owner // req_count, patch_count)
    turn = (owner % req_count - mine + req_count) % req_count
    slot = (step * req_count + turn) * per + rank
    choose = jnp.where(down == slot, 1.0, 0.0).astype(jnp.bfloat16)
    local = place - lax.axis_index("seq") * src_rows
    line = lax.broadcasted_iota(jnp.int32, (SUBLANES, src_rows), 0)
    digits = jnp.where(line == 0, local & (LANES - 1), jnp.where(line == 1, local // LANES, 0))
    places = lax.dot_general(
        digits.astype(jnp.float32).astype(jnp.bfloat16),
        choose,
        (((1,), (1,)), ((), ())),
        preferred_element_type=jnp.float32,
    ).astype(jnp.bfloat16)
    return choose, places


def pack_slots(first, per, choose, places, layer_rows, layers, outs):
    for k, out in enumerate(outs):
        tile = (first + k) * per // LANES
        out[pl.ds(out.shape[0] - SUBLANES, SUBLANES), :] = places[
            :, tile * LANES : (tile + 1) * LANES
        ]
    taken = choose[first * per : (first + len(outs)) * per]
    for layer in range(layers):
        rows = layer_rows(layer)
        blocks = rows.shape[1] // LANES
        moved = jnp.dot(taken, rows, preferred_element_type=jnp.float32).astype(jnp.bfloat16)
        for k, out in enumerate(outs):
            for c in range(blocks):
                out[pl.ds((layer * blocks + c) * per, per), :] = moved[
                    k * per : (k + 1) * per, c * LANES : (c + 1) * LANES
                ]


def first_kernel(patch_count, req_count, map_hbm, place_hbm, rows_hbm, *refs):
    choose_ref, places_ref, *outs = refs[:-5]
    owner_ref, place_ref, rows_ref, small_sem, rows_sem = refs[-5:]
    layers, src_rows, _ = rows_hbm.shape
    small = [
        pltpu.make_async_copy(map_hbm, owner_ref, small_sem.at[0]),
        pltpu.make_async_copy(place_hbm, place_ref, small_sem.at[1]),
    ]
    loads = [
        pltpu.make_async_copy(rows_hbm.at[layer], rows_ref.at[layer], rows_sem.at[layer])
        for layer in range(layers)
    ]
    for copy in small + loads:
        copy.start()
    for copy in small:
        copy.wait()
    choose, places = slot_choice(patch_count, req_count, owner_ref[...], place_ref[...])
    choose_ref[...] = choose
    places_ref[...] = places

    def layer_rows(layer):
        loads[layer].wait()
        return rows_ref[layer]

    per = src_rows // (patch_count * req_count)
    pack_slots(0, per, choose, places, layer_rows, layers, outs)


def rest_kernel(first, per, choose_ref, places_ref, rows_ref, *outs):
    pack_slots(
        first,
        per,
        choose_ref[...],
        places_ref[...],
        lambda layer: rows_ref[layer],
        rows_ref.shape[0],
        outs,
    )


def group_rows(patch_map, image_places, image_rows, patch_count, req_count):
    layers, src_rows, width = image_rows.shape
    groups = patch_count * req_count
    per = src_rows // groups
    chunk = jax.ShapeDtypeStruct((layers * per * width // LANES + SUBLANES, LANES), jnp.bfloat16)
    hbm = pl.BlockSpec(memory_space=pltpu.HBM)
    vmem = pl.BlockSpec(memory_space=pltpu.VMEM)

    def cost(count):
        return pl.CostEstimate(
            flops=2 * layers * src_rows * per * count * width,
            bytes_accessed=2 * layers * (src_rows + per * count) * width,
            transcendentals=0,
        )

    choose, places, *first = pl.pallas_call(
        functools.partial(first_kernel, patch_count, req_count),
        out_shape=[
            jax.ShapeDtypeStruct((src_rows, src_rows), jnp.bfloat16),
            jax.ShapeDtypeStruct((SUBLANES, src_rows), jnp.bfloat16),
        ]
        + [chunk] * req_count,
        in_specs=[hbm] * 3,
        out_specs=[vmem] * (2 + req_count),
        scratch_shapes=[
            pltpu.VMEM((1, src_rows), jnp.int32),
            pltpu.VMEM((1, src_rows), jnp.int32),
            pltpu.VMEM(image_rows.shape, jnp.bfloat16),
            pltpu.SemaphoreType.DMA((2,)),
            pltpu.SemaphoreType.DMA((layers,)),
        ],
        cost_estimate=cost(req_count),
        compiler_params=pltpu.CompilerParams(vmem_limit_bytes=WIDE_VMEM_LIMIT),
        name="group_first",
    )(patch_map.reshape(1, src_rows), image_places.reshape(1, src_rows), image_rows)
    rest_call = pl.pallas_call(
        functools.partial(rest_kernel, req_count, per),
        out_shape=[chunk] * (groups - req_count),
        in_specs=[vmem] * 3,
        out_specs=[vmem] * (groups - req_count),
        cost_estimate=cost(groups - req_count),
        compiler_params=pltpu.CompilerParams(vmem_limit_bytes=VMEM_LIMIT),
        name="group_rest",
    )
    rest = rest_call(choose, places, image_rows)
    return [*first, *rest]


def heads_of(line, group):
    row = lax.broadcasted_iota(jnp.int32, (SUBLANES, HEAD_DIM), 0)
    tiles = []
    for g in range(KV_HEADS):
        tile = jnp.zeros((SUBLANES, HEAD_DIM), jnp.float32)
        for i in range(group):
            h = g * group + i
            tile = jnp.where(row == i, line[:, h * HEAD_DIM : (h + 1) * HEAD_DIM], tile)
        tiles.append(tile)
    return jnp.concatenate(tiles, axis=0).astype(jnp.bfloat16)


def attend(queries, keys, values, used, scale):
    scores = jnp.concatenate(
        [
            lax.dot_general(
                queries[g * SUBLANES : (g + 1) * SUBLANES],
                keys[g],
                (((1,), (1,)), ((), ())),
                preferred_element_type=jnp.float32,
            )
            for g in range(KV_HEADS)
        ],
        axis=0,
    )
    scores = scores * scale
    if used is not None:
        scores = jnp.where(used, scores, MASKED)
    top = jnp.max(scores, axis=1, keepdims=True)
    weights = jnp.exp(scores - top)
    if used is not None:
        weights = jnp.where(used, weights, 0.0)
    total = jnp.sum(weights, axis=1, keepdims=True)
    rounded = weights.astype(jnp.bfloat16)
    summed = jnp.concatenate(
        [
            jnp.dot(
                rounded[g * SUBLANES : (g + 1) * SUBLANES],
                values[g],
                preferred_element_type=jnp.float32,
            )
            for g in range(KV_HEADS)
        ],
        axis=0,
    )
    return top, total, summed


def text_kernel(scale, len_ref, query_ref, text_ref, q_ref, top_ref, total_ref, sum_ref):
    text_dev, width = text_ref.shape
    group = query_ref.shape[1] // HEAD_DIM // KV_HEADS
    queries = heads_of(query_ref[...].astype(jnp.float32), group)
    q_ref[...] = queries
    rows = KV_HEADS * SUBLANES
    positions = lax.axis_index("seq") * text_dev + lax.broadcasted_iota(
        jnp.int32, (rows, text_dev), 1
    )
    keys = [text_ref[:, g * HEAD_DIM : (g + 1) * HEAD_DIM] for g in range(KV_HEADS)]
    values = [
        text_ref[:, width // 2 + g * HEAD_DIM : width // 2 + (g + 1) * HEAD_DIM]
        for g in range(KV_HEADS)
    ]
    top, total, summed = attend(queries, keys, values, positions < len_ref[0], scale)
    top_ref[...] = jnp.broadcast_to(top, (rows, LANES))
    total_ref[...] = jnp.broadcast_to(total, (rows, LANES))
    sum_ref[...] = summed


def text_part(query, text_cache, text_len, scale):
    layers, _, query_width = query.shape
    text_dev, width = text_cache.shape[2:]
    rows = KV_HEADS * SUBLANES
    part = pl.BlockSpec((None, rows, LANES), lambda layer, _: (layer, 0, 0))
    return pl.pallas_call(
        functools.partial(text_kernel, scale),
        out_shape=[
            jax.ShapeDtypeStruct((layers, rows, HEAD_DIM), jnp.bfloat16),
            jax.ShapeDtypeStruct((layers, rows, LANES), jnp.float32),
            jax.ShapeDtypeStruct((layers, rows, LANES), jnp.float32),
            jax.ShapeDtypeStruct((layers, rows, HEAD_DIM), jnp.float32),
        ],
        grid_spec=pltpu.PrefetchScalarGridSpec(
            num_scalar_prefetch=1,
            grid=(layers,),
            in_specs=[
                pl.BlockSpec((None, 1, query_width), lambda layer, _: (layer, 0, 0)),
                pl.BlockSpec((None, None, text_dev, width), lambda layer, _: (layer, 0, 0, 0)),
            ],
            out_specs=[part] * 4,
        ),
        cost_estimate=pl.CostEstimate(
            flops=8 * layers * SUBLANES * LANES * text_dev * width,
            bytes_accessed=2 * layers * text_dev * width,
            transcendentals=layers * rows * text_dev,
        ),
        compiler_params=pltpu.CompilerParams(vmem_limit_bytes=VMEM_LIMIT),
        name="text_part",
    )(text_len, query, text_cache)


def image_layer(scale, layer, chunks, used, q_ref, top, total, summed):
    layers = q_ref.shape[0]
    blocks = 2 * KV_HEADS
    per = (chunks[0].shape[0] - SUBLANES) // layers // blocks

    def column(c):
        span = pl.ds((layer * blocks + c) * per, per)
        return jnp.concatenate([chunk[span, :] for chunk in chunks], axis=0)

    keys = [column(g) for g in range(KV_HEADS)]
    values = [column(KV_HEADS + g) for g in range(KV_HEADS)]
    new_top, new_total, new_summed = attend(q_ref[layer], keys, values, used, scale)
    both = jnp.maximum(top, new_top)
    old_factor = jnp.exp(top - both)
    new_factor = jnp.exp(new_top - both)
    total = old_factor * total + new_factor * new_total
    summed = old_factor * summed + new_factor * new_summed
    return both, total, summed


def pack_part(top, total, summed):
    row = lax.broadcasted_iota(jnp.int32, (SUBLANES, LANES), 0)
    lane = lax.broadcasted_iota(jnp.int32, (SUBLANES, LANES), 1)
    stats = jnp.where(lane == row, top, jnp.where(lane == row + LANES // 2, total, 0.0))
    stats = jnp.sum(stats, axis=0, keepdims=True)
    return jnp.where(row == SUBLANES - 1, stats, summed)


def unpack_part(tile):
    row = lax.broadcasted_iota(jnp.int32, (SUBLANES, LANES), 0)
    lane = lax.broadcasted_iota(jnp.int32, (SUBLANES, LANES), 1)
    stats = jnp.broadcast_to(tile[SUBLANES - 1 :, :], (SUBLANES, LANES))
    top = jnp.sum(jnp.where(lane == row, stats, 0.0), axis=1, keepdims=True)
    total = jnp.sum(jnp.where(lane == row + LANES // 2, stats, 0.0), axis=1, keepdims=True)
    return jnp.where(total > 0.0, top, MASKED), total, tile


def merge_tiles(tiles):
    parts = [unpack_part(tile) for tile in tiles]
    top = functools.reduce(jnp.maximum, [part[0] for part in parts])
    factors = [jnp.exp(part[0] - top) for part in parts]
    total = sum(factor * part[1] for factor, part in zip(factors, parts))
    summed = sum(factor * part[2] for factor, part in zip(factors, parts))
    return top, total, summed


def here_kernel(scale, groups, sure, outer, q_ref, top_in, total_in, sum_in, *refs):
    chunks, outs, packed = refs[:groups], refs[groups:-1], refs[-1]
    layers, rows = q_ref.shape[:2]
    per = (chunks[0].shape[0] - SUBLANES) // layers // (2 * KV_HEADS)
    patch = lax.axis_index("patch")
    limit = functools.reduce(
        lambda found, z: jnp.where(patch == z, groups * per, found), outer, sure * per
    )
    used = lax.broadcasted_iota(jnp.int32, (rows, groups * per), 1) < limit
    for layer in range(q_ref.shape[0]):
        top, total, summed = image_layer(
            scale,
            layer,
            chunks,
            used,
            q_ref,
            top_in[layer][:, :1],
            total_in[layer][:, :1],
            sum_in[layer],
        )
        for g in range(KV_HEADS):
            span = slice(g * SUBLANES, (g + 1) * SUBLANES)
            packed[g, pl.ds(layer * SUBLANES, SUBLANES), :] = pack_part(
                top[span], total[span], summed[span]
            )
    me = lax.axis_index("seq")
    for k in range(KV_HEADS):
        outs[k][...] = packed[me ^ k]


def far_kernel(scale, count, *refs):
    queries, chunks = refs[:count], refs[count : 2 * count]
    outs, packed = refs[2 * count : -1], refs[-1]
    layers = queries[0].shape[0]
    blocks = 2 * KV_HEADS
    group = queries[0].shape[1] // HEAD_DIM // KV_HEADS
    for n in range(count):
        chunk = chunks[n]
        per = (chunk.shape[0] - SUBLANES) // layers // blocks
        for layer in range(layers):
            columns = [
                chunk[pl.ds((layer * blocks + c) * per, per), :] for c in range(blocks)
            ]
            line = queries[n][pl.ds(layer, 1), :].astype(jnp.float32)
            top, total, summed = attend(
                heads_of(line, group), columns[:KV_HEADS], columns[KV_HEADS:], None, scale
            )
            for g in range(KV_HEADS):
                span = slice(g * SUBLANES, (g + 1) * SUBLANES)
                packed[g, pl.ds((n * layers + layer) * SUBLANES, SUBLANES), :] = pack_part(
                    top[span], total[span], summed[span]
                )
    me = lax.axis_index("seq")
    for k in range(KV_HEADS):
        outs[k][...] = packed[me ^ k]


def seq_parts(kernel, operands, part_rows, chunk_rows, groups):
    shape = (part_rows, LANES)
    vmem = pl.BlockSpec(memory_space=pltpu.VMEM)
    return pl.pallas_call(
        kernel,
        out_shape=[jax.ShapeDtypeStruct(shape, jnp.float32)] * KV_HEADS,
        in_specs=[vmem] * len(operands),
        out_specs=[vmem] * KV_HEADS,
        scratch_shapes=[pltpu.VMEM((KV_HEADS,) + shape, jnp.float32)],
        cost_estimate=pl.CostEstimate(
            flops=8 * SUBLANES * chunk_rows * LANES * groups,
            bytes_accessed=2 * chunk_rows * LANES * groups,
            transcendentals=SUBLANES * chunk_rows * groups,
        ),
        compiler_params=pltpu.CompilerParams(vmem_limit_bytes=VMEM_LIMIT),
    )(*operands)


def seq_exchange(outs):
    arrived = [
        lax.ppermute(out, "seq", [(s, s ^ k) for s in range(KV_HEADS)])
        for k, out in enumerate(outs)
        if k
    ]
    return [outs[0], *arrived]


def merge_far_kernel(count, *refs):
    parts, outs = refs[:-count], refs[-count:]
    rows = parts[0].shape[0] // count
    for n, out in enumerate(outs):
        for at in range(0, rows, SUBLANES):
            tiles = [part[pl.ds(n * rows + at, SUBLANES), :] for part in parts]
            out[pl.ds(at, SUBLANES), :] = pack_part(*merge_tiles(tiles))


def merge_far(parts, count):
    rows = parts[0].shape[0] // count
    vmem = pl.BlockSpec(memory_space=pltpu.VMEM)
    return pl.pallas_call(
        functools.partial(merge_far_kernel, count),
        out_shape=[jax.ShapeDtypeStruct((rows, LANES), jnp.float32)] * count,
        in_specs=[vmem] * len(parts),
        out_specs=[vmem] * count,
        compiler_params=pltpu.CompilerParams(vmem_limit_bytes=VMEM_LIMIT),
        name="merge_far",
    )(*parts)


def place_kernel(owners, *refs):
    out_hbm, out_ref, sems = refs[-3:]
    groups = len(owners)

    def rows_of(k, span):
        first, *others = [refs[n][span, :] for n in owners[k]]
        return sum(others, first)

    layers, band, width = out_ref.shape
    blocks = width // LANES
    per = band // groups
    stores = [
        pltpu.make_async_copy(out_ref.at[layer], out_hbm.at[layer], sems.at[layer])
        for layer in range(layers)
    ]
    base = layers * blocks * per
    lane = lax.broadcasted_iota(jnp.int32, (SUBLANES, LANES), 1)
    tiles = []
    for tile in range(band // LANES):
        row = jnp.zeros((SUBLANES, LANES), jnp.float32)
        for k in range(groups):
            if k * per // LANES == tile:
                extra = rows_of(k, pl.ds(base, SUBLANES)).astype(jnp.float32)
                inside = (lane >= k * per % LANES) & (lane < k * per % LANES + per)
                row = jnp.where(inside, extra, row)
        tiles.append(row)
    digits = jnp.concatenate(tiles, axis=1).astype(jnp.int32)
    places = digits[0:1] + digits[1:2] * LANES
    down = lax.broadcasted_iota(jnp.int32, (band, band), 0)
    choose = jnp.where(down == places, 1.0, 0.0).astype(jnp.bfloat16)
    for layer in range(layers):
        for c in range(blocks):
            span = pl.ds((layer * blocks + c) * per, per)
            column = jnp.concatenate([rows_of(k, span) for k in range(groups)], axis=0)
            out_ref[layer, :, c * LANES : (c + 1) * LANES] = jnp.dot(
                choose, column, preferred_element_type=jnp.float32
            ).astype(jnp.bfloat16)
        stores[layer].start()
    for store in stores:
        store.wait()


def place_rows(slots, layers, band, width):
    operands = [chunk for slot in slots for chunk in slot]
    count = iter(range(len(operands)))
    owners = [[next(count) for _ in slot] for slot in slots]
    vmem = pl.BlockSpec(memory_space=pltpu.VMEM)
    return pl.pallas_call(
        functools.partial(place_kernel, owners),
        out_shape=jax.ShapeDtypeStruct((layers, band, width), jnp.bfloat16),
        in_specs=[vmem] * len(operands),
        out_specs=pl.BlockSpec(memory_space=pltpu.HBM),
        scratch_shapes=[
            pltpu.VMEM((layers, band, width), jnp.bfloat16),
            pltpu.SemaphoreType.DMA((layers,)),
        ],
        cost_estimate=pl.CostEstimate(
            flops=2 * layers * band * band * width,
            bytes_accessed=4 * layers * band * width,
            transcendentals=0,
        ),
        compiler_params=pltpu.CompilerParams(vmem_limit_bytes=VMEM_LIMIT),
        name="place_rows",
    )(*operands)


def merge_kernel(group, *refs):
    parts, out_ref, lines = refs[:-2], refs[-2], refs[-1]
    for layer in range(out_ref.shape[0]):
        tiles = [part[pl.ds(layer * SUBLANES, SUBLANES), :] for part in parts]
        _, total, summed = merge_tiles(tiles)
        result = summed / total
        for i in range(group):
            lines[pl.ds(layer, 1), i * HEAD_DIM : (i + 1) * HEAD_DIM] = result[i : i + 1]
    out_ref[...] = lines[...].astype(jnp.bfloat16)


def merge(parts, layers, group):
    vmem = pl.BlockSpec(memory_space=pltpu.VMEM)
    return pl.pallas_call(
        functools.partial(merge_kernel, group),
        out_shape=jax.ShapeDtypeStruct((layers, group * HEAD_DIM), jnp.bfloat16),
        in_specs=[vmem] * len(parts),
        out_specs=vmem,
        scratch_shapes=[pltpu.VMEM((layers, group * HEAD_DIM), jnp.float32)],
        compiler_params=pltpu.CompilerParams(vmem_limit_bytes=VMEM_LIMIT),
        name="merge",
    )(*parts)


def exchange_pairs(patch_count, req_count, step, turn):
    pairs = []
    for patch in range(patch_count):
        for req in range(req_count):
            target = next(p for p in range(patch_count) if step_of(patch, p, patch_count) == step)
            pairs.append(
                (patch * req_count + req, target * req_count + (req + turn) % req_count)
            )
    return pairs


def fast_body(query, text_cache, text_len, image_rows, patch_map, image_places):
    layers = query.shape[0]
    patch_count = lax.axis_size("patch")
    req_count = lax.axis_size("req")
    band, width = image_rows.shape[1:]
    group = HEADS // KV_HEADS
    scale = 1.0 / math.sqrt(HEAD_DIM)
    slots = [[step * req_count + turn for turn in range(req_count)] for step in range(patch_count)]
    last = patch_count // 2 - 1
    late = slots[last]
    early = [k for step in range(patch_count - 1) if step != last for k in slots[step]]
    own, core = slots[-1][0], slots[-1][1:]
    pairs = [
        exchange_pairs(patch_count, req_count, k // req_count, k % req_count)
        for k in range(patch_count * req_count)
    ]
    axes = ("patch", "req")
    reach = {
        source: abs(target // req_count - source // req_count) for source, target in pairs[late[0]]
    }
    near = min(reach.values())
    outer = sorted({source // req_count for source, hops in reach.items() if hops > near})
    inner_pairs = {k: [pair for pair in pairs[k] if reach[pair[0]] == near] for k in late}
    outer_pairs = {k: [pair for pair in pairs[k] if reach[pair[0]] > near] for k in late}
    flat_query = query[:, 0]

    def send(value, some):
        return lax.ppermute(value, axes, some)

    far_queries = [
        send(flat_query, [(target, source) for source, target in inner_pairs[k]])
        for k in late
    ]
    grouped = group_rows(patch_map, image_places, image_rows, patch_count, req_count)
    arrived = {own: [grouped[own]]}
    for k in early + core:
        arrived[k] = [send(grouped[k], pairs[k])]
    for k in late:
        arrived[k] = [send(grouped[k], some) for some in (inner_pairs[k], outer_pairs[k]) if some]
    chunk_rows = grouped[0].shape[0]
    part_rows = layers * SUBLANES
    far = seq_parts(
        functools.partial(far_kernel, scale, len(late)),
        [*far_queries, *(grouped[k] for k in late)],
        len(late) * part_rows,
        chunk_rows,
        len(late),
    )
    far = merge_far(seq_exchange(far), len(late))
    far = [lax.ppermute(part, axes, inner_pairs[k]) for part, k in zip(far, late)]
    text = text_part(query, text_cache, text_len, scale)
    here = [arrived[k][0] for k in early + core + [own]]
    sure = len(here)
    here += [arrived[k][1] for k in late if outer]
    parts = seq_parts(
        functools.partial(here_kernel, scale, len(here), sure, outer),
        [*text, *here],
        part_rows,
        chunk_rows,
        len(here),
    )
    attended = merge([*seq_exchange(parts), *far], layers, group)
    image_cache = place_rows([arrived[k] for k in range(len(grouped))], layers, band, width)
    return attended[:, None, :], image_cache[:, None]


def plain_body(query, text_cache, text_len, image_rows, patch_map, image_places):
    layers, req_dev, query_width = query.shape
    text_dev = text_cache.shape[2]
    full_width = text_cache.shape[3]
    kv_width = full_width // 2
    head_dim = HEAD_DIM
    kv_heads = KV_HEADS
    heads = HEADS
    group = heads // kv_heads
    src_rows = image_rows.shape[1]
    patch_count = lax.axis_size("patch")
    req_count = lax.axis_size("req")
    seq_count = lax.axis_size("seq")
    seq_index = lax.axis_index("seq")
    per_source = src_rows // (patch_count * req_count * req_dev)
    band_size = per_source * patch_count * req_count
    scale = 1.0 / math.sqrt(head_dim)
    order = jnp.argsort(patch_map, stable=True)
    grouped = jnp.take(image_rows, order, axis=1)
    grouped_places = jnp.take(image_places, order)
    sending = grouped.reshape(layers, patch_count * req_count, req_dev, per_source, full_width)
    arrived = lax.all_to_all(sending, ("patch", "req"), split_axis=1, concat_axis=3, tiled=True)
    place_send = grouped_places.reshape(patch_count * req_count, req_dev, per_source)
    arrived_places = lax.all_to_all(
        place_send, ("patch", "req"), split_axis=0, concat_axis=2, tiled=True
    )
    image_block = arrived.reshape(layers, req_dev, band_size, full_width)
    local_places = arrived_places.reshape(req_dev, band_size) - seq_index * band_size
    inverse = jnp.argsort(local_places, axis=1)
    image_cache = jnp.take_along_axis(image_block, inverse[None, :, :, None], axis=2)
    queries = query.reshape(layers, req_dev, kv_heads, group, head_dim)
    text_keys = text_cache[..., :kv_width].reshape(layers, req_dev, text_dev, kv_heads, head_dim)
    text_values = text_cache[..., kv_width:].reshape(layers, req_dev, text_dev, kv_heads, head_dim)
    image_keys = image_block[..., :kv_width].reshape(layers, req_dev, band_size, kv_heads, head_dim)
    image_values = image_block[..., kv_width:].reshape(
        layers, req_dev, band_size, kv_heads, head_dim
    )
    positions = seq_index * text_dev + jnp.arange(text_dev, dtype=jnp.int32)
    used = positions[None, :] < text_len[:, None]
    text_raw = (
        jnp.einsum("lrkgd,lrtkd->lrkgt", queries, text_keys, preferred_element_type=jnp.float32)
        * scale
    )
    text_scores = jnp.where(used[None, :, None, None, :], text_raw, -jnp.inf)
    image_scores = (
        jnp.einsum("lrkgd,lrtkd->lrkgt", queries, image_keys, preferred_element_type=jnp.float32)
        * scale
    )
    local_top = jnp.maximum(jnp.max(text_scores, axis=-1), jnp.max(image_scores, axis=-1))
    text_weights = jnp.exp(text_scores - local_top[..., None])
    image_weights = jnp.exp(image_scores - local_top[..., None])
    local_total = jnp.sum(text_weights, axis=-1) + jnp.sum(image_weights, axis=-1)
    text_rounded = text_weights.astype(jnp.bfloat16)
    image_rounded = image_weights.astype(jnp.bfloat16)
    local_values = jnp.einsum(
        "lrkgt,lrtkd->lrkgd", image_rounded, image_values, preferred_element_type=jnp.float32
    )
    local_values = local_values + jnp.einsum(
        "lrkgt,lrtkd->lrkgd", text_rounded, text_values, preferred_element_type=jnp.float32
    )
    width_dev = query_width // seq_count
    top = lax.pmax(local_top, "seq")
    factor = jnp.exp(local_top - top)
    scaled_total = factor * local_total
    scaled_values = factor[..., None] * local_values
    total_sum, value_sum = lax.psum((scaled_total, scaled_values), "seq")
    result = (value_sum / total_sum[..., None]).reshape(layers, req_dev, query_width)
    attended = lax.dynamic_slice_in_dim(result, seq_index * width_dev, width_dev, 2).astype(
        jnp.bfloat16
    )
    return (attended, image_cache)


def body(query, text_cache, text_len, image_rows, patch_map, image_places):
    groups = lax.axis_size("patch") * lax.axis_size("req")
    band = image_rows.shape[1]
    per = band // groups
    fast = (
        query.shape[1] == 1
        and lax.axis_size("patch") >= 2
        and groups <= MOST_GROUPS
        and band == per * groups
        and band % LANES == 0
        and per % 16 == 0
        and LANES % per == 0
        and lax.axis_size("seq") == KV_HEADS
        and HEADS // KV_HEADS < SUBLANES
    )
    chosen = fast_body if fast else plain_body
    return chosen(query, text_cache, text_len, image_rows, patch_map, image_places)


def solution(mesh):
    return jax.shard_map(
        body,
        mesh=mesh,
        in_specs=(
            P(None, ("patch", "req"), None),
            P(None, ("patch", "req"), "seq", None),
            P(("patch", "req")),
            P(None, ("patch", "seq", "req"), None),
            P(("patch", "seq", "req")),
            P(("patch", "seq", "req")),
        ),
        out_specs=(P(None, ("patch", "req"), "seq"), P(None, ("patch", "req"), "seq", None)),
        check_vma=False,
    )
```

profile of v0, /device:TPU:8, one launch (start us, length us, event | category | flops | bytes accessed | tf_op | source)
XLA Modules:
  0.0 86.8 jit_solution(11171222559226658637)
XLA Ops:
  0.6 3.2 %group_first.1 = (bf16[256,256]{1,0:T(8,128)(2,1)}, bf16[8,256]{1,0:T(8,128)(2,1)}, bf16[1032,128]{1,0:T(8,128)(2,1)}, bf16[1032,128]{1,0:T(8,128)(2,1)}) custom-call(s32[1,256]{1,0:T(1,128)} %bitcast.11, s32[1,256]{1,0:T(1,128)} %bitcast.12, bf16[4,256,1024]{2,1,0:T(8,128)(2,1)} %rows_ref.1), custom_call_target="tpu_custom_call" | custom-call | flops 134217728 | bytes 2621440 | tf_op jit(solution)/shard_map/group_first/pallas_call | solution.py:137
  3.9 2.6 %collective-permute-start = (bf16[1032,128]{1,0:T(8,128)(2,1)}, bf16[1032,128]{1,0:T(8,128)(2,1)S(1)}, u32[]{:S(2)}, u32[]{:S(2)}) collective-permute-start(bf16[1032,128]{1,0:T(8,128)(2,1)} %get-tuple-element.30), channel_id=1, source_target_pairs={{0,8},{1,9},{8,24},{9,25},{16,0},{17,1},{24,16},{25,17},{2,10},{3,... | collective-permute-start | bytes 792584 | tf_op jit(solution)/shard_map/ppermute | solution.py:550
  6.5 0.0 collective-permute-start.1
  6.5 1.6 %copy-done = bf16[4,256,1024]{2,1,0:T(8,128)(2,1)S(1)} copy-done((bf16[4,256,1024]{2,1,0:T(8,128)(2,1)S(1)}, bf16[4,256,1024]{2,1,0:T(8,128)(2,1)}, u32[]{:S(2)}) %copy-start) | copy-done | bytes 2097176
  8.1 0.9 %copy-done.1 = bf16[256,256]{1,0:T(8,128)(2,1)S(1)} copy-done((bf16[256,256]{1,0:T(8,128)(2,1)S(1)}, bf16[256,256]{1,0:T(8,128)(2,1)}, u32[]{:S(2)}) %copy-start.1) | copy-done | bytes 131096
  9.0 0.7 copy-done.2
  9.7 0.6 group_rest.1
  10.3 1.2 %collective-permute-start.2 = (bf16[1032,128]{1,0:T(8,128)(2,1)S(1)}, bf16[1032,128]{1,0:T(8,128)(2,1)S(1)}, u32[]{:S(2)}, u32[]{:S(2)}) collective-permute-start(bf16[1032,128]{1,0:T(8,128)(2,1)S(1)} %get-tuple-element.34), channel_id=1, source_target_pairs={{0,16},{1,17},{8,0},{9,1},{16,24},{17,25},{24,8},{25,9},{2,18},{3,... | collective-permute-start | bytes 792584 | tf_op jit(solution)/shard_map/ppermute | solution.py:550
  11.5 0.6 collective-permute-start.3
  12.1 3.5 %collective-permute-start.10 = (bf16[4,3584]{1,0:T(4,128)(2,1)S(1)}, bf16[4,3584]{1,0:T(4,128)(2,1)S(1)}, u32[]{:S(2)}, u32[]{:S(2)}) collective-permute-start(bf16[4,3584]{1,0:T(4,128)(2,1)S(1)} %bitcast.8), channel_id=1, source_target_pairs={{16,8},{17,9},{8,16},{9,17},{18,10},{19,11},{10,18},{11,19},{20,12... | collective-permute-start | bytes 86024 | tf_op jit(solution)/shard_map/ppermute | solution.py:550
  15.6 14.3 %collective-permute-done.10.refs_0_ = bf16[4,3584]{1,0:T(4,128)(2,1)S(1)} collective-permute-done((bf16[4,3584]{1,0:T(4,128)(2,1)S(1)}, bf16[4,3584]{1,0:T(4,128)(2,1)S(1)}, u32[]{:S(2)}, u32[]{:S(2)}) %collective-permute-start.10) | collective-permute-done | bytes 28704 | tf_op jit(solution)/shard_map/ppermute | solution.py:550
  30.0 2.7 %collective-permute-start.11 = (bf16[4,3584]{1,0:T(4,128)(2,1)S(1)}, bf16[4,3584]{1,0:T(4,128)(2,1)S(1)}, u32[]{:S(2)}, u32[]{:S(2)}) collective-permute-start(bf16[4,3584]{1,0:T(4,128)(2,1)S(1)} %bitcast.9), channel_id=1, source_target_pairs={{17,8},{16,9},{9,16},{8,17},{19,10},{18,11},{11,18},{10,19},{21,12... | collective-permute-start | bytes 86024 | tf_op jit(solution)/shard_map/ppermute | solution.py:550
  32.6 10.6 %collective-permute-done.11.refs_1_ = bf16[4,3584]{1,0:T(4,128)(2,1)S(1)} collective-permute-done((bf16[4,3584]{1,0:T(4,128)(2,1)S(1)}, bf16[4,3584]{1,0:T(4,128)(2,1)S(1)}, u32[]{:S(2)}, u32[]{:S(2)}) %collective-permute-start.11) | collective-permute-done | bytes 28704 | tf_op jit(solution)/shard_map/ppermute | solution.py:550
  43.2 1.9 %shard_map.78 = (f32[64,128]{1,0:T(8,128)S(1)}, f32[64,128]{1,0:T(8,128)S(1)}, f32[64,128]{1,0:T(8,128)S(1)}, f32[64,128]{1,0:T(8,128)S(1)}) custom-call(bf16[4,3584]{1,0:T(4,128)(2,1)S(1)} %collective-permute-done.10.refs_0_, bf16[4,3584]{1,0:T(4,128)(2,1)S(1)} %collective-permute-done.11.refs_1_, bf16[1032,128]{1,0:T(8,128)(2,1)S(1)} %get-tuple-element.38.refs_2_, ...), custom_call_target="tpu_custom_call" | custom-call | flops 16908288 | bytes 528384 | tf_op jit(solution)/shard_map/pallas_call | solution.py:376
  45.2 1.7 %collective-permute-start.12 = (f32[64,128]{1,0:T(8,128)S(1)}, f32[64,128]{1,0:T(8,128)S(1)}, u32[]{:S(2)}, u32[]{:S(2)}) collective-permute-start(f32[64,128]{1,0:T(8,128)S(1)} %get-tuple-element.45), channel_id=1, source_target_pairs={{0,2},{2,0},{4,6},{6,4},{1,3},{3,1},{5,7},{7,5},{8,10},{10,8},{12,... | collective-permute-start | bytes 98312 | tf_op jit(solution)/shard_map/ppermute | solution.py:393
  46.8 2.3 %collective-permute-done.12.refs_1_ = f32[64,128]{1,0:T(8,128)S(1)} collective-permute-done((f32[64,128]{1,0:T(8,128)S(1)}, f32[64,128]{1,0:T(8,128)S(1)}, u32[]{:S(2)}, u32[]{:S(2)}) %collective-permute-start.12) | collective-permute-done | bytes 32800 | tf_op jit(solution)/shard_map/ppermute | solution.py:393
  49.1 1.6 %collective-permute-start.13 = (f32[64,128]{1,0:T(8,128)S(1)}, f32[64,128]{1,0:T(8,128)S(1)}, u32[]{:S(2)}, u32[]{:S(2)}) collective-permute-start(f32[64,128]{1,0:T(8,128)S(1)} %get-tuple-element.46), channel_id=1, source_target_pairs={{0,4},{2,6},{4,0},{6,2},{1,5},{3,7},{5,1},{7,3},{8,12},{10,14},{12... | collective-permute-start | bytes 98312 | tf_op jit(solution)/shard_map/ppermute | solution.py:393
  50.8 2.3 %collective-permute-done.13.refs_2_ = f32[64,128]{1,0:T(8,128)S(1)} collective-permute-done((f32[64,128]{1,0:T(8,128)S(1)}, f32[64,128]{1,0:T(8,128)S(1)}, u32[]{:S(2)}, u32[]{:S(2)}) %collective-permute-start.13) | collective-permute-done | bytes 32800 | tf_op jit(solution)/shard_map/ppermute | solution.py:393
  53.0 2.5 %collective-permute-start.14 = (f32[64,128]{1,0:T(8,128)S(1)}, f32[64,128]{1,0:T(8,128)S(1)}, u32[]{:S(2)}, u32[]{:S(2)}) collective-permute-start(f32[64,128]{1,0:T(8,128)S(1)} %get-tuple-element.47), channel_id=1, source_target_pairs={{0,6},{2,4},{4,2},{6,0},{1,7},{3,5},{5,3},{7,1},{8,14},{10,12},{12... | collective-permute-start | bytes 98312 | tf_op jit(solution)/shard_map/ppermute | solution.py:393
  56.3 1.6 %collective-permute-done.14.refs_3_ = f32[64,128]{1,0:T(8,128)S(1)} collective-permute-done((f32[64,128]{1,0:T(8,128)S(1)}, f32[64,128]{1,0:T(8,128)S(1)}, u32[]{:S(2)}, u32[]{:S(2)}) %collective-permute-start.14) | collective-permute-done | bytes 32800 | tf_op jit(solution)/shard_map/ppermute | solution.py:393
  57.9 0.7 collective-permute-start.5
  58.5 0.0 collective-permute-done.refs_0_
  58.5 0.7 collective-permute-start.6
  59.2 0.0 collective-permute-done.1.refs_1_
  59.2 4.5 %collective-permute-start.17 = (bf16[1032,128]{1,0:T(8,128)(2,1)S(1)}, bf16[1032,128]{1,0:T(8,128)(2,1)S(1)}, u32[]{:S(2)}, u32[]{:S(2)}) collective-permute-start(bf16[1032,128]{1,0:T(8,128)(2,1)S(1)} %get-tuple-element.38.refs_2_), channel_id=1, source_target_pairs={{8,16},{9,17},{16,8},{17,9},{10,18},{11,19},{18,10},{19,11},{12,20... | collective-permute-start | bytes 792584 | tf_op jit(solution)/shard_map/ppermute | solution.py:550
  63.8 0.0 collective-permute-done.2.refs_2_.refs_6_
  63.8 1.9 %collective-permute-start.18 = (bf16[1032,128]{1,0:T(8,128)(2,1)S(1)}, bf16[1032,128]{1,0:T(8,128)(2,1)S(1)}, u32[]{:S(2)}, u32[]{:S(2)}) collective-permute-start(bf16[1032,128]{1,0:T(8,128)(2,1)S(1)} %get-tuple-element.39.refs_3_), channel_id=1, source_target_pairs={{8,17},{9,16},{16,9},{17,8},{10,19},{11,18},{18,11},{19,10},{12,21... | collective-permute-start | bytes 792584 | tf_op jit(solution)/shard_map/ppermute | solution.py:550
  65.7 0.0 collective-permute-done.3.refs_3_.refs_7_
  65.7 0.2 collective-permute-start.4
  65.9 2.8 %copy-done.3 = bf16[4,1,768,1024]{3,2,1,0:T(8,128)(2,1)S(1)} copy-done((bf16[4,1,768,1024]{3,2,1,0:T(8,128)(2,1)S(1)}, bf16[4,1,768,1024]{3,2,1,0:T(8,128)(2,1)}, u32[]{:S(2)}) %copy-start.3) | copy-done | bytes 6291480
  68.7 2.3 %text_part.1 = (bf16[4,32,128]{2,1,0:T(8,128)(2,1)S(1)}, f32[4,32,128]{2,1,0:T(8,128)S(1)}, f32[4,32,128]{2,1,0:T(8,128)S(1)}, f32[4,32,128]{2,1,0:T(8,128)S(1)}) custom-call(s32[1]{0:T(128)S(6)} %copy.10.len_ref, bf16[4,1,3584]{2,1,0:T(2,128)(2,1)S(1)} %copy.8.query_ref, bf16[4,1,768,1024]{3,2,1,0:T(8,128)(2,1)S(1)} %copy-done.3), custom_call_target="tpu_custom_call" | custom-call | flops 25769803776 | bytes 6291456 | tf_op jit(solution)/shard_map/text_part/pallas_call | solution.py:243
  71.0 0.2 merge_far.1
  71.2 0.0 collective-permute-done.4.refs_4_.refs_9_
  71.2 3.9 %collective-permute-start.15 = (f32[32,128]{1,0:T(8,128)S(1)}, f32[32,128]{1,0:T(8,128)S(1)}, u32[]{:S(2)}, u32[]{:S(2)}) collective-permute-start(f32[32,128]{1,0:T(8,128)S(1)} %get-tuple-element.48), channel_id=1, source_target_pairs={{8,16},{9,17},{16,8},{17,9},{10,18},{11,19},{18,10},{19,11},{12,20... | collective-permute-start | bytes 49160 | tf_op jit(solution)/shard_map/ppermute | solution.py:572
  75.1 0.0 collective-permute-done.5.refs_6_.refs_3_
  75.1 1.9 %collective-permute-start.16 = (f32[32,128]{1,0:T(8,128)S(1)}, f32[32,128]{1,0:T(8,128)S(1)}, u32[]{:S(2)}, u32[]{:S(2)}) collective-permute-start(f32[32,128]{1,0:T(8,128)S(1)} %get-tuple-element.49), channel_id=1, source_target_pairs={{8,17},{9,16},{16,9},{17,8},{10,19},{11,18},{18,11},{19,10},{12,21... | collective-permute-start | bytes 49160 | tf_op jit(solution)/shard_map/ppermute | solution.py:572
  77.0 0.0 collective-permute-done.6.refs_7_.refs_5_
  77.1 1.3 %shard_map.77 = (f32[32,128]{1,0:T(8,128)S(1)}, f32[32,128]{1,0:T(8,128)S(1)}, f32[32,128]{1,0:T(8,128)S(1)}, f32[32,128]{1,0:T(8,128)S(1)}) custom-call(bf16[4,32,128]{2,1,0:T(8,128)(2,1)S(1)} %get-tuple-element.26.q_ref, f32[4,32,128]{2,1,0:T(8,128)S(1)} %get-tuple-element.27.top_in, f32[4,32,128]{2,1,0:T(8,128)S(1)} %get-tuple-element.28.total_in, ...), custom_call_target="tpu_custom_call" | custom-call | flops 67633152 | bytes 2113536 | tf_op jit(solution)/shard_map/pallas_call | solution.py:376
  78.3 1.6 %collective-permute-start.7 = (f32[32,128]{1,0:T(8,128)S(1)}, f32[32,128]{1,0:T(8,128)S(1)}, u32[]{:S(2)}, u32[]{:S(2)}) collective-permute-start(f32[32,128]{1,0:T(8,128)S(1)} %get-tuple-element.41), channel_id=1, source_target_pairs={{0,2},{2,0},{4,6},{6,4},{1,3},{3,1},{5,7},{7,5},{8,10},{10,8},{12,... | collective-permute-start | bytes 49160 | tf_op jit(solution)/shard_map/ppermute | solution.py:393
  79.9 0.0 collective-permute-done.17.refs_2_
  79.9 1.5 %collective-permute-start.8 = (f32[32,128]{1,0:T(8,128)S(1)}, f32[32,128]{1,0:T(8,128)S(1)}, u32[]{:S(2)}, u32[]{:S(2)}) collective-permute-start(f32[32,128]{1,0:T(8,128)S(1)} %get-tuple-element.42), channel_id=1, source_target_pairs={{0,4},{2,6},{4,0},{6,2},{1,5},{3,7},{5,1},{7,3},{8,12},{10,14},{12... | collective-permute-start | bytes 49160 | tf_op jit(solution)/shard_map/ppermute | solution.py:393
  81.4 0.0 collective-permute-done.18.refs_4_
  81.4 0.5 collective-permute-start.9
  81.9 2.1 %place_rows.1 = bf16[4,256,1024]{2,1,0:T(8,128)(2,1)} custom-call(bf16[1032,128]{1,0:T(8,128)(2,1)S(1)} %collective-permute-done.refs_0_, bf16[1032,128]{1,0:T(8,128)(2,1)S(1)} %collective-permute-done.1.refs_1_, bf16[1032,128]{1,0:T(8,128)(2,1)S(1)} %collective-permute-done.17.refs_2_, bf16[1032,128]{1,0:T(8,128)(2,1)S(1)} %collective-permute-done.5.refs_6_.refs_3_, ...), custom_call_target="tpu_custom_call" | custom-call | flops 536870912 | bytes 4194304 | tf_op jit(solution)/shard_map/place_rows/pallas_call | solution.py:469
  84.0 0.0 collective-permute-done.15.refs_4_
  84.0 0.0 collective-permute-done.8.refs_2_
  84.0 2.0 %collective-permute-done.9.refs_3_ = f32[32,128]{1,0:T(8,128)S(1)} collective-permute-done((f32[32,128]{1,0:T(8,128)S(1)}, f32[32,128]{1,0:T(8,128)S(1)}, u32[]{:S(2)}, u32[]{:S(2)}) %collective-permute-start.9) | collective-permute-done | bytes 16416 | tf_op jit(solution)/shard_map/ppermute | solution.py:393
  86.1 0.8 merge.1
  (9 shorter events, 0.1 us)
Async XLA Ops:
  0.6 11.5 %copy-start.4 = (bf16[4,1,3584]{2,0,1:T(4,128)(2,1)S(1)}, bf16[4,1,3584]{2,0,1:T(4,128)(2,1)}, u32[]{:S(2)}) copy-start(bf16[4,1,3584]{2,0,1:T(4,128)(2,1)} %param.6) | copy-start | bytes 86020
  3.9 54.7 %collective-permute-start = (bf16[1032,128]{1,0:T(8,128)(2,1)}, bf16[1032,128]{1,0:T(8,128)(2,1)S(1)}, u32[]{:S(2)}, u32[]{:S(2)}) collective-permute-start(bf16[1032,128]{1,0:T(8,128)(2,1)} %get-tuple-element.30), channel_id=1, source_target_pairs={{0,8},{1,9},{8,24},{9,25},{16,0},{17,1},{24,16},{25,17},{2,10},{3,... | collective-permute-start | bytes 792584 | tf_op jit(solution)/shard_map/ppermute | solution.py:550
  6.5 52.7 %collective-permute-start.1 = (bf16[1032,128]{1,0:T(8,128)(2,1)}, bf16[1032,128]{1,0:T(8,128)(2,1)S(1)}, u32[]{:S(2)}, u32[]{:S(2)}) collective-permute-start(bf16[1032,128]{1,0:T(8,128)(2,1)} %get-tuple-element.31), channel_id=1, source_target_pairs={{0,9},{1,8},{8,25},{9,24},{16,1},{17,0},{24,17},{25,16},{2,11},{3,... | collective-permute-start | bytes 792584 | tf_op jit(solution)/shard_map/ppermute | solution.py:550
  6.5 1.6 %copy-start = (bf16[4,256,1024]{2,1,0:T(8,128)(2,1)S(1)}, bf16[4,256,1024]{2,1,0:T(8,128)(2,1)}, u32[]{:S(2)}) copy-start(bf16[4,256,1024]{2,1,0:T(8,128)(2,1)} %rows_ref.1) | copy-start | bytes 6291460
  8.1 0.9 %copy-start.1 = (bf16[256,256]{1,0:T(8,128)(2,1)S(1)}, bf16[256,256]{1,0:T(8,128)(2,1)}, u32[]{:S(2)}) copy-start(bf16[256,256]{1,0:T(8,128)(2,1)} %get-tuple-element.32.choose_ref) | copy-start | bytes 393220
  9.0 0.7 copy-start.2
  10.3 53.5 %collective-permute-start.2 = (bf16[1032,128]{1,0:T(8,128)(2,1)S(1)}, bf16[1032,128]{1,0:T(8,128)(2,1)S(1)}, u32[]{:S(2)}, u32[]{:S(2)}) collective-permute-start(bf16[1032,128]{1,0:T(8,128)(2,1)S(1)} %get-tuple-element.34), channel_id=1, source_target_pairs={{0,16},{1,17},{8,0},{9,1},{16,24},{17,25},{24,8},{25,9},{2,18},{3,... | collective-permute-start | bytes 792584 | tf_op jit(solution)/shard_map/ppermute | solution.py:550
  11.5 54.2 %collective-permute-start.3 = (bf16[1032,128]{1,0:T(8,128)(2,1)S(1)}, bf16[1032,128]{1,0:T(8,128)(2,1)S(1)}, u32[]{:S(2)}, u32[]{:S(2)}) collective-permute-start(bf16[1032,128]{1,0:T(8,128)(2,1)S(1)} %get-tuple-element.35), channel_id=1, source_target_pairs={{0,17},{1,16},{8,1},{9,0},{16,25},{17,24},{24,9},{25,8},{2,19},{3,... | collective-permute-start | bytes 792584 | tf_op jit(solution)/shard_map/ppermute | solution.py:550
  12.1 17.8 %collective-permute-start.10 = (bf16[4,3584]{1,0:T(4,128)(2,1)S(1)}, bf16[4,3584]{1,0:T(4,128)(2,1)S(1)}, u32[]{:S(2)}, u32[]{:S(2)}) collective-permute-start(bf16[4,3584]{1,0:T(4,128)(2,1)S(1)} %bitcast.8), channel_id=1, source_target_pairs={{16,8},{17,9},{8,16},{9,17},{18,10},{19,11},{10,18},{11,19},{20,12... | collective-permute-start | bytes 86024 | tf_op jit(solution)/shard_map/ppermute | solution.py:550
  30.0 13.3 %collective-permute-start.11 = (bf16[4,3584]{1,0:T(4,128)(2,1)S(1)}, bf16[4,3584]{1,0:T(4,128)(2,1)S(1)}, u32[]{:S(2)}, u32[]{:S(2)}) collective-permute-start(bf16[4,3584]{1,0:T(4,128)(2,1)S(1)} %bitcast.9), channel_id=1, source_target_pairs={{17,8},{16,9},{9,16},{8,17},{19,10},{18,11},{11,18},{10,19},{21,12... | collective-permute-start | bytes 86024 | tf_op jit(solution)/shard_map/ppermute | solution.py:550
  45.2 4.0 %collective-permute-start.12 = (f32[64,128]{1,0:T(8,128)S(1)}, f32[64,128]{1,0:T(8,128)S(1)}, u32[]{:S(2)}, u32[]{:S(2)}) collective-permute-start(f32[64,128]{1,0:T(8,128)S(1)} %get-tuple-element.45), channel_id=1, source_target_pairs={{0,2},{2,0},{4,6},{6,4},{1,3},{3,1},{5,7},{7,5},{8,10},{10,8},{12,... | collective-permute-start | bytes 98312 | tf_op jit(solution)/shard_map/ppermute | solution.py:393
  49.1 3.9 %collective-permute-start.13 = (f32[64,128]{1,0:T(8,128)S(1)}, f32[64,128]{1,0:T(8,128)S(1)}, u32[]{:S(2)}, u32[]{:S(2)}) collective-permute-start(f32[64,128]{1,0:T(8,128)S(1)} %get-tuple-element.46), channel_id=1, source_target_pairs={{0,4},{2,6},{4,0},{6,2},{1,5},{3,7},{5,1},{7,3},{8,12},{10,14},{12... | collective-permute-start | bytes 98312 | tf_op jit(solution)/shard_map/ppermute | solution.py:393
  53.0 4.8 %collective-permute-start.14 = (f32[64,128]{1,0:T(8,128)S(1)}, f32[64,128]{1,0:T(8,128)S(1)}, u32[]{:S(2)}, u32[]{:S(2)}) collective-permute-start(f32[64,128]{1,0:T(8,128)S(1)} %get-tuple-element.47), channel_id=1, source_target_pairs={{0,6},{2,4},{4,2},{6,0},{1,7},{3,5},{5,3},{7,1},{8,14},{10,12},{12... | collective-permute-start | bytes 98312 | tf_op jit(solution)/shard_map/ppermute | solution.py:393
  57.9 17.2 %collective-permute-start.5 = (bf16[1032,128]{1,0:T(8,128)(2,1)S(1)}, bf16[1032,128]{1,0:T(8,128)(2,1)S(1)}, u32[]{:S(2)}, u32[]{:S(2)}) collective-permute-start(bf16[1032,128]{1,0:T(8,128)(2,1)S(1)} %get-tuple-element.38.refs_2_), channel_id=1, source_target_pairs={{0,24},{1,25},{24,0},{25,1},{2,26},{3,27},{26,2},{27,3},{4,28},{5,... | collective-permute-start | bytes 792584 | tf_op jit(solution)/shard_map/ppermute | solution.py:550
  58.5 18.5 %collective-permute-start.6 = (bf16[1032,128]{1,0:T(8,128)(2,1)S(1)}, bf16[1032,128]{1,0:T(8,128)(2,1)S(1)}, u32[]{:S(2)}, u32[]{:S(2)}) collective-permute-start(bf16[1032,128]{1,0:T(8,128)(2,1)S(1)} %get-tuple-element.39.refs_3_), channel_id=1, source_target_pairs={{0,25},{1,24},{24,1},{25,0},{2,27},{3,26},{26,3},{27,2},{4,29},{5,... | collective-permute-start | bytes 792584 | tf_op jit(solution)/shard_map/ppermute | solution.py:550
  59.2 20.7 %collective-permute-start.17 = (bf16[1032,128]{1,0:T(8,128)(2,1)S(1)}, bf16[1032,128]{1,0:T(8,128)(2,1)S(1)}, u32[]{:S(2)}, u32[]{:S(2)}) collective-permute-start(bf16[1032,128]{1,0:T(8,128)(2,1)S(1)} %get-tuple-element.38.refs_2_), channel_id=1, source_target_pairs={{8,16},{9,17},{16,8},{17,9},{10,18},{11,19},{18,10},{19,11},{12,20... | collective-permute-start | bytes 792584 | tf_op jit(solution)/shard_map/ppermute | solution.py:550
  63.8 17.7 %collective-permute-start.18 = (bf16[1032,128]{1,0:T(8,128)(2,1)S(1)}, bf16[1032,128]{1,0:T(8,128)(2,1)S(1)}, u32[]{:S(2)}, u32[]{:S(2)}) collective-permute-start(bf16[1032,128]{1,0:T(8,128)(2,1)S(1)} %get-tuple-element.39.refs_3_), channel_id=1, source_target_pairs={{8,17},{9,16},{16,9},{17,8},{10,19},{11,18},{18,11},{19,10},{12,21... | collective-permute-start | bytes 792584 | tf_op jit(solution)/shard_map/ppermute | solution.py:550
  65.7 5.5 %collective-permute-start.4 = (bf16[1032,128]{1,0:T(8,128)(2,1)S(1)}, bf16[1032,128]{1,0:T(8,128)(2,1)S(1)}, u32[]{:S(2)}, u32[]{:S(2)}) collective-permute-start(bf16[1032,128]{1,0:T(8,128)(2,1)S(1)} %get-tuple-element.36), channel_id=1, source_target_pairs={{0,1},{1,0},{8,9},{9,8},{16,17},{17,16},{24,25},{25,24},{2,3},{3,2... | collective-permute-start | bytes 792584 | tf_op jit(solution)/shard_map/ppermute | solution.py:550
  65.9 2.8 %copy-start.3 = (bf16[4,1,768,1024]{3,2,1,0:T(8,128)(2,1)S(1)}, bf16[4,1,768,1024]{3,2,1,0:T(8,128)(2,1)}, u32[]{:S(2)}) copy-start(bf16[4,1,768,1024]{3,2,1,0:T(8,128)(2,1)} %text_ref.1) | copy-start | bytes 18874372
  71.2 12.8 %collective-permute-start.15 = (f32[32,128]{1,0:T(8,128)S(1)}, f32[32,128]{1,0:T(8,128)S(1)}, u32[]{:S(2)}, u32[]{:S(2)}) collective-permute-start(f32[32,128]{1,0:T(8,128)S(1)} %get-tuple-element.48), channel_id=1, source_target_pairs={{8,16},{9,17},{16,8},{17,9},{10,18},{11,19},{18,10},{19,11},{12,20... | collective-permute-start | bytes 49160 | tf_op jit(solution)/shard_map/ppermute | solution.py:572
  75.1 8.9 %collective-permute-start.16 = (f32[32,128]{1,0:T(8,128)S(1)}, f32[32,128]{1,0:T(8,128)S(1)}, u32[]{:S(2)}, u32[]{:S(2)}) collective-permute-start(f32[32,128]{1,0:T(8,128)S(1)} %get-tuple-element.49), channel_id=1, source_target_pairs={{8,17},{9,16},{16,9},{17,8},{10,19},{11,18},{18,11},{19,10},{12,21... | collective-permute-start | bytes 49160 | tf_op jit(solution)/shard_map/ppermute | solution.py:572
  78.3 5.7 %collective-permute-start.7 = (f32[32,128]{1,0:T(8,128)S(1)}, f32[32,128]{1,0:T(8,128)S(1)}, u32[]{:S(2)}, u32[]{:S(2)}) collective-permute-start(f32[32,128]{1,0:T(8,128)S(1)} %get-tuple-element.41), channel_id=1, source_target_pairs={{0,2},{2,0},{4,6},{6,4},{1,3},{3,1},{5,7},{7,5},{8,10},{10,8},{12,... | collective-permute-start | bytes 49160 | tf_op jit(solution)/shard_map/ppermute | solution.py:393
  79.9 4.1 %collective-permute-start.8 = (f32[32,128]{1,0:T(8,128)S(1)}, f32[32,128]{1,0:T(8,128)S(1)}, u32[]{:S(2)}, u32[]{:S(2)}) collective-permute-start(f32[32,128]{1,0:T(8,128)S(1)} %get-tuple-element.42), channel_id=1, source_target_pairs={{0,4},{2,6},{4,0},{6,2},{1,5},{3,7},{5,1},{7,3},{8,12},{10,14},{12... | collective-permute-start | bytes 49160 | tf_op jit(solution)/shard_map/ppermute | solution.py:393
  81.4 4.6 %collective-permute-start.9 = (f32[32,128]{1,0:T(8,128)S(1)}, f32[32,128]{1,0:T(8,128)S(1)}, u32[]{:S(2)}, u32[]{:S(2)}) collective-permute-start(f32[32,128]{1,0:T(8,128)S(1)} %get-tuple-element.43), channel_id=1, source_target_pairs={{0,6},{2,4},{4,2},{6,0},{1,7},{3,5},{5,3},{7,1},{8,14},{10,12},{12... | collective-permute-start | bytes 49160 | tf_op jit(solution)/shard_map/ppermute | solution.py:393
where the time goes:
time: 87.2 us; the launch traced here: 86.8 us
  starting transfers between devices  33.8 us (39%)
  waiting for transfers between devices  33.2 us (38%)
  Pallas kernels  12.3 us (14%)
  local copies, waits for them, and re-layouts  6.01 us (7%)
  between operations  1.5 us (2%)
    ppermute x11, waiting for transfers between devices, send(): return lax.ppermute(value, axes, some)  25 us
    ppermute x11, starting transfers between devices, send(): return lax.ppermute(value, axes, some)  18.6 us
    ppermute x6, starting transfers between devices, seq_exchange(): lax.ppermute(out, 'seq', [(s, s ^ k) for s in range(KV_HEADS)])  9.38 us
    ppermute x6, waiting for transfers between devices, seq_exchange(): lax.ppermute(out, 'seq', [(s, s ^ k) for s in range(KV_HEADS)])  8.21 us
    unnamed x11, local copies, waits for them, and re-layouts  6.01 us
    ppermute x2, starting transfers between devices, fast_body(): lax.ppermute(part, axes, inner_pairs[k])  5.84 us
    pallas_call x1, Pallas kernels, group_rows(): pl.pallas_call(functools.partial(first_kernel, patch_count, req_count), o...  3.21 us
    pallas_call x2, Pallas kernels, seq_parts(): pl.pallas_call(kernel, out_shape=[jax.ShapeDtypeStruct(shape, jnp.float32...  3.19 us
  transfers between devices with their start and end apart: 19, of which 6 were waited for; matrix products, arithmetic and copies ran while one was open for 0% of the time, Pallas kernels for 10%

commit v1 on v0

--- a/solution.py
+++ b/solution.py
@@ -134,7 +134,7 @@
             transcendentals=0,
         )
 
-    choose, places, *first = pl.pallas_call(
+    first_call = pl.pallas_call(
         functools.partial(first_kernel, patch_count, req_count),
         out_shape=[
             jax.ShapeDtypeStruct((src_rows, src_rows), jnp.bfloat16),
@@ -153,7 +153,10 @@
         cost_estimate=cost(req_count),
         compiler_params=pltpu.CompilerParams(vmem_limit_bytes=WIDE_VMEM_LIMIT),
         name="group_first",
-    )(patch_map.reshape(1, src_rows), image_places.reshape(1, src_rows), image_rows)
+    )
+    choose, places, *first = first_call(
+        patch_map.reshape(1, src_rows), image_places.reshape(1, src_rows), image_rows
+    )
     rest_call = pl.pallas_call(
         functools.partial(rest_kernel, req_count, per),
         out_shape=[chunk] * (groups - req_count),
@@ -301,11 +304,14 @@
     stats = jnp.broadcast_to(tile[SUBLANES - 1 :, :], (SUBLANES, LANES))
     top = jnp.sum(jnp.where(lane == row, stats, 0.0), axis=1, keepdims=True)
     total = jnp.sum(jnp.where(lane == row + LANES // 2, stats, 0.0), axis=1, keepdims=True)
-    return jnp.where(total > 0.0, top, MASKED), total, tile
-
-
-def merge_tiles(tiles):
+    return top, total, tile
+
+
+def merge_tiles(tiles, used=None):
     parts = [unpack_part(tile) for tile in tiles]
+    for n, part in enumerate(parts):
+        if used is not None and used[n] is not None:
+            parts[n] = [jnp.where(used[n], a, b) for a, b in zip(part, (MASKED, 0.0, 0.0))]
     top = functools.reduce(jnp.maximum, [part[0] for part in parts])
     factors = [jnp.exp(part[0] - top) for part in parts]
     total = sum(factor * part[1] for factor, part in zip(factors, parts))
@@ -317,10 +323,7 @@
     chunks, outs, packed = refs[:groups], refs[groups:-1], refs[-1]
     layers, rows = q_ref.shape[:2]
     per = (chunks[0].shape[0] - SUBLANES) // layers // (2 * KV_HEADS)
-    patch = lax.axis_index("patch")
-    limit = functools.reduce(
-        lambda found, z: jnp.where(patch == z, groups * per, found), outer, sure * per
-    )
+    limit = jnp.where(is_outer(outer), groups, sure) * per
     used = lax.broadcasted_iota(jnp.int32, (rows, groups * per), 1) < limit
     for layer in range(q_ref.shape[0]):
         top, total, summed = image_layer(
@@ -419,13 +422,19 @@
     )(*parts)
 
 
-def place_kernel(owners, *refs):
+def is_outer(outer):
+    patch = lax.axis_index("patch")
+    return functools.reduce(jnp.logical_or, [patch == z for z in outer])
+
+
+def place_kernel(owners, outer, *refs):
     out_hbm, out_ref, sems = refs[-3:]
     groups = len(owners)
+    outside = is_outer(outer)
 
     def rows_of(k, span):
         first, *others = [refs[n][span, :] for n in owners[k]]
-        return sum(others, first)
+        return jnp.where(outside, others[0], first) if others else first
 
     layers, band, width = out_ref.shape
     blocks = width // LANES
@@ -461,13 +470,13 @@
         store.wait()
 
 
-def place_rows(slots, layers, band, width):
+def place_rows(slots, outer, layers, band, width):
     operands = [chunk for slot in slots for chunk in slot]
     count = iter(range(len(operands)))
     owners = [[next(count) for _ in slot] for slot in slots]
     vmem = pl.BlockSpec(memory_space=pltpu.VMEM)
     return pl.pallas_call(
-        functools.partial(place_kernel, owners),
+        functools.partial(place_kernel, owners, outer),
         out_shape=jax.ShapeDtypeStruct((layers, band, width), jnp.bfloat16),
         in_specs=[vmem] * len(operands),
         out_specs=pl.BlockSpec(memory_space=pltpu.HBM),
@@ -485,21 +494,23 @@
     )(*operands)
 
 
-def merge_kernel(group, *refs):
+def merge_kernel(group, sure, outer, *refs):
     parts, out_ref, lines = refs[:-2], refs[-2], refs[-1]
+    inside = jnp.logical_not(is_outer(outer))
+    used = [None if n < sure else inside for n in range(len(parts))]
     for layer in range(out_ref.shape[0]):
         tiles = [part[pl.ds(layer * SUBLANES, SUBLANES), :] for part in parts]
-        _, total, summed = merge_tiles(tiles)
+        _, total, summed = merge_tiles(tiles, used)
         result = summed / total
         for i in range(group):
             lines[pl.ds(layer, 1), i * HEAD_DIM : (i + 1) * HEAD_DIM] = result[i : i + 1]
     out_ref[...] = lines[...].astype(jnp.bfloat16)
 
 
-def merge(parts, layers, group):
+def merge(parts, sure, outer, layers, group):
     vmem = pl.BlockSpec(memory_space=pltpu.VMEM)
     return pl.pallas_call(
-        functools.partial(merge_kernel, group),
+        functools.partial(merge_kernel, group, sure, outer),
         out_shape=jax.ShapeDtypeStruct((layers, group * HEAD_DIM), jnp.bfloat16),
         in_specs=[vmem] * len(parts),
         out_specs=vmem,
@@ -542,8 +553,12 @@
     }
     near = min(reach.values())
     outer = sorted({source // req_count for source, hops in reach.items() if hops > near})
-    inner_pairs = {k: [pair for pair in pairs[k] if reach[pair[0]] == near] for k in late}
-    outer_pairs = {k: [pair for pair in pairs[k] if reach[pair[0]] > near] for k in late}
+
+    def stay(pair):
+        return (pair[0], pair[0] // req_count * req_count + pair[1] % req_count)
+
+    inner_pairs = {k: [p if reach[p[0]] == near else stay(p) for p in pairs[k]] for k in late}
+    outer_pairs = {k: [p if reach[p[0]] > near else stay(p) for p in pairs[k]] for k in late}
     flat_query = query[:, 0]
 
     def send(value, some):
@@ -558,7 +573,7 @@
     for k in early + core:
         arrived[k] = [send(grouped[k], pairs[k])]
     for k in late:
-        arrived[k] = [send(grouped[k], some) for some in (inner_pairs[k], outer_pairs[k]) if some]
+        arrived[k] = [send(grouped[k], some) for some in (inner_pairs[k], outer_pairs[k])]
     chunk_rows = grouped[0].shape[0]
     part_rows = layers * SUBLANES
     far = seq_parts(
@@ -573,7 +588,7 @@
     text = text_part(query, text_cache, text_len, scale)
     here = [arrived[k][0] for k in early + core + [own]]
     sure = len(here)
-    here += [arrived[k][1] for k in late if outer]
+    here += [arrived[k][1] for k in late]
     parts = seq_parts(
         functools.partial(here_kernel, scale, len(here), sure, outer),
         [*text, *here],
@@ -581,8 +596,10 @@
         chunk_rows,
         len(here),
     )
-    attended = merge([*seq_exchange(parts), *far], layers, group)
-    image_cache = place_rows([arrived[k] for k in range(len(grouped))], layers, band, width)
+    attended = merge([*seq_exchange(parts), *far], KV_HEADS, outer, layers, group)
+    image_cache = place_rows(
+        [arrived[k] for k in range(len(grouped))], outer, layers, band, width
+    )
     return attended[:, None, :], image_cache[:, None]
 
 
@@ -665,7 +682,7 @@
     per = band // groups
     fast = (
         query.shape[1] == 1
-        and lax.axis_size("patch") >= 2
+        and lax.axis_size("patch") == 4
         and groups <= MOST_GROUPS
         and band == per * groups
         and band % LANES == 0

time: 87.2 us -> 74.3 us (0.85)
  waiting for transfers between devices: 33.2 us -> 26.4 us
  starting transfers between devices: 33.8 us -> 27.8 us
    ppermute x11, waiting for transfers between devices: 25 us -> 18.4 us  [send(): return lax.ppermute(value, axes, some)]
    ppermute x11, starting transfers between devices: 18.6 us -> 14.4 us  [send(): return lax.ppermute(value, axes, some)]
    ppermute x2, starting transfers between devices: 5.84 us -> 3.84 us  [fast_body(): lax.ppermute(part, axes, inner_pairs[k])]
  transfers between devices with their start and end apart: 19 -> 19, of which waited for: 6 -> 6; matrix products, arithmetic and copies ran while one was open for 0% -> 0% of each run, Pallas kernels for 10% -> 11%
where the time goes in v1:
time: 74.3 us; the launch traced here: 74 us
  starting transfers between devices  27.8 us (37%)
  waiting for transfers between devices  26.4 us (36%)
  Pallas kernels  12.3 us (17%)
  local copies, waits for them, and re-layouts  6.01 us (8%)
  between operations  1.48 us (2%)
    ppermute x11, waiting for transfers between devices, send(): return lax.ppermute(value, axes, some)  18.4 us
    ppermute x11, starting transfers between devices, send(): return lax.ppermute(value, axes, some)  14.4 us
    ppermute x6, starting transfers between devices, seq_exchange(): lax.ppermute(out, 'seq', [(s, s ^ k) for s in range(KV_HEADS)])  9.61 us
    ppermute x6, waiting for transfers between devices, seq_exchange(): lax.ppermute(out, 'seq', [(s, s ^ k) for s in range(KV_HEADS)])  7.97 us
    unnamed x11, local copies, waits for them, and re-layouts  6.01 us
    ppermute x2, starting transfers between devices, fast_body(): lax.ppermute(part, axes, inner_pairs[k])  3.84 us
    pallas_call x1, Pallas kernels, group_rows(): first_call(patch_map.reshape(1, src_rows), image_places.reshape(1, src_ro...  3.21 us
    pallas_call x2, Pallas kernels, seq_parts(): pl.pallas_call(kernel, out_shape=[jax.ShapeDtypeStruct(shape, jnp.float32...  3.19 us
  transfers between devices with their start and end apart: 19, of which 6 were waited for; matrix products, arithmetic and copies ran while one was open for 0% of the time, Pallas kernels for 11%

profile of v1, /device:TPU:8, one launch (start us, length us, event | category | flops | bytes accessed | tf_op | source)
XLA Modules:
  0.0 74.0 jit_solution(14755778362898415743)
XLA Ops:
  0.6 3.2 %group_first.1 = (bf16[256,256]{1,0:T(8,128)(2,1)}, bf16[8,256]{1,0:T(8,128)(2,1)}, bf16[1032,128]{1,0:T(8,128)(2,1)}, bf16[1032,128]{1,0:T(8,128)(2,1)}) custom-call(s32[1,256]{1,0:T(1,128)} %bitcast.11, s32[1,256]{1,0:T(1,128)} %bitcast.12, bf16[4,256,1024]{2,1,0:T(8,128)(2,1)} %rows_ref.1), custom_call_target="tpu_custom_call" | custom-call | flops 134217728 | bytes 2621440 | tf_op jit(solution)/shard_map/group_first/pallas_call | solution.py:157
  3.9 2.6 %collective-permute-start = (bf16[1032,128]{1,0:T(8,128)(2,1)}, bf16[1032,128]{1,0:T(8,128)(2,1)S(1)}, u32[]{:S(2)}, u32[]{:S(2)}) collective-permute-start(bf16[1032,128]{1,0:T(8,128)(2,1)} %get-tuple-element.30), channel_id=1, source_target_pairs={{0,8},{1,9},{8,24},{9,25},{16,0},{17,1},{24,16},{25,17},{2,10},{3,... | collective-permute-start | bytes 792584 | tf_op jit(solution)/shard_map/ppermute | solution.py:565
  6.5 0.0 collective-permute-start.1
  6.5 1.6 %copy-done = bf16[4,256,1024]{2,1,0:T(8,128)(2,1)S(1)} copy-done((bf16[4,256,1024]{2,1,0:T(8,128)(2,1)S(1)}, bf16[4,256,1024]{2,1,0:T(8,128)(2,1)}, u32[]{:S(2)}) %copy-start) | copy-done | bytes 2097176
  8.1 0.9 %copy-done.1 = bf16[256,256]{1,0:T(8,128)(2,1)S(1)} copy-done((bf16[256,256]{1,0:T(8,128)(2,1)S(1)}, bf16[256,256]{1,0:T(8,128)(2,1)}, u32[]{:S(2)}) %copy-start.1) | copy-done | bytes 131096
  9.0 0.7 copy-done.2
  9.7 0.6 group_rest.1
  10.3 1.2 %collective-permute-start.2 = (bf16[1032,128]{1,0:T(8,128)(2,1)S(1)}, bf16[1032,128]{1,0:T(8,128)(2,1)S(1)}, u32[]{:S(2)}, u32[]{:S(2)}) collective-permute-start(bf16[1032,128]{1,0:T(8,128)(2,1)S(1)} %get-tuple-element.34), channel_id=1, source_target_pairs={{0,16},{1,17},{8,0},{9,1},{16,24},{17,25},{24,8},{25,9},{2,18},{3,... | collective-permute-start | bytes 792584 | tf_op jit(solution)/shard_map/ppermute | solution.py:565
  11.5 0.6 collective-permute-start.3
  12.1 3.5 %collective-permute-start.10 = (bf16[4,3584]{1,0:T(4,128)(2,1)S(1)}, bf16[4,3584]{1,0:T(4,128)(2,1)S(1)}, u32[]{:S(2)}, u32[]{:S(2)}) collective-permute-start(bf16[4,3584]{1,0:T(4,128)(2,1)S(1)} %bitcast.8), channel_id=1, source_target_pairs={{0,0},{1,1},{16,8},{17,9},{8,16},{9,17},{24,24},{25,25},{2,2},{3,3... | collective-permute-start | bytes 86024 | tf_op jit(solution)/shard_map/ppermute | solution.py:565
  15.6 14.3 %collective-permute-done.10.refs_0_ = bf16[4,3584]{1,0:T(4,128)(2,1)S(1)} collective-permute-done((bf16[4,3584]{1,0:T(4,128)(2,1)S(1)}, bf16[4,3584]{1,0:T(4,128)(2,1)S(1)}, u32[]{:S(2)}, u32[]{:S(2)}) %collective-permute-start.10) | collective-permute-done | bytes 28704 | tf_op jit(solution)/shard_map/ppermute | solution.py:565
  30.0 0.8 %collective-permute-start.11 = (bf16[4,3584]{1,0:T(4,128)(2,1)S(1)}, bf16[4,3584]{1,0:T(4,128)(2,1)S(1)}, u32[]{:S(2)}, u32[]{:S(2)}) collective-permute-start(bf16[4,3584]{1,0:T(4,128)(2,1)S(1)} %bitcast.9), channel_id=1, source_target_pairs={{1,0},{0,1},{17,8},{16,9},{9,16},{8,17},{25,24},{24,25},{3,2},{2,3... | collective-permute-start | bytes 86024 | tf_op jit(solution)/shard_map/ppermute | solution.py:565
  30.7 4.1 %collective-permute-done.11.refs_1_ = bf16[4,3584]{1,0:T(4,128)(2,1)S(1)} collective-permute-done((bf16[4,3584]{1,0:T(4,128)(2,1)S(1)}, bf16[4,3584]{1,0:T(4,128)(2,1)S(1)}, u32[]{:S(2)}, u32[]{:S(2)}) %collective-permute-start.11) | collective-permute-done | bytes 28704 | tf_op jit(solution)/shard_map/ppermute | solution.py:565
  34.8 1.9 %shard_map.78 = (f32[64,128]{1,0:T(8,128)S(1)}, f32[64,128]{1,0:T(8,128)S(1)}, f32[64,128]{1,0:T(8,128)S(1)}, f32[64,128]{1,0:T(8,128)S(1)}) custom-call(bf16[4,3584]{1,0:T(4,128)(2,1)S(1)} %collective-permute-done.10.refs_0_, bf16[4,3584]{1,0:T(4,128)(2,1)S(1)} %collective-permute-done.11.refs_1_, bf16[1032,128]{1,0:T(8,128)(2,1)S(1)} %get-tuple-element.38.refs_2_, ...), custom_call_target="tpu_custom_call" | custom-call | flops 16908288 | bytes 528384 | tf_op jit(solution)/shard_map/pallas_call | solution.py:379
  36.7 1.6 %collective-permute-start.12 = (f32[64,128]{1,0:T(8,128)S(1)}, f32[64,128]{1,0:T(8,128)S(1)}, u32[]{:S(2)}, u32[]{:S(2)}) collective-permute-start(f32[64,128]{1,0:T(8,128)S(1)} %get-tuple-element.45), channel_id=1, source_target_pairs={{0,2},{2,0},{4,6},{6,4},{1,3},{3,1},{5,7},{7,5},{8,10},{10,8},{12,... | collective-permute-start | bytes 98312 | tf_op jit(solution)/shard_map/ppermute | solution.py:396
  38.3 2.4 %collective-permute-done.12.refs_1_ = f32[64,128]{1,0:T(8,128)S(1)} collective-permute-done((f32[64,128]{1,0:T(8,128)S(1)}, f32[64,128]{1,0:T(8,128)S(1)}, u32[]{:S(2)}, u32[]{:S(2)}) %collective-permute-start.12) | collective-permute-done | bytes 32800 | tf_op jit(solution)/shard_map/ppermute | solution.py:396
  40.7 1.5 %collective-permute-start.13 = (f32[64,128]{1,0:T(8,128)S(1)}, f32[64,128]{1,0:T(8,128)S(1)}, u32[]{:S(2)}, u32[]{:S(2)}) collective-permute-start(f32[64,128]{1,0:T(8,128)S(1)} %get-tuple-element.46), channel_id=1, source_target_pairs={{0,4},{2,6},{4,0},{6,2},{1,5},{3,7},{5,1},{7,3},{8,12},{10,14},{12... | collective-permute-start | bytes 98312 | tf_op jit(solution)/shard_map/ppermute | solution.py:396
  42.2 2.4 %collective-permute-done.13.refs_2_ = f32[64,128]{1,0:T(8,128)S(1)} collective-permute-done((f32[64,128]{1,0:T(8,128)S(1)}, f32[64,128]{1,0:T(8,128)S(1)}, u32[]{:S(2)}, u32[]{:S(2)}) %collective-permute-start.13) | collective-permute-done | bytes 32800 | tf_op jit(solution)/shard_map/ppermute | solution.py:396
  44.6 2.5 %collective-permute-start.14 = (f32[64,128]{1,0:T(8,128)S(1)}, f32[64,128]{1,0:T(8,128)S(1)}, u32[]{:S(2)}, u32[]{:S(2)}) collective-permute-start(f32[64,128]{1,0:T(8,128)S(1)} %get-tuple-element.47), channel_id=1, source_target_pairs={{0,6},{2,4},{4,2},{6,0},{1,7},{3,5},{5,3},{7,1},{8,14},{10,12},{12... | collective-permute-start | bytes 98312 | tf_op jit(solution)/shard_map/ppermute | solution.py:396
  47.7 1.7 %collective-permute-done.14.refs_3_ = f32[64,128]{1,0:T(8,128)S(1)} collective-permute-done((f32[64,128]{1,0:T(8,128)S(1)}, f32[64,128]{1,0:T(8,128)S(1)}, u32[]{:S(2)}, u32[]{:S(2)}) %collective-permute-start.14) | collective-permute-done | bytes 32800 | tf_op jit(solution)/shard_map/ppermute | solution.py:396
  49.4 0.7 collective-permute-start.5
  50.1 0.0 collective-permute-done.refs_0_
  50.1 0.1 collective-permute-start.6
  50.2 0.0 collective-permute-done.1.refs_1_
  50.2 4.5 %collective-permute-start.17 = (bf16[1032,128]{1,0:T(8,128)(2,1)S(1)}, bf16[1032,128]{1,0:T(8,128)(2,1)S(1)}, u32[]{:S(2)}, u32[]{:S(2)}) collective-permute-start(bf16[1032,128]{1,0:T(8,128)(2,1)S(1)} %get-tuple-element.38.refs_2_), channel_id=1, source_target_pairs={{0,0},{1,1},{8,16},{9,17},{16,8},{17,9},{24,24},{25,25},{2,2},{3,3... | collective-permute-start | bytes 792584 | tf_op jit(solution)/shard_map/ppermute | solution.py:565
  54.7 0.0 collective-permute-done.2.refs_2_.refs_6_
  54.7 0.2 collective-permute-start.18
  54.9 0.0 collective-permute-done.3.refs_3_.refs_7_
  54.9 0.2 collective-permute-start.4
  55.1 2.8 %copy-done.3 = bf16[4,1,768,1024]{3,2,1,0:T(8,128)(2,1)S(1)} copy-done((bf16[4,1,768,1024]{3,2,1,0:T(8,128)(2,1)S(1)}, bf16[4,1,768,1024]{3,2,1,0:T(8,128)(2,1)}, u32[]{:S(2)}) %copy-start.3) | copy-done | bytes 6291480
  57.9 2.3 %text_part.1 = (bf16[4,32,128]{2,1,0:T(8,128)(2,1)S(1)}, f32[4,32,128]{2,1,0:T(8,128)S(1)}, f32[4,32,128]{2,1,0:T(8,128)S(1)}, f32[4,32,128]{2,1,0:T(8,128)S(1)}) custom-call(s32[1]{0:T(128)S(6)} %copy.10.len_ref, bf16[4,1,3584]{2,1,0:T(2,128)(2,1)S(1)} %copy.8.query_ref, bf16[4,1,768,1024]{3,2,1,0:T(8,128)(2,1)S(1)} %copy-done.3), custom_call_target="tpu_custom_call" | custom-call | flops 25769803776 | bytes 6291456 | tf_op jit(solution)/shard_map/text_part/pallas_call | solution.py:246
  60.2 0.2 merge_far.1
  60.3 0.0 collective-permute-done.4.refs_4_.refs_9_
  60.3 3.8 %collective-permute-start.15 = (f32[32,128]{1,0:T(8,128)S(1)}, f32[32,128]{1,0:T(8,128)S(1)}, u32[]{:S(2)}, u32[]{:S(2)}) collective-permute-start(f32[32,128]{1,0:T(8,128)S(1)} %get-tuple-element.48), channel_id=1, source_target_pairs={{0,0},{1,1},{8,16},{9,17},{16,8},{17,9},{24,24},{25,25},{2,2},{3,3... | collective-permute-start | bytes 49160 | tf_op jit(solution)/shard_map/ppermute | solution.py:587
  64.1 0.0 collective-permute-done.5.refs_6_.refs_3_
  64.1 0.1 collective-permute-start.16
  64.2 0.0 collective-permute-done.6.refs_7_.refs_5_
  64.2 1.3 %shard_map.77 = (f32[32,128]{1,0:T(8,128)S(1)}, f32[32,128]{1,0:T(8,128)S(1)}, f32[32,128]{1,0:T(8,128)S(1)}, f32[32,128]{1,0:T(8,128)S(1)}) custom-call(bf16[4,32,128]{2,1,0:T(8,128)(2,1)S(1)} %get-tuple-element.26.q_ref, f32[4,32,128]{2,1,0:T(8,128)S(1)} %get-tuple-element.27.top_in, f32[4,32,128]{2,1,0:T(8,128)S(1)} %get-tuple-element.28.total_in, ...), custom_call_target="tpu_custom_call" | custom-call | flops 67633152 | bytes 2113536 | tf_op jit(solution)/shard_map/pallas_call | solution.py:379
  65.5 1.6 %collective-permute-start.7 = (f32[32,128]{1,0:T(8,128)S(1)}, f32[32,128]{1,0:T(8,128)S(1)}, u32[]{:S(2)}, u32[]{:S(2)}) collective-permute-start(f32[32,128]{1,0:T(8,128)S(1)} %get-tuple-element.41), channel_id=1, source_target_pairs={{0,2},{2,0},{4,6},{6,4},{1,3},{3,1},{5,7},{7,5},{8,10},{10,8},{12,... | collective-permute-start | bytes 49160 | tf_op jit(solution)/shard_map/ppermute | solution.py:396
  67.1 0.0 collective-permute-done.17.refs_2_
  67.1 1.5 %collective-permute-start.8 = (f32[32,128]{1,0:T(8,128)S(1)}, f32[32,128]{1,0:T(8,128)S(1)}, u32[]{:S(2)}, u32[]{:S(2)}) collective-permute-start(f32[32,128]{1,0:T(8,128)S(1)} %get-tuple-element.42), channel_id=1, source_target_pairs={{0,4},{2,6},{4,0},{6,2},{1,5},{3,7},{5,1},{7,3},{8,12},{10,14},{12... | collective-permute-start | bytes 49160 | tf_op jit(solution)/shard_map/ppermute | solution.py:396
  68.6 1.0 %collective-permute-start.9 = (f32[32,128]{1,0:T(8,128)S(1)}, f32[32,128]{1,0:T(8,128)S(1)}, u32[]{:S(2)}, u32[]{:S(2)}) collective-permute-start(f32[32,128]{1,0:T(8,128)S(1)} %get-tuple-element.43), channel_id=1, source_target_pairs={{0,6},{2,4},{4,2},{6,0},{1,7},{3,5},{5,3},{7,1},{8,14},{10,12},{12... | collective-permute-start | bytes 49160 | tf_op jit(solution)/shard_map/ppermute | solution.py:396
  69.6 2.1 %place_rows.1 = bf16[4,256,1024]{2,1,0:T(8,128)(2,1)} custom-call(bf16[1032,128]{1,0:T(8,128)(2,1)S(1)} %collective-permute-done.refs_0_, bf16[1032,128]{1,0:T(8,128)(2,1)S(1)} %collective-permute-done.1.refs_1_, bf16[1032,128]{1,0:T(8,128)(2,1)S(1)} %collective-permute-done.17.refs_2_, bf16[1032,128]{1,0:T(8,128)(2,1)S(1)} %collective-permute-done.5.refs_6_.refs_3_, ...), custom_call_target="tpu_custom_call" | custom-call | flops 536870912 | bytes 4194304 | tf_op jit(solution)/shard_map/place_rows/pallas_call | solution.py:478
  71.7 0.0 collective-permute-done.15.refs_4_
  71.7 0.0 collective-permute-done.7.refs_1_
  71.7 0.0 collective-permute-done.8.refs_2_
  71.7 1.5 %collective-permute-done.9.refs_3_ = f32[32,128]{1,0:T(8,128)S(1)} collective-permute-done((f32[32,128]{1,0:T(8,128)S(1)}, f32[32,128]{1,0:T(8,128)S(1)}, u32[]{:S(2)}, u32[]{:S(2)}) %collective-permute-start.9) | collective-permute-done | bytes 16416 | tf_op jit(solution)/shard_map/ppermute | solution.py:396
  73.2 0.7 %merge.1 = bf16[4,896]{1,0:T(4,128)(2,1)} custom-call(f32[32,128]{1,0:T(8,128)S(1)} %get-tuple-element.40.refs_0_, f32[32,128]{1,0:T(8,128)S(1)} %collective-permute-done.7.refs_1_, f32[32,128]{1,0:T(8,128)S(1)} %collective-permute-done.8.refs_2_, f32[32,128]{1,0:T(8,128)S(1)} %collective-permute-done.9.refs_3_, ...), custom_call_target="tpu_custom_call" | custom-call | tf_op jit(solution)/shard_map/merge/pallas_call | solution.py:512
  (9 shorter events, 0.1 us)
Async XLA Ops:
  0.6 11.5 %copy-start.4 = (bf16[4,1,3584]{2,0,1:T(4,128)(2,1)S(1)}, bf16[4,1,3584]{2,0,1:T(4,128)(2,1)}, u32[]{:S(2)}) copy-start(bf16[4,1,3584]{2,0,1:T(4,128)(2,1)} %param.6) | copy-start | bytes 86020
  3.9 46.2 %collective-permute-start = (bf16[1032,128]{1,0:T(8,128)(2,1)}, bf16[1032,128]{1,0:T(8,128)(2,1)S(1)}, u32[]{:S(2)}, u32[]{:S(2)}) collective-permute-start(bf16[1032,128]{1,0:T(8,128)(2,1)} %get-tuple-element.30), channel_id=1, source_target_pairs={{0,8},{1,9},{8,24},{9,25},{16,0},{17,1},{24,16},{25,17},{2,10},{3,... | collective-permute-start | bytes 792584 | tf_op jit(solution)/shard_map/ppermute | solution.py:565
  6.5 43.7 %collective-permute-start.1 = (bf16[1032,128]{1,0:T(8,128)(2,1)}, bf16[1032,128]{1,0:T(8,128)(2,1)S(1)}, u32[]{:S(2)}, u32[]{:S(2)}) collective-permute-start(bf16[1032,128]{1,0:T(8,128)(2,1)} %get-tuple-element.31), channel_id=1, source_target_pairs={{0,9},{1,8},{8,25},{9,24},{16,1},{17,0},{24,17},{25,16},{2,11},{3,... | collective-permute-start | bytes 792584 | tf_op jit(solution)/shard_map/ppermute | solution.py:565
  6.5 1.6 %copy-start = (bf16[4,256,1024]{2,1,0:T(8,128)(2,1)S(1)}, bf16[4,256,1024]{2,1,0:T(8,128)(2,1)}, u32[]{:S(2)}) copy-start(bf16[4,256,1024]{2,1,0:T(8,128)(2,1)} %rows_ref.1) | copy-start | bytes 6291460
  8.1 0.9 %copy-start.1 = (bf16[256,256]{1,0:T(8,128)(2,1)S(1)}, bf16[256,256]{1,0:T(8,128)(2,1)}, u32[]{:S(2)}) copy-start(bf16[256,256]{1,0:T(8,128)(2,1)} %get-tuple-element.32.choose_ref) | copy-start | bytes 393220
  9.0 0.7 copy-start.2
  10.3 44.5 %collective-permute-start.2 = (bf16[1032,128]{1,0:T(8,128)(2,1)S(1)}, bf16[1032,128]{1,0:T(8,128)(2,1)S(1)}, u32[]{:S(2)}, u32[]{:S(2)}) collective-permute-start(bf16[1032,128]{1,0:T(8,128)(2,1)S(1)} %get-tuple-element.34), channel_id=1, source_target_pairs={{0,16},{1,17},{8,0},{9,1},{16,24},{17,25},{24,8},{25,9},{2,18},{3,... | collective-permute-start | bytes 792584 | tf_op jit(solution)/shard_map/ppermute | solution.py:565
  11.5 43.4 %collective-permute-start.3 = (bf16[1032,128]{1,0:T(8,128)(2,1)S(1)}, bf16[1032,128]{1,0:T(8,128)(2,1)S(1)}, u32[]{:S(2)}, u32[]{:S(2)}) collective-permute-start(bf16[1032,128]{1,0:T(8,128)(2,1)S(1)} %get-tuple-element.35), channel_id=1, source_target_pairs={{0,17},{1,16},{8,1},{9,0},{16,25},{17,24},{24,9},{25,8},{2,19},{3,... | collective-permute-start | bytes 792584 | tf_op jit(solution)/shard_map/ppermute | solution.py:565
  12.1 17.8 %collective-permute-start.10 = (bf16[4,3584]{1,0:T(4,128)(2,1)S(1)}, bf16[4,3584]{1,0:T(4,128)(2,1)S(1)}, u32[]{:S(2)}, u32[]{:S(2)}) collective-permute-start(bf16[4,3584]{1,0:T(4,128)(2,1)S(1)} %bitcast.8), channel_id=1, source_target_pairs={{0,0},{1,1},{16,8},{17,9},{8,16},{9,17},{24,24},{25,25},{2,2},{3,3... | collective-permute-start | bytes 86024 | tf_op jit(solution)/shard_map/ppermute | solution.py:565
  30.0 4.8 %collective-permute-start.11 = (bf16[4,3584]{1,0:T(4,128)(2,1)S(1)}, bf16[4,3584]{1,0:T(4,128)(2,1)S(1)}, u32[]{:S(2)}, u32[]{:S(2)}) collective-permute-start(bf16[4,3584]{1,0:T(4,128)(2,1)S(1)} %bitcast.9), channel_id=1, source_target_pairs={{1,0},{0,1},{17,8},{16,9},{9,16},{8,17},{25,24},{24,25},{3,2},{2,3... | collective-permute-start | bytes 86024 | tf_op jit(solution)/shard_map/ppermute | solution.py:565
  36.7 4.0 %collective-permute-start.12 = (f32[64,128]{1,0:T(8,128)S(1)}, f32[64,128]{1,0:T(8,128)S(1)}, u32[]{:S(2)}, u32[]{:S(2)}) collective-permute-start(f32[64,128]{1,0:T(8,128)S(1)} %get-tuple-element.45), channel_id=1, source_target_pairs={{0,2},{2,0},{4,6},{6,4},{1,3},{3,1},{5,7},{7,5},{8,10},{10,8},{12,... | collective-permute-start | bytes 98312 | tf_op jit(solution)/shard_map/ppermute | solution.py:396
  40.7 3.9 %collective-permute-start.13 = (f32[64,128]{1,0:T(8,128)S(1)}, f32[64,128]{1,0:T(8,128)S(1)}, u32[]{:S(2)}, u32[]{:S(2)}) collective-permute-start(f32[64,128]{1,0:T(8,128)S(1)} %get-tuple-element.46), channel_id=1, source_target_pairs={{0,4},{2,6},{4,0},{6,2},{1,5},{3,7},{5,1},{7,3},{8,12},{10,14},{12... | collective-permute-start | bytes 98312 | tf_op jit(solution)/shard_map/ppermute | solution.py:396
  44.6 4.8 %collective-permute-start.14 = (f32[64,128]{1,0:T(8,128)S(1)}, f32[64,128]{1,0:T(8,128)S(1)}, u32[]{:S(2)}, u32[]{:S(2)}) collective-permute-start(f32[64,128]{1,0:T(8,128)S(1)} %get-tuple-element.47), channel_id=1, source_target_pairs={{0,6},{2,4},{4,2},{6,0},{1,7},{3,5},{5,3},{7,1},{8,14},{10,12},{12... | collective-permute-start | bytes 98312 | tf_op jit(solution)/shard_map/ppermute | solution.py:396
  49.4 14.7 %collective-permute-start.5 = (bf16[1032,128]{1,0:T(8,128)(2,1)S(1)}, bf16[1032,128]{1,0:T(8,128)(2,1)S(1)}, u32[]{:S(2)}, u32[]{:S(2)}) collective-permute-start(bf16[1032,128]{1,0:T(8,128)(2,1)S(1)} %get-tuple-element.38.refs_2_), channel_id=1, source_target_pairs={{0,24},{1,25},{8,8},{9,9},{16,16},{17,17},{24,0},{25,1},{2,26},{3,... | collective-permute-start | bytes 792584 | tf_op jit(solution)/shard_map/ppermute | solution.py:565
  50.1 14.1 %collective-permute-start.6 = (bf16[1032,128]{1,0:T(8,128)(2,1)S(1)}, bf16[1032,128]{1,0:T(8,128)(2,1)S(1)}, u32[]{:S(2)}, u32[]{:S(2)}) collective-permute-start(bf16[1032,128]{1,0:T(8,128)(2,1)S(1)} %get-tuple-element.39.refs_3_), channel_id=1, source_target_pairs={{0,25},{1,24},{8,9},{9,8},{16,17},{17,16},{24,1},{25,0},{2,27},{3,... | collective-permute-start | bytes 792584 | tf_op jit(solution)/shard_map/ppermute | solution.py:565
  50.2 16.9 %collective-permute-start.17 = (bf16[1032,128]{1,0:T(8,128)(2,1)S(1)}, bf16[1032,128]{1,0:T(8,128)(2,1)S(1)}, u32[]{:S(2)}, u32[]{:S(2)}) collective-permute-start(bf16[1032,128]{1,0:T(8,128)(2,1)S(1)} %get-tuple-element.38.refs_2_), channel_id=1, source_target_pairs={{0,0},{1,1},{8,16},{9,17},{16,8},{17,9},{24,24},{25,25},{2,2},{3,3... | collective-permute-start | bytes 792584 | tf_op jit(solution)/shard_map/ppermute | solution.py:565
  54.7 13.9 %collective-permute-start.18 = (bf16[1032,128]{1,0:T(8,128)(2,1)S(1)}, bf16[1032,128]{1,0:T(8,128)(2,1)S(1)}, u32[]{:S(2)}, u32[]{:S(2)}) collective-permute-start(bf16[1032,128]{1,0:T(8,128)(2,1)S(1)} %get-tuple-element.39.refs_3_), channel_id=1, source_target_pairs={{0,1},{1,0},{8,17},{9,16},{16,9},{17,8},{24,25},{25,24},{2,3},{3,2... | collective-permute-start | bytes 792584 | tf_op jit(solution)/shard_map/ppermute | solution.py:565
  54.9 5.4 %collective-permute-start.4 = (bf16[1032,128]{1,0:T(8,128)(2,1)S(1)}, bf16[1032,128]{1,0:T(8,128)(2,1)S(1)}, u32[]{:S(2)}, u32[]{:S(2)}) collective-permute-start(bf16[1032,128]{1,0:T(8,128)(2,1)S(1)} %get-tuple-element.36), channel_id=1, source_target_pairs={{0,1},{1,0},{8,9},{9,8},{16,17},{17,16},{24,25},{25,24},{2,3},{3,2... | collective-permute-start | bytes 792584 | tf_op jit(solution)/shard_map/ppermute | solution.py:565
  55.1 2.8 %copy-start.3 = (bf16[4,1,768,1024]{3,2,1,0:T(8,128)(2,1)S(1)}, bf16[4,1,768,1024]{3,2,1,0:T(8,128)(2,1)}, u32[]{:S(2)}) copy-start(bf16[4,1,768,1024]{3,2,1,0:T(8,128)(2,1)} %text_ref.1) | copy-start | bytes 18874372
  60.3 11.4 %collective-permute-start.15 = (f32[32,128]{1,0:T(8,128)S(1)}, f32[32,128]{1,0:T(8,128)S(1)}, u32[]{:S(2)}, u32[]{:S(2)}) collective-permute-start(f32[32,128]{1,0:T(8,128)S(1)} %get-tuple-element.48), channel_id=1, source_target_pairs={{0,0},{1,1},{8,16},{9,17},{16,8},{17,9},{24,24},{25,25},{2,2},{3,3... | collective-permute-start | bytes 49160 | tf_op jit(solution)/shard_map/ppermute | solution.py:587
  64.1 7.6 %collective-permute-start.16 = (f32[32,128]{1,0:T(8,128)S(1)}, f32[32,128]{1,0:T(8,128)S(1)}, u32[]{:S(2)}, u32[]{:S(2)}) collective-permute-start(f32[32,128]{1,0:T(8,128)S(1)} %get-tuple-element.49), channel_id=1, source_target_pairs={{0,1},{1,0},{8,17},{9,16},{16,9},{17,8},{24,25},{25,24},{2,3},{3,2... | collective-permute-start | bytes 49160 | tf_op jit(solution)/shard_map/ppermute | solution.py:587
  65.5 6.2 %collective-permute-start.7 = (f32[32,128]{1,0:T(8,128)S(1)}, f32[32,128]{1,0:T(8,128)S(1)}, u32[]{:S(2)}, u32[]{:S(2)}) collective-permute-start(f32[32,128]{1,0:T(8,128)S(1)} %get-tuple-element.41), channel_id=1, source_target_pairs={{0,2},{2,0},{4,6},{6,4},{1,3},{3,1},{5,7},{7,5},{8,10},{10,8},{12,... | collective-permute-start | bytes 49160 | tf_op jit(solution)/shard_map/ppermute | solution.py:396
  67.1 4.7 %collective-permute-start.8 = (f32[32,128]{1,0:T(8,128)S(1)}, f32[32,128]{1,0:T(8,128)S(1)}, u32[]{:S(2)}, u32[]{:S(2)}) collective-permute-start(f32[32,128]{1,0:T(8,128)S(1)} %get-tuple-element.42), channel_id=1, source_target_pairs={{0,4},{2,6},{4,0},{6,2},{1,5},{3,7},{5,1},{7,3},{8,12},{10,14},{12... | collective-permute-start | bytes 49160 | tf_op jit(solution)/shard_map/ppermute | solution.py:396
  68.6 4.6 %collective-permute-start.9 = (f32[32,128]{1,0:T(8,128)S(1)}, f32[32,128]{1,0:T(8,128)S(1)}, u32[]{:S(2)}, u32[]{:S(2)}) collective-permute-start(f32[32,128]{1,0:T(8,128)S(1)} %get-tuple-element.43), channel_id=1, source_target_pairs={{0,6},{2,4},{4,2},{6,0},{1,7},{3,5},{5,3},{7,1},{8,14},{10,12},{12... | collective-permute-start | bytes 49160 | tf_op jit(solution)/shard_map/ppermute | solution.py:396

commit v2 on v1

--- a/solution.py
+++ b/solution.py
@@ -18,17 +18,11 @@
 
 MOST_GROUPS = 16
 VMEM_LIMIT = 16 * 1024 * 1024
-WIDE_VMEM_LIMIT = 62 * 1024 * 1024
-
-
-def gray(index):
-    return index ^ (index >> 1)
 
 
 def step_of(source, target, count):
-    if count & (count - 1) == 0:
-        return (gray(target) - gray(source) + count - 1) & (count - 1)
-    return (target - source + count - 1) % count
+    turned = (source ^ target) ^ (count // 2)
+    return turned ^ (turned >> 1)
 
 
 def slot_choice(patch_count, req_count, owner, place):
@@ -80,8 +74,8 @@
 
 
 def first_kernel(patch_count, req_count, map_hbm, place_hbm, rows_hbm, *refs):
-    choose_ref, places_ref, *outs = refs[:-5]
-    owner_ref, place_ref, rows_ref, small_sem, rows_sem = refs[-5:]
+    choose_ref, places_ref, rows_ref, *outs = refs[:-4]
+    owner_ref, place_ref, small_sem, rows_sem = refs[-4:]
     layers, src_rows, _ = rows_hbm.shape
     small = [
         pltpu.make_async_copy(map_hbm, owner_ref, small_sem.at[0]),
@@ -119,6 +113,10 @@
     )
 
 
+def in_hbm(array):
+    return pltpu.with_memory_space_constraint(array, pltpu.HBM)
+
+
 def group_rows(patch_map, image_places, image_rows, patch_count, req_count):
     layers, src_rows, width = image_rows.shape
     groups = patch_count * req_count
@@ -139,23 +137,25 @@
         out_shape=[
             jax.ShapeDtypeStruct((src_rows, src_rows), jnp.bfloat16),
             jax.ShapeDtypeStruct((SUBLANES, src_rows), jnp.bfloat16),
+            jax.ShapeDtypeStruct(image_rows.shape, jnp.bfloat16),
         ]
         + [chunk] * req_count,
         in_specs=[hbm] * 3,
-        out_specs=[vmem] * (2 + req_count),
+        out_specs=[vmem] * (3 + req_count),
         scratch_shapes=[
             pltpu.VMEM((1, src_rows), jnp.int32),
             pltpu.VMEM((1, src_rows), jnp.int32),
-            pltpu.VMEM(image_rows.shape, jnp.bfloat16),
             pltpu.SemaphoreType.DMA((2,)),
             pltpu.SemaphoreType.DMA((layers,)),
         ],
         cost_estimate=cost(req_count),
-        compiler_params=pltpu.CompilerParams(vmem_limit_bytes=WIDE_VMEM_LIMIT),
+        compiler_params=pltpu.CompilerParams(vmem_limit_bytes=VMEM_LIMIT),
         name="group_first",
     )
-    choose, places, *first = first_call(
-        patch_map.reshape(1, src_rows), image_places.reshape(1, src_rows), image_rows
+    choose, places, rows, *first = first_call(
+        in_hbm(patch_map.reshape(1, src_rows)),
+        in_hbm(image_places.reshape(1, src_rows)),
+        in_hbm(image_rows),
     )
     rest_call = pl.pallas_call(
         functools.partial(rest_kernel, req_count, per),
@@ -166,7 +166,7 @@
         compiler_params=pltpu.CompilerParams(vmem_limit_bytes=VMEM_LIMIT),
         name="group_rest",
     )
-    rest = rest_call(choose, places, image_rows)
+    rest = rest_call(choose, places, rows)
     return [*first, *rest]
 
 
@@ -267,7 +267,7 @@
         ),
         compiler_params=pltpu.CompilerParams(vmem_limit_bytes=VMEM_LIMIT),
         name="text_part",
-    )(text_len, query, text_cache)
+    )(text_len, query, in_hbm(text_cache))
 
 
 def image_layer(scale, layer, chunks, used, q_ref, top, total, summed):
@@ -459,11 +459,14 @@
     down = lax.broadcasted_iota(jnp.int32, (band, band), 0)
     choose = jnp.where(down == places, 1.0, 0.0).astype(jnp.bfloat16)
     for layer in range(layers):
-        for c in range(blocks):
-            span = pl.ds((layer * blocks + c) * per, per)
-            column = jnp.concatenate([rows_of(k, span) for k in range(groups)], axis=0)
-            out_ref[layer, :, c * LANES : (c + 1) * LANES] = jnp.dot(
-                choose, column, preferred_element_type=jnp.float32
+        for c in range(0, blocks, 2):
+            spans = [pl.ds((layer * blocks + c + n) * per, per) for n in range(2)]
+            columns = [
+                jnp.concatenate([rows_of(k, span) for k in range(groups)], axis=0)
+                for span in spans
+            ]
+            out_ref[layer, :, c * LANES : (c + 2) * LANES] = jnp.dot(
+                choose, jnp.concatenate(columns, axis=1), preferred_element_type=jnp.float32
             ).astype(jnp.bfloat16)
         stores[layer].start()
     for store in stores:
@@ -584,7 +587,7 @@
         len(late),
     )
     far = merge_far(seq_exchange(far), len(late))
-    far = [lax.ppermute(part, axes, inner_pairs[k]) for part, k in zip(far, late)]
+    far = [send(far[n], inner_pairs[k]) for n, k in enumerate(late)]
     text = text_part(query, text_cache, text_len, scale)
     here = [arrived[k][0] for k in early + core + [own]]
     sure = len(here)

time: 74.3 us -> 82.4 us (1.11)
  waiting for transfers between devices: 26.4 us -> 38.1 us
  local copies, waits for them, and re-layouts: 6.01 us -> 0.05 us
  starting transfers between devices: 27.8 us -> 29.2 us
  Pallas kernels: 12.3 us -> 13.4 us
    ppermute x11 -> x13, waiting for transfers between devices: 18.4 us -> 30.1 us  [send(): return lax.ppermute(value, axes, some)]
    unnamed x11 -> x3, local copies, waits for them, and re-layouts: 6.01 us -> 0.05 us
    ppermute x11 -> x13, starting transfers between devices: 14.4 us -> 19.1 us  [send(): return lax.ppermute(value, axes, some)]
    ppermute x2 -> x0, starting transfers between devices: 3.84 us -> none  [fast_body(): lax.ppermute(part, axes, inner_pairs[k])]
    pallas_call x1, Pallas kernels: 2.29 us -> 4.64 us  [text_part(): pl.pallas_call(functools.partial(text_kernel, scale), out_shape=[jax.Shap...]
  transfers between devices with their start and end apart: 19 -> 19, of which waited for: 6 -> 6; matrix products, arithmetic and copies ran while one was open for 0% -> 0% of each run, Pallas kernels for 11% -> 12%
where the time goes in v2:
time: 82.4 us; the launch traced here: 82.2 us
  waiting for transfers between devices  38.1 us (46%)
  starting transfers between devices  29.2 us (35%)
  Pallas kernels  13.4 us (16%)
  between operations  1.47 us (2%)
    ppermute x13, waiting for transfers between devices, send(): return lax.ppermute(value, axes, some)  30.1 us
    ppermute x13, starting transfers between devices, send(): return lax.ppermute(value, axes, some)  19.1 us
    ppermute x6, starting transfers between devices, seq_exchange(): lax.ppermute(out, 'seq', [(s, s ^ k) for s in range(KV_HEADS)])  10 us
    ppermute x6, waiting for transfers between devices, seq_exchange(): lax.ppermute(out, 'seq', [(s, s ^ k) for s in range(KV_HEADS)])  7.97 us
    pallas_call x1, Pallas kernels, text_part(): pl.pallas_call(functools.partial(text_kernel, scale), out_shape=[jax.Shap...  4.64 us
    pallas_call x2, Pallas kernels, seq_parts(): pl.pallas_call(kernel, out_shape=[jax.ShapeDtypeStruct(shape, jnp.float32...  3.19 us
    pallas_call x1, Pallas kernels, group_rows(): first_call(in_hbm(patch_map.reshape(1, src_rows)), in_hbm(image_places.re...  2.43 us
    pallas_call x1, Pallas kernels, place_rows(): pl.pallas_call(functools.partial(place_kernel, owners, outer), out_shape=...  1.67 us
  transfers between devices with their start and end apart: 19, of which 6 were waited for; matrix products, arithmetic and copies ran while one was open for 0% of the time, Pallas kernels for 12%

profile of v2, /device:TPU:8, one launch (start us, length us, event | category | flops | bytes accessed | tf_op | source)
XLA Modules:
  0.0 82.2 jit_solution(8186772779343940033)
XLA Ops:
  0.6 0.0 copy-start
  0.6 2.4 %group_first.1 = (bf16[256,256]{1,0:T(8,128)(2,1)S(1)}, bf16[8,256]{1,0:T(8,128)(2,1)S(1)}, bf16[4,256,1024]{2,1,0:T(8,128)(2,1)S(1)}, bf16[1032,128]{1,0:T(8,128)(2,1)S(1)}, bf16[1032,128]{1,0:T(8,128)(2,1)S(1)}) custom-call(s32[1,256]{1,0:T(1,128)} %bitcast.11, s32[1,256]{1,0:T(1,128)} %bitcast.12, bf16[4,256,1024]{2,1,0:T(8,128)(2,1)} %rows_hbm.1), custom_call_target="tpu_custom_call" | custom-call | flops 134217728 | bytes 2621440 | tf_op jit(solution)/shard_map/group_first/pallas_call | solution.py:155
  3.1 2.7 %collective-permute-start = (bf16[1032,128]{1,0:T(8,128)(2,1)S(1)}, bf16[1032,128]{1,0:T(8,128)(2,1)S(1)}, u32[]{:S(2)}, u32[]{:S(2)}) collective-permute-start(bf16[1032,128]{1,0:T(8,128)(2,1)S(1)} %get-tuple-element.31), channel_id=1, source_target_pairs={{0,16},{1,17},{8,24},{9,25},{16,0},{17,1},{24,8},{25,9},{2,18},{3,... | collective-permute-start | bytes 792584 | tf_op jit(solution)/shard_map/ppermute | solution.py:568
  5.7 0.0 collective-permute-start.1
  5.7 0.6 group_rest.1
  6.3 0.5 collective-permute-start.2
  6.8 1.4 %collective-permute-start.3 = (bf16[1032,128]{1,0:T(8,128)(2,1)S(1)}, bf16[1032,128]{1,0:T(8,128)(2,1)S(1)}, u32[]{:S(2)}, u32[]{:S(2)}) collective-permute-start(bf16[1032,128]{1,0:T(8,128)(2,1)S(1)} %get-tuple-element.37), channel_id=1, source_target_pairs={{0,9},{1,8},{8,1},{9,0},{16,25},{17,24},{24,17},{25,16},{2,11},{3,... | collective-permute-start | bytes 792584 | tf_op jit(solution)/shard_map/ppermute | solution.py:568
  8.2 0.0 copy-done
  8.2 3.5 %collective-permute-start.10 = (bf16[4,3584]{1,0:T(4,128)(2,1)S(1)}, bf16[4,3584]{1,0:T(4,128)(2,1)S(1)}, u32[]{:S(2)}, u32[]{:S(2)}) collective-permute-start(bf16[4,3584]{1,0:T(4,128)(2,1)S(1)} %bitcast.8), channel_id=1, source_target_pairs={{0,0},{1,1},{16,8},{17,9},{8,16},{9,17},{24,24},{25,25},{2,2},{3,3... | collective-permute-start | bytes 86024 | tf_op jit(solution)/shard_map/ppermute | solution.py:568
  11.7 28.6 %collective-permute-done.10.refs_0_ = bf16[4,3584]{1,0:T(4,128)(2,1)S(1)} collective-permute-done((bf16[4,3584]{1,0:T(4,128)(2,1)S(1)}, bf16[4,3584]{1,0:T(4,128)(2,1)S(1)}, u32[]{:S(2)}, u32[]{:S(2)}) %collective-permute-start.10) | collective-permute-done | bytes 28704 | tf_op jit(solution)/shard_map/ppermute | solution.py:568
  40.2 2.1 %collective-permute-start.11 = (bf16[4,3584]{1,0:T(4,128)(2,1)S(1)}, bf16[4,3584]{1,0:T(4,128)(2,1)S(1)}, u32[]{:S(2)}, u32[]{:S(2)}) collective-permute-start(bf16[4,3584]{1,0:T(4,128)(2,1)S(1)} %bitcast.9), channel_id=1, source_target_pairs={{1,0},{0,1},{17,8},{16,9},{9,16},{8,17},{25,24},{24,25},{3,2},{2,3... | collective-permute-start | bytes 86024 | tf_op jit(solution)/shard_map/ppermute | solution.py:568
  42.3 1.6 %collective-permute-done.11.refs_1_ = bf16[4,3584]{1,0:T(4,128)(2,1)S(1)} collective-permute-done((bf16[4,3584]{1,0:T(4,128)(2,1)S(1)}, bf16[4,3584]{1,0:T(4,128)(2,1)S(1)}, u32[]{:S(2)}, u32[]{:S(2)}) %collective-permute-start.11) | collective-permute-done | bytes 28704 | tf_op jit(solution)/shard_map/ppermute | solution.py:568
  43.9 1.9 %shard_map.78 = (f32[64,128]{1,0:T(8,128)S(1)}, f32[64,128]{1,0:T(8,128)S(1)}, f32[64,128]{1,0:T(8,128)S(1)}, f32[64,128]{1,0:T(8,128)S(1)}) custom-call(bf16[4,3584]{1,0:T(4,128)(2,1)S(1)} %collective-permute-done.10.refs_0_, bf16[4,3584]{1,0:T(4,128)(2,1)S(1)} %collective-permute-done.11.refs_1_, bf16[1032,128]{1,0:T(8,128)(2,1)S(1)} %get-tuple-element.40.refs_2_, ...), custom_call_target="tpu_custom_call" | custom-call | flops 16908288 | bytes 528384 | tf_op jit(solution)/shard_map/pallas_call | solution.py:379
  45.8 1.6 %collective-permute-start.12 = (f32[64,128]{1,0:T(8,128)S(1)}, f32[64,128]{1,0:T(8,128)S(1)}, u32[]{:S(2)}, u32[]{:S(2)}) collective-permute-start(f32[64,128]{1,0:T(8,128)S(1)} %get-tuple-element.47), channel_id=1, source_target_pairs={{0,2},{2,0},{4,6},{6,4},{1,3},{3,1},{5,7},{7,5},{8,10},{10,8},{12,... | collective-permute-start | bytes 98312 | tf_op jit(solution)/shard_map/ppermute | solution.py:396
  47.3 2.4 %collective-permute-done.12.refs_1_ = f32[64,128]{1,0:T(8,128)S(1)} collective-permute-done((f32[64,128]{1,0:T(8,128)S(1)}, f32[64,128]{1,0:T(8,128)S(1)}, u32[]{:S(2)}, u32[]{:S(2)}) %collective-permute-start.12) | collective-permute-done | bytes 32800 | tf_op jit(solution)/shard_map/ppermute | solution.py:396
  49.8 1.5 %collective-permute-start.13 = (f32[64,128]{1,0:T(8,128)S(1)}, f32[64,128]{1,0:T(8,128)S(1)}, u32[]{:S(2)}, u32[]{:S(2)}) collective-permute-start(f32[64,128]{1,0:T(8,128)S(1)} %get-tuple-element.48), channel_id=1, source_target_pairs={{0,4},{2,6},{4,0},{6,2},{1,5},{3,7},{5,1},{7,3},{8,12},{10,14},{12... | collective-permute-start | bytes 98312 | tf_op jit(solution)/shard_map/ppermute | solution.py:396
  51.3 2.4 %collective-permute-done.13.refs_2_ = f32[64,128]{1,0:T(8,128)S(1)} collective-permute-done((f32[64,128]{1,0:T(8,128)S(1)}, f32[64,128]{1,0:T(8,128)S(1)}, u32[]{:S(2)}, u32[]{:S(2)}) %collective-permute-start.13) | collective-permute-done | bytes 32800 | tf_op jit(solution)/shard_map/ppermute | solution.py:396
  53.7 2.4 %collective-permute-start.14 = (f32[64,128]{1,0:T(8,128)S(1)}, f32[64,128]{1,0:T(8,128)S(1)}, u32[]{:S(2)}, u32[]{:S(2)}) collective-permute-start(f32[64,128]{1,0:T(8,128)S(1)} %get-tuple-element.49), channel_id=1, source_target_pairs={{0,6},{2,4},{4,2},{6,0},{1,7},{3,5},{5,3},{7,1},{8,14},{10,12},{12... | collective-permute-start | bytes 98312 | tf_op jit(solution)/shard_map/ppermute | solution.py:396
  56.8 1.7 %collective-permute-done.14.refs_3_ = f32[64,128]{1,0:T(8,128)S(1)} collective-permute-done((f32[64,128]{1,0:T(8,128)S(1)}, f32[64,128]{1,0:T(8,128)S(1)}, u32[]{:S(2)}, u32[]{:S(2)}) %collective-permute-start.14) | collective-permute-done | bytes 32800 | tf_op jit(solution)/shard_map/ppermute | solution.py:396
  58.5 0.7 collective-permute-start.5
  59.2 0.0 collective-permute-done.refs_0_
  59.2 0.1 collective-permute-start.6
  59.3 0.0 collective-permute-done.1.refs_1_
  59.3 4.1 %collective-permute-start.17 = (bf16[1032,128]{1,0:T(8,128)(2,1)S(1)}, bf16[1032,128]{1,0:T(8,128)(2,1)S(1)}, u32[]{:S(2)}, u32[]{:S(2)}) collective-permute-start(bf16[1032,128]{1,0:T(8,128)(2,1)S(1)} %get-tuple-element.40.refs_2_), channel_id=1, source_target_pairs={{0,0},{1,1},{8,16},{9,17},{16,8},{17,9},{24,24},{25,25},{2,2},{3,3... | collective-permute-start | bytes 792584 | tf_op jit(solution)/shard_map/ppermute | solution.py:568
  63.4 0.0 collective-permute-done.2.refs_2_.refs_6_
  63.4 0.2 collective-permute-start.18
  63.6 0.0 collective-permute-done.3.refs_3_.refs_7_
  63.6 0.2 collective-permute-start.4
  63.8 4.6 %text_part.1 = (bf16[4,32,128]{2,1,0:T(8,128)(2,1)S(1)}, f32[4,32,128]{2,1,0:T(8,128)S(1)}, f32[4,32,128]{2,1,0:T(8,128)S(1)}, f32[4,32,128]{2,1,0:T(8,128)S(1)}) custom-call(s32[1]{0:T(128)S(6)} %copy.10.len_ref, bf16[4,1,3584]{2,1,0:T(2,128)(2,1)S(1)} %copy.8.query_ref, bf16[4,1,768,1024]{3,2,1,0:T(8,128)(2,1)} %text_ref.1), custom_call_target="tpu_custom_call" | custom-call | flops 25769803776 | bytes 6291456 | tf_op jit(solution)/shard_map/text_part/pallas_call | solution.py:246
  68.4 0.2 merge_far.1
  68.6 0.0 collective-permute-done.4.refs_4_.refs_9_
  68.6 3.8 %collective-permute-start.15 = (f32[32,128]{1,0:T(8,128)S(1)}, f32[32,128]{1,0:T(8,128)S(1)}, u32[]{:S(2)}, u32[]{:S(2)}) collective-permute-start(f32[32,128]{1,0:T(8,128)S(1)} %get-tuple-element.50), channel_id=1, source_target_pairs={{0,0},{1,1},{8,16},{9,17},{16,8},{17,9},{24,24},{25,25},{2,2},{3,3... | collective-permute-start | bytes 49160 | tf_op jit(solution)/shard_map/ppermute | solution.py:568
  72.4 0.0 collective-permute-done.5.refs_6_.refs_3_
  72.4 0.1 collective-permute-start.16
  72.4 0.0 collective-permute-done.6.refs_7_.refs_5_
  72.5 1.3 %shard_map.77 = (f32[32,128]{1,0:T(8,128)S(1)}, f32[32,128]{1,0:T(8,128)S(1)}, f32[32,128]{1,0:T(8,128)S(1)}, f32[32,128]{1,0:T(8,128)S(1)}) custom-call(bf16[4,32,128]{2,1,0:T(8,128)(2,1)S(1)} %get-tuple-element.27.q_ref, f32[4,32,128]{2,1,0:T(8,128)S(1)} %get-tuple-element.28.top_in, f32[4,32,128]{2,1,0:T(8,128)S(1)} %get-tuple-element.29.total_in, ...), custom_call_target="tpu_custom_call" | custom-call | flops 67633152 | bytes 2113536 | tf_op jit(solution)/shard_map/pallas_call | solution.py:379
  73.7 1.6 %collective-permute-start.7 = (f32[32,128]{1,0:T(8,128)S(1)}, f32[32,128]{1,0:T(8,128)S(1)}, u32[]{:S(2)}, u32[]{:S(2)}) collective-permute-start(f32[32,128]{1,0:T(8,128)S(1)} %get-tuple-element.43), channel_id=1, source_target_pairs={{0,2},{2,0},{4,6},{6,4},{1,3},{3,1},{5,7},{7,5},{8,10},{10,8},{12,... | collective-permute-start | bytes 49160 | tf_op jit(solution)/shard_map/ppermute | solution.py:396
  75.3 0.0 collective-permute-done.17.refs_2_
  75.3 1.5 %collective-permute-start.8 = (f32[32,128]{1,0:T(8,128)S(1)}, f32[32,128]{1,0:T(8,128)S(1)}, u32[]{:S(2)}, u32[]{:S(2)}) collective-permute-start(f32[32,128]{1,0:T(8,128)S(1)} %get-tuple-element.44), channel_id=1, source_target_pairs={{0,4},{2,6},{4,0},{6,2},{1,5},{3,7},{5,1},{7,3},{8,12},{10,14},{12... | collective-permute-start | bytes 49160 | tf_op jit(solution)/shard_map/ppermute | solution.py:396
  76.8 0.0 collective-permute-done.18.refs_4_
  76.8 1.4 %collective-permute-start.9 = (f32[32,128]{1,0:T(8,128)S(1)}, f32[32,128]{1,0:T(8,128)S(1)}, u32[]{:S(2)}, u32[]{:S(2)}) collective-permute-start(f32[32,128]{1,0:T(8,128)S(1)} %get-tuple-element.45), channel_id=1, source_target_pairs={{0,6},{2,4},{4,2},{6,0},{1,7},{3,5},{5,3},{7,1},{8,14},{10,12},{12... | collective-permute-start | bytes 49160 | tf_op jit(solution)/shard_map/ppermute | solution.py:396
  78.3 1.7 %place_rows.1 = bf16[4,256,1024]{2,1,0:T(8,128)(2,1)} custom-call(bf16[1032,128]{1,0:T(8,128)(2,1)S(1)} %collective-permute-done.refs_0_, bf16[1032,128]{1,0:T(8,128)(2,1)S(1)} %collective-permute-done.1.refs_1_, bf16[1032,128]{1,0:T(8,128)(2,1)S(1)} %collective-permute-done.17.refs_2_, bf16[1032,128]{1,0:T(8,128)(2,1)S(1)} %collective-permute-done.5.refs_6_.refs_3_, ...), custom_call_target="tpu_custom_call" | custom-call | flops 536870912 | bytes 4194304 | tf_op jit(solution)/shard_map/place_rows/pallas_call | solution.py:481
  80.0 0.0 collective-permute-done.15.refs_4_
  80.0 0.0 collective-permute-done.16.refs_5_
  80.0 0.0 collective-permute-done.7.refs_1_
  80.0 0.0 collective-permute-done.8.refs_2_
  80.0 1.5 %collective-permute-done.9.refs_3_ = f32[32,128]{1,0:T(8,128)S(1)} collective-permute-done((f32[32,128]{1,0:T(8,128)S(1)}, f32[32,128]{1,0:T(8,128)S(1)}, u32[]{:S(2)}, u32[]{:S(2)}) %collective-permute-start.9) | collective-permute-done | bytes 16416 | tf_op jit(solution)/shard_map/ppermute | solution.py:396
  81.5 0.7 merge.1
  (1 shorter events, 0.0 us)
Async XLA Ops:
  0.6 7.6 %copy-start = (bf16[4,1,3584]{2,0,1:T(4,128)(2,1)S(1)}, bf16[4,1,3584]{2,0,1:T(4,128)(2,1)}, u32[]{:S(2)}) copy-start(bf16[4,1,3584]{2,0,1:T(4,128)(2,1)} %param.6) | copy-start | bytes 86020
  3.1 56.1 %collective-permute-start = (bf16[1032,128]{1,0:T(8,128)(2,1)S(1)}, bf16[1032,128]{1,0:T(8,128)(2,1)S(1)}, u32[]{:S(2)}, u32[]{:S(2)}) collective-permute-start(bf16[1032,128]{1,0:T(8,128)(2,1)S(1)} %get-tuple-element.31), channel_id=1, source_target_pairs={{0,16},{1,17},{8,24},{9,25},{16,0},{17,1},{24,8},{25,9},{2,18},{3,... | collective-permute-start | bytes 792584 | tf_op jit(solution)/shard_map/ppermute | solution.py:568
  5.7 53.5 %collective-permute-start.1 = (bf16[1032,128]{1,0:T(8,128)(2,1)S(1)}, bf16[1032,128]{1,0:T(8,128)(2,1)S(1)}, u32[]{:S(2)}, u32[]{:S(2)}) collective-permute-start(bf16[1032,128]{1,0:T(8,128)(2,1)S(1)} %get-tuple-element.32), channel_id=1, source_target_pairs={{0,17},{1,16},{8,25},{9,24},{16,1},{17,0},{24,9},{25,8},{2,19},{3,... | collective-permute-start | bytes 792584 | tf_op jit(solution)/shard_map/ppermute | solution.py:568
  6.3 57.1 %collective-permute-start.2 = (bf16[1032,128]{1,0:T(8,128)(2,1)S(1)}, bf16[1032,128]{1,0:T(8,128)(2,1)S(1)}, u32[]{:S(2)}, u32[]{:S(2)}) collective-permute-start(bf16[1032,128]{1,0:T(8,128)(2,1)S(1)} %get-tuple-element.36), channel_id=1, source_target_pairs={{0,8},{1,9},{8,0},{9,1},{16,24},{17,25},{24,16},{25,17},{2,10},{3,... | collective-permute-start | bytes 792584 | tf_op jit(solution)/shard_map/ppermute | solution.py:568
  6.8 56.7 %collective-permute-start.3 = (bf16[1032,128]{1,0:T(8,128)(2,1)S(1)}, bf16[1032,128]{1,0:T(8,128)(2,1)S(1)}, u32[]{:S(2)}, u32[]{:S(2)}) collective-permute-start(bf16[1032,128]{1,0:T(8,128)(2,1)S(1)} %get-tuple-element.37), channel_id=1, source_target_pairs={{0,9},{1,8},{8,1},{9,0},{16,25},{17,24},{24,17},{25,16},{2,11},{3,... | collective-permute-start | bytes 792584 | tf_op jit(solution)/shard_map/ppermute | solution.py:568
  8.2 32.0 %collective-permute-start.10 = (bf16[4,3584]{1,0:T(4,128)(2,1)S(1)}, bf16[4,3584]{1,0:T(4,128)(2,1)S(1)}, u32[]{:S(2)}, u32[]{:S(2)}) collective-permute-start(bf16[4,3584]{1,0:T(4,128)(2,1)S(1)} %bitcast.8), channel_id=1, source_target_pairs={{0,0},{1,1},{16,8},{17,9},{8,16},{9,17},{24,24},{25,25},{2,2},{3,3... | collective-permute-start | bytes 86024 | tf_op jit(solution)/shard_map/ppermute | solution.py:568
  40.2 3.6 %collective-permute-start.11 = (bf16[4,3584]{1,0:T(4,128)(2,1)S(1)}, bf16[4,3584]{1,0:T(4,128)(2,1)S(1)}, u32[]{:S(2)}, u32[]{:S(2)}) collective-permute-start(bf16[4,3584]{1,0:T(4,128)(2,1)S(1)} %bitcast.9), channel_id=1, source_target_pairs={{1,0},{0,1},{17,8},{16,9},{9,16},{8,17},{25,24},{24,25},{3,2},{2,3... | collective-permute-start | bytes 86024 | tf_op jit(solution)/shard_map/ppermute | solution.py:568
  45.8 4.0 %collective-permute-start.12 = (f32[64,128]{1,0:T(8,128)S(1)}, f32[64,128]{1,0:T(8,128)S(1)}, u32[]{:S(2)}, u32[]{:S(2)}) collective-permute-start(f32[64,128]{1,0:T(8,128)S(1)} %get-tuple-element.47), channel_id=1, source_target_pairs={{0,2},{2,0},{4,6},{6,4},{1,3},{3,1},{5,7},{7,5},{8,10},{10,8},{12,... | collective-permute-start | bytes 98312 | tf_op jit(solution)/shard_map/ppermute | solution.py:396
  49.8 3.9 %collective-permute-start.13 = (f32[64,128]{1,0:T(8,128)S(1)}, f32[64,128]{1,0:T(8,128)S(1)}, u32[]{:S(2)}, u32[]{:S(2)}) collective-permute-start(f32[64,128]{1,0:T(8,128)S(1)} %get-tuple-element.48), channel_id=1, source_target_pairs={{0,4},{2,6},{4,0},{6,2},{1,5},{3,7},{5,1},{7,3},{8,12},{10,14},{12... | collective-permute-start | bytes 98312 | tf_op jit(solution)/shard_map/ppermute | solution.py:396
  53.7 4.8 %collective-permute-start.14 = (f32[64,128]{1,0:T(8,128)S(1)}, f32[64,128]{1,0:T(8,128)S(1)}, u32[]{:S(2)}, u32[]{:S(2)}) collective-permute-start(f32[64,128]{1,0:T(8,128)S(1)} %get-tuple-element.49), channel_id=1, source_target_pairs={{0,6},{2,4},{4,2},{6,0},{1,7},{3,5},{5,3},{7,1},{8,14},{10,12},{12... | collective-permute-start | bytes 98312 | tf_op jit(solution)/shard_map/ppermute | solution.py:396
  58.5 13.9 %collective-permute-start.5 = (bf16[1032,128]{1,0:T(8,128)(2,1)S(1)}, bf16[1032,128]{1,0:T(8,128)(2,1)S(1)}, u32[]{:S(2)}, u32[]{:S(2)}) collective-permute-start(bf16[1032,128]{1,0:T(8,128)(2,1)S(1)} %get-tuple-element.40.refs_2_), channel_id=1, source_target_pairs={{0,24},{1,25},{8,8},{9,9},{16,16},{17,17},{24,0},{25,1},{2,26},{3,... | collective-permute-start | bytes 792584 | tf_op jit(solution)/shard_map/ppermute | solution.py:568
  59.2 13.3 %collective-permute-start.6 = (bf16[1032,128]{1,0:T(8,128)(2,1)S(1)}, bf16[1032,128]{1,0:T(8,128)(2,1)S(1)}, u32[]{:S(2)}, u32[]{:S(2)}) collective-permute-start(bf16[1032,128]{1,0:T(8,128)(2,1)S(1)} %get-tuple-element.41.refs_3_), channel_id=1, source_target_pairs={{0,25},{1,24},{8,9},{9,8},{16,17},{17,16},{24,1},{25,0},{2,27},{3,... | collective-permute-start | bytes 792584 | tf_op jit(solution)/shard_map/ppermute | solution.py:568
  59.3 16.0 %collective-permute-start.17 = (bf16[1032,128]{1,0:T(8,128)(2,1)S(1)}, bf16[1032,128]{1,0:T(8,128)(2,1)S(1)}, u32[]{:S(2)}, u32[]{:S(2)}) collective-permute-start(bf16[1032,128]{1,0:T(8,128)(2,1)S(1)} %get-tuple-element.40.refs_2_), channel_id=1, source_target_pairs={{0,0},{1,1},{8,16},{9,17},{16,8},{17,9},{24,24},{25,25},{2,2},{3,3... | collective-permute-start | bytes 792584 | tf_op jit(solution)/shard_map/ppermute | solution.py:568
  63.4 13.4 %collective-permute-start.18 = (bf16[1032,128]{1,0:T(8,128)(2,1)S(1)}, bf16[1032,128]{1,0:T(8,128)(2,1)S(1)}, u32[]{:S(2)}, u32[]{:S(2)}) collective-permute-start(bf16[1032,128]{1,0:T(8,128)(2,1)S(1)} %get-tuple-element.41.refs_3_), channel_id=1, source_target_pairs={{0,1},{1,0},{8,17},{9,16},{16,9},{17,8},{24,25},{25,24},{2,3},{3,2... | collective-permute-start | bytes 792584 | tf_op jit(solution)/shard_map/ppermute | solution.py:568
  63.6 5.0 %collective-permute-start.4 = (bf16[1032,128]{1,0:T(8,128)(2,1)S(1)}, bf16[1032,128]{1,0:T(8,128)(2,1)S(1)}, u32[]{:S(2)}, u32[]{:S(2)}) collective-permute-start(bf16[1032,128]{1,0:T(8,128)(2,1)S(1)} %get-tuple-element.38), channel_id=1, source_target_pairs={{0,1},{1,0},{8,9},{9,8},{16,17},{17,16},{24,25},{25,24},{2,3},{3,2... | collective-permute-start | bytes 792584 | tf_op jit(solution)/shard_map/ppermute | solution.py:568
  68.6 11.4 %collective-permute-start.15 = (f32[32,128]{1,0:T(8,128)S(1)}, f32[32,128]{1,0:T(8,128)S(1)}, u32[]{:S(2)}, u32[]{:S(2)}) collective-permute-start(f32[32,128]{1,0:T(8,128)S(1)} %get-tuple-element.50), channel_id=1, source_target_pairs={{0,0},{1,1},{8,16},{9,17},{16,8},{17,9},{24,24},{25,25},{2,2},{3,3... | collective-permute-start | bytes 49160 | tf_op jit(solution)/shard_map/ppermute | solution.py:568
  72.4 7.6 %collective-permute-start.16 = (f32[32,128]{1,0:T(8,128)S(1)}, f32[32,128]{1,0:T(8,128)S(1)}, u32[]{:S(2)}, u32[]{:S(2)}) collective-permute-start(f32[32,128]{1,0:T(8,128)S(1)} %get-tuple-element.51), channel_id=1, source_target_pairs={{0,1},{1,0},{8,17},{9,16},{16,9},{17,8},{24,25},{25,24},{2,3},{3,2... | collective-permute-start | bytes 49160 | tf_op jit(solution)/shard_map/ppermute | solution.py:568
  73.7 6.2 %collective-permute-start.7 = (f32[32,128]{1,0:T(8,128)S(1)}, f32[32,128]{1,0:T(8,128)S(1)}, u32[]{:S(2)}, u32[]{:S(2)}) collective-permute-start(f32[32,128]{1,0:T(8,128)S(1)} %get-tuple-element.43), channel_id=1, source_target_pairs={{0,2},{2,0},{4,6},{6,4},{1,3},{3,1},{5,7},{7,5},{8,10},{10,8},{12,... | collective-permute-start | bytes 49160 | tf_op jit(solution)/shard_map/ppermute | solution.py:396
  75.3 4.7 %collective-permute-start.8 = (f32[32,128]{1,0:T(8,128)S(1)}, f32[32,128]{1,0:T(8,128)S(1)}, u32[]{:S(2)}, u32[]{:S(2)}) collective-permute-start(f32[32,128]{1,0:T(8,128)S(1)} %get-tuple-element.44), channel_id=1, source_target_pairs={{0,4},{2,6},{4,0},{6,2},{1,5},{3,7},{5,1},{7,3},{8,12},{10,14},{12... | collective-permute-start | bytes 49160 | tf_op jit(solution)/shard_map/ppermute | solution.py:396
  76.8 4.6 %collective-permute-start.9 = (f32[32,128]{1,0:T(8,128)S(1)}, f32[32,128]{1,0:T(8,128)S(1)}, u32[]{:S(2)}, u32[]{:S(2)}) collective-permute-start(f32[32,128]{1,0:T(8,128)S(1)} %get-tuple-element.45), channel_id=1, source_target_pairs={{0,6},{2,4},{4,2},{6,0},{1,7},{3,5},{5,3},{7,1},{8,14},{10,12},{12... | collective-permute-start | bytes 49160 | tf_op jit(solution)/shard_map/ppermute | solution.py:396

commit v3 on v2

--- a/solution.py
+++ b/solution.py
@@ -17,6 +17,7 @@
 MASKED = -1e30
 
 MOST_GROUPS = 16
+LAST_CHUNKS = 1
 VMEM_LIMIT = 16 * 1024 * 1024
 
 
@@ -183,15 +184,15 @@
 
 
 def attend(queries, keys, values, used, scale):
+    def tile(rows, n):
+        return rows[n * SUBLANES : (n + 1) * SUBLANES]
+
     scores = jnp.concatenate(
         [
             lax.dot_general(
-                queries[g * SUBLANES : (g + 1) * SUBLANES],
-                keys[g],
-                (((1,), (1,)), ((), ())),
-                preferred_element_type=jnp.float32,
+                tile(queries, n), key, (((1,), (1,)), ((), ())), preferred_element_type=jnp.float32
             )
-            for g in range(KV_HEADS)
+            for n, key in enumerate(keys)
         ],
         axis=0,
     )
@@ -206,12 +207,8 @@
     rounded = weights.astype(jnp.bfloat16)
     summed = jnp.concatenate(
         [
-            jnp.dot(
-                rounded[g * SUBLANES : (g + 1) * SUBLANES],
-                values[g],
-                preferred_element_type=jnp.float32,
-            )
-            for g in range(KV_HEADS)
+            jnp.dot(tile(rounded, n), value, preferred_element_type=jnp.float32)
+            for n, value in enumerate(values)
         ],
         axis=0,
     )
@@ -270,45 +267,56 @@
     )(text_len, query, in_hbm(text_cache))
 
 
-def image_layer(scale, layer, chunks, used, q_ref, top, total, summed):
-    layers = q_ref.shape[0]
+def image_columns(chunks, layers):
     blocks = 2 * KV_HEADS
     per = (chunks[0].shape[0] - SUBLANES) // layers // blocks
 
-    def column(c):
+    def column(layer, c):
         span = pl.ds((layer * blocks + c) * per, per)
         return jnp.concatenate([chunk[span, :] for chunk in chunks], axis=0)
 
-    keys = [column(g) for g in range(KV_HEADS)]
-    values = [column(KV_HEADS + g) for g in range(KV_HEADS)]
-    new_top, new_total, new_summed = attend(q_ref[layer], keys, values, used, scale)
+    keys = [column(layer, g) for layer in range(layers) for g in range(KV_HEADS)]
+    values = [column(layer, KV_HEADS + g) for layer in range(layers) for g in range(KV_HEADS)]
+    return keys, values
+
+
+def join_image(scale, chunks, used, q_ref, top_in, total_in, sum_in):
+    layers, rows, _ = q_ref.shape
+    lines = layers * rows
+    keys, values = image_columns(chunks, layers)
+    queries = q_ref[...].reshape(lines, HEAD_DIM)
+    new_top, new_total, new_summed = attend(queries, keys, values, used, scale)
+    top = top_in[...].reshape(lines, LANES)[:, :1]
     both = jnp.maximum(top, new_top)
     old_factor = jnp.exp(top - both)
     new_factor = jnp.exp(new_top - both)
-    total = old_factor * total + new_factor * new_total
-    summed = old_factor * summed + new_factor * new_summed
+    total = old_factor * total_in[...].reshape(lines, LANES)[:, :1] + new_factor * new_total
+    summed = old_factor * sum_in[...].reshape(lines, LANES) + new_factor * new_summed
     return both, total, summed
 
 
 def pack_part(top, total, summed):
-    row = lax.broadcasted_iota(jnp.int32, (SUBLANES, LANES), 0)
-    lane = lax.broadcasted_iota(jnp.int32, (SUBLANES, LANES), 1)
+    shape = summed.shape
+    row = lax.broadcasted_iota(jnp.int32, shape, len(shape) - 2)
+    lane = lax.broadcasted_iota(jnp.int32, shape, len(shape) - 1)
     stats = jnp.where(lane == row, top, jnp.where(lane == row + LANES // 2, total, 0.0))
-    stats = jnp.sum(stats, axis=0, keepdims=True)
+    stats = jnp.sum(stats, axis=-2, keepdims=True)
     return jnp.where(row == SUBLANES - 1, stats, summed)
 
 
-def unpack_part(tile):
-    row = lax.broadcasted_iota(jnp.int32, (SUBLANES, LANES), 0)
-    lane = lax.broadcasted_iota(jnp.int32, (SUBLANES, LANES), 1)
-    stats = jnp.broadcast_to(tile[SUBLANES - 1 :, :], (SUBLANES, LANES))
-    top = jnp.sum(jnp.where(lane == row, stats, 0.0), axis=1, keepdims=True)
-    total = jnp.sum(jnp.where(lane == row + LANES // 2, stats, 0.0), axis=1, keepdims=True)
-    return top, total, tile
-
-
-def merge_tiles(tiles, used=None):
-    parts = [unpack_part(tile) for tile in tiles]
+def unpack_part(tiles):
+    shape = tiles.shape
+    row = lax.broadcasted_iota(jnp.int32, shape, len(shape) - 2)
+    lane = lax.broadcasted_iota(jnp.int32, shape, len(shape) - 1)
+    stats = jnp.broadcast_to(tiles[..., SUBLANES - 1 :, :], shape)
+    top = jnp.sum(jnp.where(lane == row, stats, 0.0), axis=-1, keepdims=True)
+    total = jnp.sum(jnp.where(lane == row + LANES // 2, stats, 0.0), axis=-1, keepdims=True)
+    return top, total, tiles
+
+
+def merge_parts(parts, used=None):
+    tiled = (parts[0].shape[0] // SUBLANES, SUBLANES, LANES)
+    parts = [unpack_part(part.reshape(tiled)) for part in parts]
     for n, part in enumerate(parts):
         if used is not None and used[n] is not None:
             parts[n] = [jnp.where(used[n], a, b) for a, b in zip(part, (MASKED, 0.0, 0.0))]
@@ -319,58 +327,72 @@
     return top, total, summed
 
 
+def store_packed(outs, packed, top, total, summed, layers):
+    tiled = (layers, KV_HEADS, SUBLANES)
+    tiles = pack_part(
+        top.reshape(*tiled, 1), total.reshape(*tiled, 1), summed.reshape(*tiled, LANES)
+    )
+    for g in range(KV_HEADS):
+        packed[g] = tiles[:, g].reshape(layers * SUBLANES, LANES)
+    me = lax.axis_index("seq")
+    for k in range(KV_HEADS):
+        outs[k][...] = packed[me ^ k]
+
+
 def here_kernel(scale, groups, sure, outer, q_ref, top_in, total_in, sum_in, *refs):
-    chunks, outs, packed = refs[:groups], refs[groups:-1], refs[-1]
+    chunks, (top_ref, total_ref, sum_ref) = refs[:groups], refs[groups:]
     layers, rows = q_ref.shape[:2]
     per = (chunks[0].shape[0] - SUBLANES) // layers // (2 * KV_HEADS)
     limit = jnp.where(is_outer(outer), groups, sure) * per
-    used = lax.broadcasted_iota(jnp.int32, (rows, groups * per), 1) < limit
-    for layer in range(q_ref.shape[0]):
-        top, total, summed = image_layer(
-            scale,
-            layer,
-            chunks,
-            used,
-            q_ref,
-            top_in[layer][:, :1],
-            total_in[layer][:, :1],
-            sum_in[layer],
-        )
-        for g in range(KV_HEADS):
-            span = slice(g * SUBLANES, (g + 1) * SUBLANES)
-            packed[g, pl.ds(layer * SUBLANES, SUBLANES), :] = pack_part(
-                top[span], total[span], summed[span]
-            )
-    me = lax.axis_index("seq")
-    for k in range(KV_HEADS):
-        outs[k][...] = packed[me ^ k]
+    lines = layers * rows
+    used = lax.broadcasted_iota(jnp.int32, (lines, groups * per), 1) < limit
+    top, total, summed = join_image(scale, chunks, used, q_ref, top_in, total_in, sum_in)
+    whole = (layers, rows, LANES)
+    top_ref[...] = jnp.broadcast_to(top, (lines, LANES)).reshape(whole)
+    total_ref[...] = jnp.broadcast_to(total, (lines, LANES)).reshape(whole)
+    sum_ref[...] = summed.reshape(whole)
+
+
+def here_part(parts, chunks, sure, outer, scale):
+    groups = len(chunks)
+    vmem = pl.BlockSpec(memory_space=pltpu.VMEM)
+    rows = chunks[0].shape[0]
+    made = pl.pallas_call(
+        functools.partial(here_kernel, scale, groups, sure, outer),
+        out_shape=[jax.ShapeDtypeStruct(part.shape, part.dtype) for part in parts[1:]],
+        in_specs=[vmem] * (4 + groups),
+        out_specs=[vmem] * 3,
+        cost_estimate=pl.CostEstimate(
+            flops=8 * SUBLANES * rows * LANES * groups,
+            bytes_accessed=2 * rows * LANES * groups,
+            transcendentals=SUBLANES * rows * groups,
+        ),
+        compiler_params=pltpu.CompilerParams(vmem_limit_bytes=VMEM_LIMIT),
+        name="here_part",
+    )(*parts, *chunks)
+    return [parts[0], *made]
+
+
+def last_kernel(scale, groups, q_ref, top_in, total_in, sum_in, *refs):
+    chunks, outs, packed = refs[:groups], refs[groups:-1], refs[-1]
+    parts = join_image(scale, chunks, None, q_ref, top_in, total_in, sum_in)
+    store_packed(outs, packed, *parts, q_ref.shape[0])
 
 
 def far_kernel(scale, count, *refs):
     queries, chunks = refs[:count], refs[count : 2 * count]
     outs, packed = refs[2 * count : -1], refs[-1]
     layers = queries[0].shape[0]
-    blocks = 2 * KV_HEADS
     group = queries[0].shape[1] // HEAD_DIM // KV_HEADS
-    for n in range(count):
-        chunk = chunks[n]
-        per = (chunk.shape[0] - SUBLANES) // layers // blocks
+    lines, keys, values = [], [], []
+    for query, chunk in zip(queries, chunks):
         for layer in range(layers):
-            columns = [
-                chunk[pl.ds((layer * blocks + c) * per, per), :] for c in range(blocks)
-            ]
-            line = queries[n][pl.ds(layer, 1), :].astype(jnp.float32)
-            top, total, summed = attend(
-                heads_of(line, group), columns[:KV_HEADS], columns[KV_HEADS:], None, scale
-            )
-            for g in range(KV_HEADS):
-                span = slice(g * SUBLANES, (g + 1) * SUBLANES)
-                packed[g, pl.ds((n * layers + layer) * SUBLANES, SUBLANES), :] = pack_part(
-                    top[span], total[span], summed[span]
-                )
-    me = lax.axis_index("seq")
-    for k in range(KV_HEADS):
-        outs[k][...] = packed[me ^ k]
+            lines.append(heads_of(query[pl.ds(layer, 1), :].astype(jnp.float32), group))
+        new_keys, new_values = image_columns([chunk], layers)
+        keys += new_keys
+        values += new_values
+    parts = attend(jnp.concatenate(lines, axis=0), keys, values, None, scale)
+    store_packed(outs, packed, *parts, count * layers)
 
 
 def seq_parts(kernel, operands, part_rows, chunk_rows, groups):
@@ -403,10 +425,10 @@
 def merge_far_kernel(count, *refs):
     parts, outs = refs[:-count], refs[-count:]
     rows = parts[0].shape[0] // count
+    merged = pack_part(*merge_parts([part[...] for part in parts]))
+    merged = merged.reshape(parts[0].shape)
     for n, out in enumerate(outs):
-        for at in range(0, rows, SUBLANES):
-            tiles = [part[pl.ds(n * rows + at, SUBLANES), :] for part in parts]
-            out[pl.ds(at, SUBLANES), :] = pack_part(*merge_tiles(tiles))
+        out[...] = merged[n * rows : (n + 1) * rows]
 
 
 def merge_far(parts, count):
@@ -501,12 +523,10 @@
     parts, out_ref, lines = refs[:-2], refs[-2], refs[-1]
     inside = jnp.logical_not(is_outer(outer))
     used = [None if n < sure else inside for n in range(len(parts))]
-    for layer in range(out_ref.shape[0]):
-        tiles = [part[pl.ds(layer * SUBLANES, SUBLANES), :] for part in parts]
-        _, total, summed = merge_tiles(tiles, used)
-        result = summed / total
-        for i in range(group):
-            lines[pl.ds(layer, 1), i * HEAD_DIM : (i + 1) * HEAD_DIM] = result[i : i + 1]
+    _, total, summed = merge_parts([part[...] for part in parts], used)
+    result = summed / total
+    for i in range(group):
+        lines[:, i * HEAD_DIM : (i + 1) * HEAD_DIM] = result[:, i, :]
     out_ref[...] = lines[...].astype(jnp.bfloat16)
 
 
@@ -589,15 +609,16 @@
     far = merge_far(seq_exchange(far), len(late))
     far = [send(far[n], inner_pairs[k]) for n, k in enumerate(late)]
     text = text_part(query, text_cache, text_len, scale)
-    here = [arrived[k][0] for k in early + core + [own]]
+    here = [arrived[k][0] for k in early[:-LAST_CHUNKS] + core + [own]]
     sure = len(here)
     here += [arrived[k][1] for k in late]
+    ends = [arrived[k][0] for k in early[-LAST_CHUNKS:]]
     parts = seq_parts(
-        functools.partial(here_kernel, scale, len(here), sure, outer),
-        [*text, *here],
+        functools.partial(last_kernel, scale, len(ends)),
+        [*here_part(text, here, sure, outer, scale), *ends],
         part_rows,
         chunk_rows,
-        len(here),
+        len(ends),
     )
     attended = merge([*seq_exchange(parts), *far], KV_HEADS, outer, layers, group)
     image_cache = place_rows(

time: 82.4 us -> 81 us (0.983)
  the two profiles are of different devices: /device:TPU:8 before, /device:TPU:0 now
where the time goes in v3:
time: 81 us; the launch traced here: 80.8 us
  starting transfers between devices  45.5 us (56%)
  waiting for transfers between devices  21.6 us (27%)
  Pallas kernels  12.2 us (15%)
  between operations  1.45 us (2%)
    ppermute x13, starting transfers between devices, send(): return lax.ppermute(value, axes, some)  36.4 us
    ppermute x13, waiting for transfers between devices, send(): return lax.ppermute(value, axes, some)  12.7 us
    ppermute x6, starting transfers between devices, seq_exchange(): lax.ppermute(out, 'seq', [(s, s ^ k) for s in range(KV_HEADS)])  9.07 us
    ppermute x6, waiting for transfers between devices, seq_exchange(): lax.ppermute(out, 'seq', [(s, s ^ k) for s in range(KV_HEADS)])  8.94 us
    pallas_call x1, Pallas kernels, text_part(): pl.pallas_call(functools.partial(text_kernel, scale), out_shape=[jax.Shap...  4.64 us
    pallas_call x1, Pallas kernels, group_rows(): first_call(in_hbm(patch_map.reshape(1, src_rows)), in_hbm(image_places.re...  2.43 us
    pallas_call x1, Pallas kernels, place_rows(): pl.pallas_call(functools.partial(place_kernel, owners, outer), out_shape=...  1.67 us
  transfers between devices with their start and end apart: 19, of which 6 were waited for; matrix products, arithmetic and copies ran while one was open for 0% of the time, Pallas kernels for 11%

profile of v3, /device:TPU:0, one launch (start us, length us, event | category | flops | bytes accessed | tf_op | source)
XLA Modules:
  0.0 80.8 jit_solution(13784106565006372106)
XLA Ops:
  0.6 0.0 copy-start
  0.6 2.4 %group_first.1 = (bf16[256,256]{1,0:T(8,128)(2,1)S(1)}, bf16[8,256]{1,0:T(8,128)(2,1)S(1)}, bf16[4,256,1024]{2,1,0:T(8,128)(2,1)S(1)}, bf16[1032,128]{1,0:T(8,128)(2,1)S(1)}, bf16[1032,128]{1,0:T(8,128)(2,1)S(1)}) custom-call(s32[1,256]{1,0:T(1,128)} %bitcast.11, s32[1,256]{1,0:T(1,128)} %bitcast.12, bf16[4,256,1024]{2,1,0:T(8,128)(2,1)} %rows_hbm.1), custom_call_target="tpu_custom_call" | custom-call | flops 134217728 | bytes 2621440 | tf_op jit(solution)/shard_map/group_first/pallas_call | solution.py:156
  3.1 4.1 %collective-permute-start = (bf16[1032,128]{1,0:T(8,128)(2,1)S(1)}, bf16[1032,128]{1,0:T(8,128)(2,1)S(1)}, u32[]{:S(2)}, u32[]{:S(2)}) collective-permute-start(bf16[1032,128]{1,0:T(8,128)(2,1)S(1)} %get-tuple-element.34), channel_id=1, source_target_pairs={{0,16},{1,17},{8,24},{9,25},{16,0},{17,1},{24,8},{25,9},{2,18},{3,... | collective-permute-start | bytes 792584 | tf_op jit(solution)/shard_map/ppermute | solution.py:588
  7.2 0.0 collective-permute-start.1
  7.2 0.6 group_rest.1
  7.8 1.6 %collective-permute-start.2 = (bf16[1032,128]{1,0:T(8,128)(2,1)S(1)}, bf16[1032,128]{1,0:T(8,128)(2,1)S(1)}, u32[]{:S(2)}, u32[]{:S(2)}) collective-permute-start(bf16[1032,128]{1,0:T(8,128)(2,1)S(1)} %get-tuple-element.39), channel_id=1, source_target_pairs={{0,8},{1,9},{8,0},{9,1},{16,24},{17,25},{24,16},{25,17},{2,10},{3,... | collective-permute-start | bytes 792584 | tf_op jit(solution)/shard_map/ppermute | solution.py:588
  9.4 0.2 collective-permute-start.3
  9.6 0.7 collective-permute-start.10
  10.3 0.0 collective-permute-done.10.refs_0_
  10.3 0.4 collective-permute-start.11
  10.7 0.9 %collective-permute-done.11.refs_1_ = bf16[4,3584]{1,0:T(4,128)(2,1)S(1)} collective-permute-done((bf16[4,3584]{1,0:T(4,128)(2,1)S(1)}, bf16[4,3584]{1,0:T(4,128)(2,1)S(1)}, u32[]{:S(2)}, u32[]{:S(2)}) %collective-permute-start.11) | collective-permute-done | bytes 28704 | tf_op jit(solution)/shard_map/ppermute | solution.py:588
  11.6 0.5 shard_map.78
  12.1 1.6 %collective-permute-start.12 = (f32[64,128]{1,0:T(8,128)S(1)}, f32[64,128]{1,0:T(8,128)S(1)}, u32[]{:S(2)}, u32[]{:S(2)}) collective-permute-start(f32[64,128]{1,0:T(8,128)S(1)} %get-tuple-element.53), channel_id=1, source_target_pairs={{0,2},{2,0},{4,6},{6,4},{1,3},{3,1},{5,7},{7,5},{8,10},{10,8},{12,... | collective-permute-start | bytes 98312 | tf_op jit(solution)/shard_map/ppermute | solution.py:418
  13.6 2.4 %collective-permute-done.12.refs_1_ = f32[64,128]{1,0:T(8,128)S(1)} collective-permute-done((f32[64,128]{1,0:T(8,128)S(1)}, f32[64,128]{1,0:T(8,128)S(1)}, u32[]{:S(2)}, u32[]{:S(2)}) %collective-permute-start.12) | collective-permute-done | bytes 32800 | tf_op jit(solution)/shard_map/ppermute | solution.py:418
  16.0 1.5 %collective-permute-start.13 = (f32[64,128]{1,0:T(8,128)S(1)}, f32[64,128]{1,0:T(8,128)S(1)}, u32[]{:S(2)}, u32[]{:S(2)}) collective-permute-start(f32[64,128]{1,0:T(8,128)S(1)} %get-tuple-element.54), channel_id=1, source_target_pairs={{0,4},{2,6},{4,0},{6,2},{1,5},{3,7},{5,1},{7,3},{8,12},{10,14},{12... | collective-permute-start | bytes 98312 | tf_op jit(solution)/shard_map/ppermute | solution.py:418
  17.6 2.4 %collective-permute-done.13.refs_2_ = f32[64,128]{1,0:T(8,128)S(1)} collective-permute-done((f32[64,128]{1,0:T(8,128)S(1)}, f32[64,128]{1,0:T(8,128)S(1)}, u32[]{:S(2)}, u32[]{:S(2)}) %collective-permute-start.13) | collective-permute-done | bytes 32800 | tf_op jit(solution)/shard_map/ppermute | solution.py:418
  19.9 2.4 %collective-permute-start.14 = (f32[64,128]{1,0:T(8,128)S(1)}, f32[64,128]{1,0:T(8,128)S(1)}, u32[]{:S(2)}, u32[]{:S(2)}) collective-permute-start(f32[64,128]{1,0:T(8,128)S(1)} %get-tuple-element.55), channel_id=1, source_target_pairs={{0,6},{2,4},{4,2},{6,0},{1,7},{3,5},{5,3},{7,1},{8,14},{10,12},{12... | collective-permute-start | bytes 98312 | tf_op jit(solution)/shard_map/ppermute | solution.py:418
  23.1 1.7 %collective-permute-done.14.refs_3_ = f32[64,128]{1,0:T(8,128)S(1)} collective-permute-done((f32[64,128]{1,0:T(8,128)S(1)}, f32[64,128]{1,0:T(8,128)S(1)}, u32[]{:S(2)}, u32[]{:S(2)}) %collective-permute-start.14) | collective-permute-done | bytes 32800 | tf_op jit(solution)/shard_map/ppermute | solution.py:418
  24.8 4.4 %collective-permute-start.4 = (bf16[1032,128]{1,0:T(8,128)(2,1)S(1)}, bf16[1032,128]{1,0:T(8,128)(2,1)S(1)}, u32[]{:S(2)}, u32[]{:S(2)}) collective-permute-start(bf16[1032,128]{1,0:T(8,128)(2,1)S(1)} %get-tuple-element.42.refs_2_), channel_id=1, source_target_pairs={{0,24},{1,25},{8,8},{9,9},{16,16},{17,17},{24,0},{25,1},{2,26},{3,... | collective-permute-start | bytes 792584 | tf_op jit(solution)/shard_map/ppermute | solution.py:588
  29.1 0.0 collective-permute-done.refs_0_
  29.1 0.1 collective-permute-start.5
  29.2 11.8 %collective-permute-done.1.refs_1_ = bf16[1032,128]{1,0:T(8,128)(2,1)S(1)} collective-permute-done((bf16[1032,128]{1,0:T(8,128)(2,1)S(1)}, bf16[1032,128]{1,0:T(8,128)(2,1)S(1)}, u32[]{:S(2)}, u32[]{:S(2)}) %collective-permute-start.1) | collective-permute-done | bytes 264224 | tf_op jit(solution)/shard_map/ppermute | solution.py:588
  41.0 0.7 collective-permute-start.17
  41.7 0.0 collective-permute-done.2.refs_2_.refs_6_
  41.7 1.0 %collective-permute-start.18 = (bf16[1032,128]{1,0:T(8,128)(2,1)S(1)}, bf16[1032,128]{1,0:T(8,128)(2,1)S(1)}, u32[]{:S(2)}, u32[]{:S(2)}) collective-permute-start(bf16[1032,128]{1,0:T(8,128)(2,1)S(1)} %get-tuple-element.43.refs_3_), channel_id=1, source_target_pairs={{0,1},{1,0},{8,17},{9,16},{16,9},{17,8},{24,25},{25,24},{2,3},{3,2... | collective-permute-start | bytes 792584 | tf_op jit(solution)/shard_map/ppermute | solution.py:588
  42.8 0.0 collective-permute-done.3.refs_3_.refs_9_
  42.8 22.2 %collective-permute-start.6 = (bf16[1032,128]{1,0:T(8,128)(2,1)S(1)}, bf16[1032,128]{1,0:T(8,128)(2,1)S(1)}, u32[]{:S(2)}, u32[]{:S(2)}) collective-permute-start(bf16[1032,128]{1,0:T(8,128)(2,1)S(1)} %get-tuple-element.47), channel_id=1, source_target_pairs={{0,9},{1,8},{8,1},{9,0},{16,25},{17,24},{24,17},{25,16},{2,11},{3,... | collective-permute-start | bytes 792584 | tf_op jit(solution)/shard_map/ppermute | solution.py:588
  64.9 4.6 %text_part.1 = (bf16[4,32,128]{2,1,0:T(8,128)(2,1)S(1)}, f32[4,32,128]{2,1,0:T(8,128)S(1)}, f32[4,32,128]{2,1,0:T(8,128)S(1)}, f32[4,32,128]{2,1,0:T(8,128)S(1)}) custom-call(s32[1]{0:T(128)S(6)} %copy.10.len_ref, bf16[4,1,3584]{2,1,0:T(2,128)(2,1)S(1)} %copy.8.query_ref, bf16[4,1,768,1024]{3,2,1,0:T(8,128)(2,1)} %text_ref.1), custom_call_target="tpu_custom_call" | custom-call | flops 25769803776 | bytes 6291456 | tf_op jit(solution)/shard_map/text_part/pallas_call | solution.py:243
  69.6 0.2 merge_far.1
  69.8 0.0 collective-permute-done.4.refs_5_.refs_3_
  69.8 0.7 collective-permute-start.15
  70.4 0.0 collective-permute-done.5.refs_6_.refs_5_
  70.4 0.4 collective-permute-start.16
  70.8 0.8 %here_part.1 = (f32[4,32,128]{2,1,0:T(8,128)S(1)}, f32[4,32,128]{2,1,0:T(8,128)S(1)}, f32[4,32,128]{2,1,0:T(8,128)S(1)}) custom-call(bf16[4,32,128]{2,1,0:T(8,128)(2,1)S(1)} %get-tuple-element.30.q_ref, f32[4,32,128]{2,1,0:T(8,128)S(1)} %get-tuple-element.31.top_in, f32[4,32,128]{2,1,0:T(8,128)S(1)} %get-tuple-element.32.total_in, ...), custom_call_target="tpu_custom_call" | custom-call | flops 59179008 | bytes 1849344 | tf_op jit(solution)/shard_map/here_part/pallas_call | solution.py:360
  71.7 0.0 collective-permute-done.6.refs_0_.refs_7_
  71.7 0.6 shard_map.77
  72.3 1.6 %collective-permute-start.7 = (f32[32,128]{1,0:T(8,128)S(1)}, f32[32,128]{1,0:T(8,128)S(1)}, u32[]{:S(2)}, u32[]{:S(2)}) collective-permute-start(f32[32,128]{1,0:T(8,128)S(1)} %get-tuple-element.49), channel_id=1, source_target_pairs={{0,2},{2,0},{4,6},{6,4},{1,3},{3,1},{5,7},{7,5},{8,10},{10,8},{12,... | collective-permute-start | bytes 49160 | tf_op jit(solution)/shard_map/ppermute | solution.py:418
  73.9 0.0 collective-permute-done.17.refs_2_
  73.9 1.5 %collective-permute-start.8 = (f32[32,128]{1,0:T(8,128)S(1)}, f32[32,128]{1,0:T(8,128)S(1)}, u32[]{:S(2)}, u32[]{:S(2)}) collective-permute-start(f32[32,128]{1,0:T(8,128)S(1)} %get-tuple-element.50), channel_id=1, source_target_pairs={{0,4},{2,6},{4,0},{6,2},{1,5},{3,7},{5,1},{7,3},{8,12},{10,14},{12... | collective-permute-start | bytes 49160 | tf_op jit(solution)/shard_map/ppermute | solution.py:418
  75.4 0.0 collective-permute-done.18.refs_4_
  75.4 0.5 collective-permute-start.9
  75.9 1.7 %place_rows.1 = bf16[4,256,1024]{2,1,0:T(8,128)(2,1)} custom-call(bf16[1032,128]{1,0:T(8,128)(2,1)S(1)} %collective-permute-done.refs_0_, bf16[1032,128]{1,0:T(8,128)(2,1)S(1)} %collective-permute-done.1.refs_1_, bf16[1032,128]{1,0:T(8,128)(2,1)S(1)} %collective-permute-done.17.refs_2_, bf16[1032,128]{1,0:T(8,128)(2,1)S(1)} %collective-permute-done.4.refs_5_.refs_3_, ...), custom_call_target="tpu_custom_call" | custom-call | flops 536870912 | bytes 4194304 | tf_op jit(solution)/shard_map/place_rows/pallas_call | solution.py:503
  77.5 0.0 collective-permute-done.15.refs_4_
  77.6 0.0 collective-permute-done.16.refs_5_
  77.6 0.0 collective-permute-done.7.refs_1_
  77.6 0.0 collective-permute-done.8.refs_2_
  77.6 2.4 %collective-permute-done.9.refs_3_ = f32[32,128]{1,0:T(8,128)S(1)} collective-permute-done((f32[32,128]{1,0:T(8,128)S(1)}, f32[32,128]{1,0:T(8,128)S(1)}, u32[]{:S(2)}, u32[]{:S(2)}) %collective-permute-start.9) | collective-permute-done | bytes 16416 | tf_op jit(solution)/shard_map/ppermute | solution.py:418
  80.0 0.7 merge.1
  (2 shorter events, 0.0 us)
Async XLA Ops:
  0.6 9.0 %copy-start = (bf16[4,1,3584]{2,0,1:T(4,128)(2,1)S(1)}, bf16[4,1,3584]{2,0,1:T(4,128)(2,1)}, u32[]{:S(2)}) copy-start(bf16[4,1,3584]{2,0,1:T(4,128)(2,1)} %param.6) | copy-start | bytes 86020
  3.1 26.0 %collective-permute-start = (bf16[1032,128]{1,0:T(8,128)(2,1)S(1)}, bf16[1032,128]{1,0:T(8,128)(2,1)S(1)}, u32[]{:S(2)}, u32[]{:S(2)}) collective-permute-start(bf16[1032,128]{1,0:T(8,128)(2,1)S(1)} %get-tuple-element.34), channel_id=1, source_target_pairs={{0,16},{1,17},{8,24},{9,25},{16,0},{17,1},{24,8},{25,9},{2,18},{3,... | collective-permute-start | bytes 792584 | tf_op jit(solution)/shard_map/ppermute | solution.py:588
  7.2 33.8 %collective-permute-start.1 = (bf16[1032,128]{1,0:T(8,128)(2,1)S(1)}, bf16[1032,128]{1,0:T(8,128)(2,1)S(1)}, u32[]{:S(2)}, u32[]{:S(2)}) collective-permute-start(bf16[1032,128]{1,0:T(8,128)(2,1)S(1)} %get-tuple-element.35), channel_id=1, source_target_pairs={{0,17},{1,16},{8,25},{9,24},{16,1},{17,0},{24,9},{25,8},{2,19},{3,... | collective-permute-start | bytes 792584 | tf_op jit(solution)/shard_map/ppermute | solution.py:588
  7.8 33.9 %collective-permute-start.2 = (bf16[1032,128]{1,0:T(8,128)(2,1)S(1)}, bf16[1032,128]{1,0:T(8,128)(2,1)S(1)}, u32[]{:S(2)}, u32[]{:S(2)}) collective-permute-start(bf16[1032,128]{1,0:T(8,128)(2,1)S(1)} %get-tuple-element.39), channel_id=1, source_target_pairs={{0,8},{1,9},{8,0},{9,1},{16,24},{17,25},{24,16},{25,17},{2,10},{3,... | collective-permute-start | bytes 792584 | tf_op jit(solution)/shard_map/ppermute | solution.py:588
  9.4 33.3 %collective-permute-start.3 = (bf16[1032,128]{1,0:T(8,128)(2,1)S(1)}, bf16[1032,128]{1,0:T(8,128)(2,1)S(1)}, u32[]{:S(2)}, u32[]{:S(2)}) collective-permute-start(bf16[1032,128]{1,0:T(8,128)(2,1)S(1)} %get-tuple-element.40), channel_id=1, source_target_pairs={{0,1},{1,0},{8,9},{9,8},{16,17},{17,16},{24,25},{25,24},{2,3},{3,2... | collective-permute-start | bytes 792584 | tf_op jit(solution)/shard_map/ppermute | solution.py:588
  9.6 0.7 collective-permute-start.10
  10.3 1.3 %collective-permute-start.11 = (bf16[4,3584]{1,0:T(4,128)(2,1)S(1)}, bf16[4,3584]{1,0:T(4,128)(2,1)S(1)}, u32[]{:S(2)}, u32[]{:S(2)}) collective-permute-start(bf16[4,3584]{1,0:T(4,128)(2,1)S(1)} %bitcast.9), channel_id=1, source_target_pairs={{1,0},{0,1},{17,8},{16,9},{9,16},{8,17},{25,24},{24,25},{3,2},{2,3... | collective-permute-start | bytes 86024 | tf_op jit(solution)/shard_map/ppermute | solution.py:588
  12.1 4.0 %collective-permute-start.12 = (f32[64,128]{1,0:T(8,128)S(1)}, f32[64,128]{1,0:T(8,128)S(1)}, u32[]{:S(2)}, u32[]{:S(2)}) collective-permute-start(f32[64,128]{1,0:T(8,128)S(1)} %get-tuple-element.53), channel_id=1, source_target_pairs={{0,2},{2,0},{4,6},{6,4},{1,3},{3,1},{5,7},{7,5},{8,10},{10,8},{12,... | collective-permute-start | bytes 98312 | tf_op jit(solution)/shard_map/ppermute | solution.py:418
  16.0 3.9 %collective-permute-start.13 = (f32[64,128]{1,0:T(8,128)S(1)}, f32[64,128]{1,0:T(8,128)S(1)}, u32[]{:S(2)}, u32[]{:S(2)}) collective-permute-start(f32[64,128]{1,0:T(8,128)S(1)} %get-tuple-element.54), channel_id=1, source_target_pairs={{0,4},{2,6},{4,0},{6,2},{1,5},{3,7},{5,1},{7,3},{8,12},{10,14},{12... | collective-permute-start | bytes 98312 | tf_op jit(solution)/shard_map/ppermute | solution.py:418
  19.9 4.8 %collective-permute-start.14 = (f32[64,128]{1,0:T(8,128)S(1)}, f32[64,128]{1,0:T(8,128)S(1)}, u32[]{:S(2)}, u32[]{:S(2)}) collective-permute-start(f32[64,128]{1,0:T(8,128)S(1)} %get-tuple-element.55), channel_id=1, source_target_pairs={{0,6},{2,4},{4,2},{6,0},{1,7},{3,5},{5,3},{7,1},{8,14},{10,12},{12... | collective-permute-start | bytes 98312 | tf_op jit(solution)/shard_map/ppermute | solution.py:418
  24.8 45.0 %collective-permute-start.4 = (bf16[1032,128]{1,0:T(8,128)(2,1)S(1)}, bf16[1032,128]{1,0:T(8,128)(2,1)S(1)}, u32[]{:S(2)}, u32[]{:S(2)}) collective-permute-start(bf16[1032,128]{1,0:T(8,128)(2,1)S(1)} %get-tuple-element.42.refs_2_), channel_id=1, source_target_pairs={{0,24},{1,25},{8,8},{9,9},{16,16},{17,17},{24,0},{25,1},{2,26},{3,... | collective-permute-start | bytes 792584 | tf_op jit(solution)/shard_map/ppermute | solution.py:588
  29.1 41.3 %collective-permute-start.5 = (bf16[1032,128]{1,0:T(8,128)(2,1)S(1)}, bf16[1032,128]{1,0:T(8,128)(2,1)S(1)}, u32[]{:S(2)}, u32[]{:S(2)}) collective-permute-start(bf16[1032,128]{1,0:T(8,128)(2,1)S(1)} %get-tuple-element.43.refs_3_), channel_id=1, source_target_pairs={{0,25},{1,24},{8,9},{9,8},{16,17},{17,16},{24,1},{25,0},{2,27},{3,... | collective-permute-start | bytes 792584 | tf_op jit(solution)/shard_map/ppermute | solution.py:588
  41.0 32.8 %collective-permute-start.17 = (bf16[1032,128]{1,0:T(8,128)(2,1)S(1)}, bf16[1032,128]{1,0:T(8,128)(2,1)S(1)}, u32[]{:S(2)}, u32[]{:S(2)}) collective-permute-start(bf16[1032,128]{1,0:T(8,128)(2,1)S(1)} %get-tuple-element.42.refs_2_), channel_id=1, source_target_pairs={{0,0},{1,1},{8,16},{9,17},{16,8},{17,9},{24,24},{25,25},{2,2},{3,3... | collective-permute-start | bytes 792584 | tf_op jit(solution)/shard_map/ppermute | solution.py:588
  41.7 33.7 %collective-permute-start.18 = (bf16[1032,128]{1,0:T(8,128)(2,1)S(1)}, bf16[1032,128]{1,0:T(8,128)(2,1)S(1)}, u32[]{:S(2)}, u32[]{:S(2)}) collective-permute-start(bf16[1032,128]{1,0:T(8,128)(2,1)S(1)} %get-tuple-element.43.refs_3_), channel_id=1, source_target_pairs={{0,1},{1,0},{8,17},{9,16},{16,9},{17,8},{24,25},{25,24},{2,3},{3,2... | collective-permute-start | bytes 792584 | tf_op jit(solution)/shard_map/ppermute | solution.py:588
  42.8 28.9 %collective-permute-start.6 = (bf16[1032,128]{1,0:T(8,128)(2,1)S(1)}, bf16[1032,128]{1,0:T(8,128)(2,1)S(1)}, u32[]{:S(2)}, u32[]{:S(2)}) collective-permute-start(bf16[1032,128]{1,0:T(8,128)(2,1)S(1)} %get-tuple-element.47), channel_id=1, source_target_pairs={{0,9},{1,8},{8,1},{9,0},{16,25},{17,24},{24,17},{25,16},{2,11},{3,... | collective-permute-start | bytes 792584 | tf_op jit(solution)/shard_map/ppermute | solution.py:588
  69.8 7.8 %collective-permute-start.15 = (f32[32,128]{1,0:T(8,128)S(1)}, f32[32,128]{1,0:T(8,128)S(1)}, u32[]{:S(2)}, u32[]{:S(2)}) collective-permute-start(f32[32,128]{1,0:T(8,128)S(1)} %get-tuple-element.56), channel_id=1, source_target_pairs={{0,0},{1,1},{8,16},{9,17},{16,8},{17,9},{24,24},{25,25},{2,2},{3,3... | collective-permute-start | bytes 49160 | tf_op jit(solution)/shard_map/ppermute | solution.py:588
  70.4 7.1 %collective-permute-start.16 = (f32[32,128]{1,0:T(8,128)S(1)}, f32[32,128]{1,0:T(8,128)S(1)}, u32[]{:S(2)}, u32[]{:S(2)}) collective-permute-start(f32[32,128]{1,0:T(8,128)S(1)} %get-tuple-element.57), channel_id=1, source_target_pairs={{0,1},{1,0},{8,17},{9,16},{16,9},{17,8},{24,25},{25,24},{2,3},{3,2... | collective-permute-start | bytes 49160 | tf_op jit(solution)/shard_map/ppermute | solution.py:588
  72.3 5.3 %collective-permute-start.7 = (f32[32,128]{1,0:T(8,128)S(1)}, f32[32,128]{1,0:T(8,128)S(1)}, u32[]{:S(2)}, u32[]{:S(2)}) collective-permute-start(f32[32,128]{1,0:T(8,128)S(1)} %get-tuple-element.49), channel_id=1, source_target_pairs={{0,2},{2,0},{4,6},{6,4},{1,3},{3,1},{5,7},{7,5},{8,10},{10,8},{12,... | collective-permute-start | bytes 49160 | tf_op jit(solution)/shard_map/ppermute | solution.py:418
  73.9 3.7 %collective-permute-start.8 = (f32[32,128]{1,0:T(8,128)S(1)}, f32[32,128]{1,0:T(8,128)S(1)}, u32[]{:S(2)}, u32[]{:S(2)}) collective-permute-start(f32[32,128]{1,0:T(8,128)S(1)} %get-tuple-element.50), channel_id=1, source_target_pairs={{0,4},{2,6},{4,0},{6,2},{1,5},{3,7},{5,1},{7,3},{8,12},{10,14},{12... | collective-permute-start | bytes 49160 | tf_op jit(solution)/shard_map/ppermute | solution.py:418
  75.4 4.6 %collective-permute-start.9 = (f32[32,128]{1,0:T(8,128)S(1)}, f32[32,128]{1,0:T(8,128)S(1)}, u32[]{:S(2)}, u32[]{:S(2)}) collective-permute-start(f32[32,128]{1,0:T(8,128)S(1)} %get-tuple-element.51), channel_id=1, source_target_pairs={{0,6},{2,4},{4,2},{6,0},{1,7},{3,5},{5,3},{7,1},{8,14},{10,12},{12... | collective-permute-start | bytes 49160 | tf_op jit(solution)/shard_map/ppermute | solution.py:418

commit v4 on v3

--- a/solution.py
+++ b/solution.py
@@ -183,7 +183,7 @@
     return jnp.concatenate(tiles, axis=0).astype(jnp.bfloat16)
 
 
-def attend(queries, keys, values, used, scale):
+def attend(queries, keys, values, used, scale, least=None):
     def tile(rows, n):
         return rows[n * SUBLANES : (n + 1) * SUBLANES]
 
@@ -200,6 +200,8 @@
     if used is not None:
         scores = jnp.where(used, scores, MASKED)
     top = jnp.max(scores, axis=1, keepdims=True)
+    if least is not None:
+        top = jnp.maximum(top, least)
     weights = jnp.exp(scores - top)
     if used is not None:
         weights = jnp.where(used, weights, 0.0)
@@ -285,14 +287,12 @@
     lines = layers * rows
     keys, values = image_columns(chunks, layers)
     queries = q_ref[...].reshape(lines, HEAD_DIM)
-    new_top, new_total, new_summed = attend(queries, keys, values, used, scale)
-    top = top_in[...].reshape(lines, LANES)[:, :1]
-    both = jnp.maximum(top, new_top)
-    old_factor = jnp.exp(top - both)
-    new_factor = jnp.exp(new_top - both)
-    total = old_factor * total_in[...].reshape(lines, LANES)[:, :1] + new_factor * new_total
-    summed = old_factor * sum_in[...].reshape(lines, LANES) + new_factor * new_summed
-    return both, total, summed
+    old_top = top_in[...].reshape(lines, LANES)[:, :1]
+    top, total, summed = attend(queries, keys, values, used, scale, old_top)
+    factor = jnp.exp(old_top - top)
+    total += factor * total_in[...].reshape(lines, LANES)[:, :1]
+    summed += factor * sum_in[...].reshape(lines, LANES)
+    return top, total, summed
 
 
 def pack_part(top, total, summed):

time: 81 us -> 81 us (level)
  no operation moved by 1% of the time
where the time goes in v4:
time: 81 us; the launch traced here: 80.7 us
  starting transfers between devices  45.5 us (56%)
  waiting for transfers between devices  21.6 us (27%)
  Pallas kernels  12.1 us (15%)
  between operations  1.45 us (2%)
    ppermute x13, starting transfers between devices, send(): return lax.ppermute(value, axes, some)  36.4 us
    ppermute x13, waiting for transfers between devices, send(): return lax.ppermute(value, axes, some)  12.7 us
    ppermute x6, starting transfers between devices, seq_exchange(): lax.ppermute(out, 'seq', [(s, s ^ k) for s in range(KV_HEADS)])  9.07 us
    ppermute x6, waiting for transfers between devices, seq_exchange(): lax.ppermute(out, 'seq', [(s, s ^ k) for s in range(KV_HEADS)])  8.94 us
    pallas_call x1, Pallas kernels, text_part(): pl.pallas_call(functools.partial(text_kernel, scale), out_shape=[jax.Shap...  4.64 us
    pallas_call x1, Pallas kernels, group_rows(): first_call(in_hbm(patch_map.reshape(1, src_rows)), in_hbm(image_places.re...  2.43 us
    pallas_call x1, Pallas kernels, place_rows(): pl.pallas_call(functools.partial(place_kernel, owners, outer), out_shape=...  1.67 us
  transfers between devices with their start and end apart: 19, of which 6 were waited for; matrix products, arithmetic and copies ran while one was open for 0% of the time, Pallas kernels for 11%

profile of v4, /device:TPU:0, one launch (start us, length us, event | category | flops | bytes accessed | tf_op | source)
XLA Modules:
  0.0 80.7 jit_solution(9025176021747440149)
XLA Ops:
  0.6 0.0 copy-start
  0.6 2.4 %group_first.1 = (bf16[256,256]{1,0:T(8,128)(2,1)S(1)}, bf16[8,256]{1,0:T(8,128)(2,1)S(1)}, bf16[4,256,1024]{2,1,0:T(8,128)(2,1)S(1)}, bf16[1032,128]{1,0:T(8,128)(2,1)S(1)}, bf16[1032,128]{1,0:T(8,128)(2,1)S(1)}) custom-call(s32[1,256]{1,0:T(1,128)} %bitcast.11, s32[1,256]{1,0:T(1,128)} %bitcast.12, bf16[4,256,1024]{2,1,0:T(8,128)(2,1)} %rows_hbm.1), custom_call_target="tpu_custom_call" | custom-call | flops 134217728 | bytes 2621440 | tf_op jit(solution)/shard_map/group_first/pallas_call | solution.py:156
  3.1 4.1 %collective-permute-start = (bf16[1032,128]{1,0:T(8,128)(2,1)S(1)}, bf16[1032,128]{1,0:T(8,128)(2,1)S(1)}, u32[]{:S(2)}, u32[]{:S(2)}) collective-permute-start(bf16[1032,128]{1,0:T(8,128)(2,1)S(1)} %get-tuple-element.34), channel_id=1, source_target_pairs={{0,16},{1,17},{8,24},{9,25},{16,0},{17,1},{24,8},{25,9},{2,18},{3,... | collective-permute-start | bytes 792584 | tf_op jit(solution)/shard_map/ppermute | solution.py:588
  7.2 0.0 collective-permute-start.1
  7.2 0.6 group_rest.1
  7.8 1.6 %collective-permute-start.2 = (bf16[1032,128]{1,0:T(8,128)(2,1)S(1)}, bf16[1032,128]{1,0:T(8,128)(2,1)S(1)}, u32[]{:S(2)}, u32[]{:S(2)}) collective-permute-start(bf16[1032,128]{1,0:T(8,128)(2,1)S(1)} %get-tuple-element.39), channel_id=1, source_target_pairs={{0,8},{1,9},{8,0},{9,1},{16,24},{17,25},{24,16},{25,17},{2,10},{3,... | collective-permute-start | bytes 792584 | tf_op jit(solution)/shard_map/ppermute | solution.py:588
  9.4 0.2 collective-permute-start.3
  9.6 0.7 collective-permute-start.10
  10.3 0.0 collective-permute-done.10.refs_0_
  10.3 0.4 collective-permute-start.11
  10.7 0.9 %collective-permute-done.11.refs_1_ = bf16[4,3584]{1,0:T(4,128)(2,1)S(1)} collective-permute-done((bf16[4,3584]{1,0:T(4,128)(2,1)S(1)}, bf16[4,3584]{1,0:T(4,128)(2,1)S(1)}, u32[]{:S(2)}, u32[]{:S(2)}) %collective-permute-start.11) | collective-permute-done | bytes 28704 | tf_op jit(solution)/shard_map/ppermute | solution.py:588
  11.6 0.5 shard_map.78
  12.1 1.6 %collective-permute-start.12 = (f32[64,128]{1,0:T(8,128)S(1)}, f32[64,128]{1,0:T(8,128)S(1)}, u32[]{:S(2)}, u32[]{:S(2)}) collective-permute-start(f32[64,128]{1,0:T(8,128)S(1)} %get-tuple-element.53), channel_id=1, source_target_pairs={{0,2},{2,0},{4,6},{6,4},{1,3},{3,1},{5,7},{7,5},{8,10},{10,8},{12,... | collective-permute-start | bytes 98312 | tf_op jit(solution)/shard_map/ppermute | solution.py:418
  13.6 2.4 %collective-permute-done.12.refs_1_ = f32[64,128]{1,0:T(8,128)S(1)} collective-permute-done((f32[64,128]{1,0:T(8,128)S(1)}, f32[64,128]{1,0:T(8,128)S(1)}, u32[]{:S(2)}, u32[]{:S(2)}) %collective-permute-start.12) | collective-permute-done | bytes 32800 | tf_op jit(solution)/shard_map/ppermute | solution.py:418
  16.0 1.5 %collective-permute-start.13 = (f32[64,128]{1,0:T(8,128)S(1)}, f32[64,128]{1,0:T(8,128)S(1)}, u32[]{:S(2)}, u32[]{:S(2)}) collective-permute-start(f32[64,128]{1,0:T(8,128)S(1)} %get-tuple-element.54), channel_id=1, source_target_pairs={{0,4},{2,6},{4,0},{6,2},{1,5},{3,7},{5,1},{7,3},{8,12},{10,14},{12... | collective-permute-start | bytes 98312 | tf_op jit(solution)/shard_map/ppermute | solution.py:418
  17.6 2.4 %collective-permute-done.13.refs_2_ = f32[64,128]{1,0:T(8,128)S(1)} collective-permute-done((f32[64,128]{1,0:T(8,128)S(1)}, f32[64,128]{1,0:T(8,128)S(1)}, u32[]{:S(2)}, u32[]{:S(2)}) %collective-permute-start.13) | collective-permute-done | bytes 32800 | tf_op jit(solution)/shard_map/ppermute | solution.py:418
  19.9 2.4 %collective-permute-start.14 = (f32[64,128]{1,0:T(8,128)S(1)}, f32[64,128]{1,0:T(8,128)S(1)}, u32[]{:S(2)}, u32[]{:S(2)}) collective-permute-start(f32[64,128]{1,0:T(8,128)S(1)} %get-tuple-element.55), channel_id=1, source_target_pairs={{0,6},{2,4},{4,2},{6,0},{1,7},{3,5},{5,3},{7,1},{8,14},{10,12},{12... | collective-permute-start | bytes 98312 | tf_op jit(solution)/shard_map/ppermute | solution.py:418
  23.1 1.7 %collective-permute-done.14.refs_3_ = f32[64,128]{1,0:T(8,128)S(1)} collective-permute-done((f32[64,128]{1,0:T(8,128)S(1)}, f32[64,128]{1,0:T(8,128)S(1)}, u32[]{:S(2)}, u32[]{:S(2)}) %collective-permute-start.14) | collective-permute-done | bytes 32800 | tf_op jit(solution)/shard_map/ppermute | solution.py:418
  24.8 4.4 %collective-permute-start.4 = (bf16[1032,128]{1,0:T(8,128)(2,1)S(1)}, bf16[1032,128]{1,0:T(8,128)(2,1)S(1)}, u32[]{:S(2)}, u32[]{:S(2)}) collective-permute-start(bf16[1032,128]{1,0:T(8,128)(2,1)S(1)} %get-tuple-element.42.refs_2_), channel_id=1, source_target_pairs={{0,24},{1,25},{8,8},{9,9},{16,16},{17,17},{24,0},{25,1},{2,26},{3,... | collective-permute-start | bytes 792584 | tf_op jit(solution)/shard_map/ppermute | solution.py:588
  29.1 0.0 collective-permute-done.refs_0_
  29.1 0.1 collective-permute-start.5
  29.2 11.8 %collective-permute-done.1.refs_1_ = bf16[1032,128]{1,0:T(8,128)(2,1)S(1)} collective-permute-done((bf16[1032,128]{1,0:T(8,128)(2,1)S(1)}, bf16[1032,128]{1,0:T(8,128)(2,1)S(1)}, u32[]{:S(2)}, u32[]{:S(2)}) %collective-permute-start.1) | collective-permute-done | bytes 264224 | tf_op jit(solution)/shard_map/ppermute | solution.py:588
  41.0 0.7 collective-permute-start.17
  41.7 0.0 collective-permute-done.2.refs_2_.refs_6_
  41.7 1.0 %collective-permute-start.18 = (bf16[1032,128]{1,0:T(8,128)(2,1)S(1)}, bf16[1032,128]{1,0:T(8,128)(2,1)S(1)}, u32[]{:S(2)}, u32[]{:S(2)}) collective-permute-start(bf16[1032,128]{1,0:T(8,128)(2,1)S(1)} %get-tuple-element.43.refs_3_), channel_id=1, source_target_pairs={{0,1},{1,0},{8,17},{9,16},{16,9},{17,8},{24,25},{25,24},{2,3},{3,2... | collective-permute-start | bytes 792584 | tf_op jit(solution)/shard_map/ppermute | solution.py:588
  42.8 0.0 collective-permute-done.3.refs_3_.refs_9_
  42.8 22.2 %collective-permute-start.6 = (bf16[1032,128]{1,0:T(8,128)(2,1)S(1)}, bf16[1032,128]{1,0:T(8,128)(2,1)S(1)}, u32[]{:S(2)}, u32[]{:S(2)}) collective-permute-start(bf16[1032,128]{1,0:T(8,128)(2,1)S(1)} %get-tuple-element.47), channel_id=1, source_target_pairs={{0,9},{1,8},{8,1},{9,0},{16,25},{17,24},{24,17},{25,16},{2,11},{3,... | collective-permute-start | bytes 792584 | tf_op jit(solution)/shard_map/ppermute | solution.py:588
  64.9 4.6 %text_part.1 = (bf16[4,32,128]{2,1,0:T(8,128)(2,1)S(1)}, f32[4,32,128]{2,1,0:T(8,128)S(1)}, f32[4,32,128]{2,1,0:T(8,128)S(1)}, f32[4,32,128]{2,1,0:T(8,128)S(1)}) custom-call(s32[1]{0:T(128)S(6)} %copy.10.len_ref, bf16[4,1,3584]{2,1,0:T(2,128)(2,1)S(1)} %copy.8.query_ref, bf16[4,1,768,1024]{3,2,1,0:T(8,128)(2,1)} %text_ref.1), custom_call_target="tpu_custom_call" | custom-call | flops 25769803776 | bytes 6291456 | tf_op jit(solution)/shard_map/text_part/pallas_call | solution.py:245
  69.6 0.2 merge_far.1
  69.8 0.0 collective-permute-done.4.refs_5_.refs_3_
  69.8 0.7 collective-permute-start.15
  70.4 0.0 collective-permute-done.5.refs_6_.refs_5_
  70.4 0.4 collective-permute-start.16
  70.8 0.9 %here_part.1 = (f32[4,32,128]{2,1,0:T(8,128)S(1)}, f32[4,32,128]{2,1,0:T(8,128)S(1)}, f32[4,32,128]{2,1,0:T(8,128)S(1)}) custom-call(bf16[4,32,128]{2,1,0:T(8,128)(2,1)S(1)} %get-tuple-element.30.q_ref, f32[4,32,128]{2,1,0:T(8,128)S(1)} %get-tuple-element.31.top_in, f32[4,32,128]{2,1,0:T(8,128)S(1)} %get-tuple-element.32.total_in, ...), custom_call_target="tpu_custom_call" | custom-call | flops 59179008 | bytes 1849344 | tf_op jit(solution)/shard_map/here_part/pallas_call | solution.py:360
  71.7 0.0 collective-permute-done.6.refs_0_.refs_7_
  71.7 0.5 shard_map.77
  72.3 1.6 %collective-permute-start.7 = (f32[32,128]{1,0:T(8,128)S(1)}, f32[32,128]{1,0:T(8,128)S(1)}, u32[]{:S(2)}, u32[]{:S(2)}) collective-permute-start(f32[32,128]{1,0:T(8,128)S(1)} %get-tuple-element.49), channel_id=1, source_target_pairs={{0,2},{2,0},{4,6},{6,4},{1,3},{3,1},{5,7},{7,5},{8,10},{10,8},{12,... | collective-permute-start | bytes 49160 | tf_op jit(solution)/shard_map/ppermute | solution.py:418
  73.8 0.0 collective-permute-done.17.refs_2_
  73.8 1.5 %collective-permute-start.8 = (f32[32,128]{1,0:T(8,128)S(1)}, f32[32,128]{1,0:T(8,128)S(1)}, u32[]{:S(2)}, u32[]{:S(2)}) collective-permute-start(f32[32,128]{1,0:T(8,128)S(1)} %get-tuple-element.50), channel_id=1, source_target_pairs={{0,4},{2,6},{4,0},{6,2},{1,5},{3,7},{5,1},{7,3},{8,12},{10,14},{12... | collective-permute-start | bytes 49160 | tf_op jit(solution)/shard_map/ppermute | solution.py:418
  75.3 0.0 collective-permute-done.18.refs_4_
  75.3 0.5 collective-permute-start.9
  75.8 1.7 %place_rows.1 = bf16[4,256,1024]{2,1,0:T(8,128)(2,1)} custom-call(bf16[1032,128]{1,0:T(8,128)(2,1)S(1)} %collective-permute-done.refs_0_, bf16[1032,128]{1,0:T(8,128)(2,1)S(1)} %collective-permute-done.1.refs_1_, bf16[1032,128]{1,0:T(8,128)(2,1)S(1)} %collective-permute-done.17.refs_2_, bf16[1032,128]{1,0:T(8,128)(2,1)S(1)} %collective-permute-done.4.refs_5_.refs_3_, ...), custom_call_target="tpu_custom_call" | custom-call | flops 536870912 | bytes 4194304 | tf_op jit(solution)/shard_map/place_rows/pallas_call | solution.py:503
  77.5 0.0 collective-permute-done.15.refs_4_
  77.5 0.0 collective-permute-done.16.refs_5_
  77.5 0.0 collective-permute-done.7.refs_1_
  77.5 0.0 collective-permute-done.8.refs_2_
  77.6 2.4 %collective-permute-done.9.refs_3_ = f32[32,128]{1,0:T(8,128)S(1)} collective-permute-done((f32[32,128]{1,0:T(8,128)S(1)}, f32[32,128]{1,0:T(8,128)S(1)}, u32[]{:S(2)}, u32[]{:S(2)}) %collective-permute-start.9) | collective-permute-done | bytes 16416 | tf_op jit(solution)/shard_map/ppermute | solution.py:418
  80.0 0.7 merge.1
  (2 shorter events, 0.0 us)
Async XLA Ops:
  0.6 9.0 %copy-start = (bf16[4,1,3584]{2,0,1:T(4,128)(2,1)S(1)}, bf16[4,1,3584]{2,0,1:T(4,128)(2,1)}, u32[]{:S(2)}) copy-start(bf16[4,1,3584]{2,0,1:T(4,128)(2,1)} %param.6) | copy-start | bytes 86020
  3.1 26.0 %collective-permute-start = (bf16[1032,128]{1,0:T(8,128)(2,1)S(1)}, bf16[1032,128]{1,0:T(8,128)(2,1)S(1)}, u32[]{:S(2)}, u32[]{:S(2)}) collective-permute-start(bf16[1032,128]{1,0:T(8,128)(2,1)S(1)} %get-tuple-element.34), channel_id=1, source_target_pairs={{0,16},{1,17},{8,24},{9,25},{16,0},{17,1},{24,8},{25,9},{2,18},{3,... | collective-permute-start | bytes 792584 | tf_op jit(solution)/shard_map/ppermute | solution.py:588
  7.2 33.8 %collective-permute-start.1 = (bf16[1032,128]{1,0:T(8,128)(2,1)S(1)}, bf16[1032,128]{1,0:T(8,128)(2,1)S(1)}, u32[]{:S(2)}, u32[]{:S(2)}) collective-permute-start(bf16[1032,128]{1,0:T(8,128)(2,1)S(1)} %get-tuple-element.35), channel_id=1, source_target_pairs={{0,17},{1,16},{8,25},{9,24},{16,1},{17,0},{24,9},{25,8},{2,19},{3,... | collective-permute-start | bytes 792584 | tf_op jit(solution)/shard_map/ppermute | solution.py:588
  7.8 33.9 %collective-permute-start.2 = (bf16[1032,128]{1,0:T(8,128)(2,1)S(1)}, bf16[1032,128]{1,0:T(8,128)(2,1)S(1)}, u32[]{:S(2)}, u32[]{:S(2)}) collective-permute-start(bf16[1032,128]{1,0:T(8,128)(2,1)S(1)} %get-tuple-element.39), channel_id=1, source_target_pairs={{0,8},{1,9},{8,0},{9,1},{16,24},{17,25},{24,16},{25,17},{2,10},{3,... | collective-permute-start | bytes 792584 | tf_op jit(solution)/shard_map/ppermute | solution.py:588
  9.4 33.3 %collective-permute-start.3 = (bf16[1032,128]{1,0:T(8,128)(2,1)S(1)}, bf16[1032,128]{1,0:T(8,128)(2,1)S(1)}, u32[]{:S(2)}, u32[]{:S(2)}) collective-permute-start(bf16[1032,128]{1,0:T(8,128)(2,1)S(1)} %get-tuple-element.40), channel_id=1, source_target_pairs={{0,1},{1,0},{8,9},{9,8},{16,17},{17,16},{24,25},{25,24},{2,3},{3,2... | collective-permute-start | bytes 792584 | tf_op jit(solution)/shard_map/ppermute | solution.py:588
  9.6 0.7 collective-permute-start.10
  10.3 1.3 %collective-permute-start.11 = (bf16[4,3584]{1,0:T(4,128)(2,1)S(1)}, bf16[4,3584]{1,0:T(4,128)(2,1)S(1)}, u32[]{:S(2)}, u32[]{:S(2)}) collective-permute-start(bf16[4,3584]{1,0:T(4,128)(2,1)S(1)} %bitcast.9), channel_id=1, source_target_pairs={{1,0},{0,1},{17,8},{16,9},{9,16},{8,17},{25,24},{24,25},{3,2},{2,3... | collective-permute-start | bytes 86024 | tf_op jit(solution)/shard_map/ppermute | solution.py:588
  12.1 4.0 %collective-permute-start.12 = (f32[64,128]{1,0:T(8,128)S(1)}, f32[64,128]{1,0:T(8,128)S(1)}, u32[]{:S(2)}, u32[]{:S(2)}) collective-permute-start(f32[64,128]{1,0:T(8,128)S(1)} %get-tuple-element.53), channel_id=1, source_target_pairs={{0,2},{2,0},{4,6},{6,4},{1,3},{3,1},{5,7},{7,5},{8,10},{10,8},{12,... | collective-permute-start | bytes 98312 | tf_op jit(solution)/shard_map/ppermute | solution.py:418
  16.0 3.9 %collective-permute-start.13 = (f32[64,128]{1,0:T(8,128)S(1)}, f32[64,128]{1,0:T(8,128)S(1)}, u32[]{:S(2)}, u32[]{:S(2)}) collective-permute-start(f32[64,128]{1,0:T(8,128)S(1)} %get-tuple-element.54), channel_id=1, source_target_pairs={{0,4},{2,6},{4,0},{6,2},{1,5},{3,7},{5,1},{7,3},{8,12},{10,14},{12... | collective-permute-start | bytes 98312 | tf_op jit(solution)/shard_map/ppermute | solution.py:418
  19.9 4.8 %collective-permute-start.14 = (f32[64,128]{1,0:T(8,128)S(1)}, f32[64,128]{1,0:T(8,128)S(1)}, u32[]{:S(2)}, u32[]{:S(2)}) collective-permute-start(f32[64,128]{1,0:T(8,128)S(1)} %get-tuple-element.55), channel_id=1, source_target_pairs={{0,6},{2,4},{4,2},{6,0},{1,7},{3,5},{5,3},{7,1},{8,14},{10,12},{12... | collective-permute-start | bytes 98312 | tf_op jit(solution)/shard_map/ppermute | solution.py:418
  24.8 45.0 %collective-permute-start.4 = (bf16[1032,128]{1,0:T(8,128)(2,1)S(1)}, bf16[1032,128]{1,0:T(8,128)(2,1)S(1)}, u32[]{:S(2)}, u32[]{:S(2)}) collective-permute-start(bf16[1032,128]{1,0:T(8,128)(2,1)S(1)} %get-tuple-element.42.refs_2_), channel_id=1, source_target_pairs={{0,24},{1,25},{8,8},{9,9},{16,16},{17,17},{24,0},{25,1},{2,26},{3,... | collective-permute-start | bytes 792584 | tf_op jit(solution)/shard_map/ppermute | solution.py:588
  29.1 41.3 %collective-permute-start.5 = (bf16[1032,128]{1,0:T(8,128)(2,1)S(1)}, bf16[1032,128]{1,0:T(8,128)(2,1)S(1)}, u32[]{:S(2)}, u32[]{:S(2)}) collective-permute-start(bf16[1032,128]{1,0:T(8,128)(2,1)S(1)} %get-tuple-element.43.refs_3_), channel_id=1, source_target_pairs={{0,25},{1,24},{8,9},{9,8},{16,17},{17,16},{24,1},{25,0},{2,27},{3,... | collective-permute-start | bytes 792584 | tf_op jit(solution)/shard_map/ppermute | solution.py:588
  41.0 32.8 %collective-permute-start.17 = (bf16[1032,128]{1,0:T(8,128)(2,1)S(1)}, bf16[1032,128]{1,0:T(8,128)(2,1)S(1)}, u32[]{:S(2)}, u32[]{:S(2)}) collective-permute-start(bf16[1032,128]{1,0:T(8,128)(2,1)S(1)} %get-tuple-element.42.refs_2_), channel_id=1, source_target_pairs={{0,0},{1,1},{8,16},{9,17},{16,8},{17,9},{24,24},{25,25},{2,2},{3,3... | collective-permute-start | bytes 792584 | tf_op jit(solution)/shard_map/ppermute | solution.py:588
  41.7 33.6 %collective-permute-start.18 = (bf16[1032,128]{1,0:T(8,128)(2,1)S(1)}, bf16[1032,128]{1,0:T(8,128)(2,1)S(1)}, u32[]{:S(2)}, u32[]{:S(2)}) collective-permute-start(bf16[1032,128]{1,0:T(8,128)(2,1)S(1)} %get-tuple-element.43.refs_3_), channel_id=1, source_target_pairs={{0,1},{1,0},{8,17},{9,16},{16,9},{17,8},{24,25},{25,24},{2,3},{3,2... | collective-permute-start | bytes 792584 | tf_op jit(solution)/shard_map/ppermute | solution.py:588
  42.8 29.0 %collective-permute-start.6 = (bf16[1032,128]{1,0:T(8,128)(2,1)S(1)}, bf16[1032,128]{1,0:T(8,128)(2,1)S(1)}, u32[]{:S(2)}, u32[]{:S(2)}) collective-permute-start(bf16[1032,128]{1,0:T(8,128)(2,1)S(1)} %get-tuple-element.47), channel_id=1, source_target_pairs={{0,9},{1,8},{8,1},{9,0},{16,25},{17,24},{24,17},{25,16},{2,11},{3,... | collective-permute-start | bytes 792584 | tf_op jit(solution)/shard_map/ppermute | solution.py:588
  69.8 7.7 %collective-permute-start.15 = (f32[32,128]{1,0:T(8,128)S(1)}, f32[32,128]{1,0:T(8,128)S(1)}, u32[]{:S(2)}, u32[]{:S(2)}) collective-permute-start(f32[32,128]{1,0:T(8,128)S(1)} %get-tuple-element.56), channel_id=1, source_target_pairs={{0,0},{1,1},{8,16},{9,17},{16,8},{17,9},{24,24},{25,25},{2,2},{3,3... | collective-permute-start | bytes 49160 | tf_op jit(solution)/shard_map/ppermute | solution.py:588
  70.4 7.1 %collective-permute-start.16 = (f32[32,128]{1,0:T(8,128)S(1)}, f32[32,128]{1,0:T(8,128)S(1)}, u32[]{:S(2)}, u32[]{:S(2)}) collective-permute-start(f32[32,128]{1,0:T(8,128)S(1)} %get-tuple-element.57), channel_id=1, source_target_pairs={{0,1},{1,0},{8,17},{9,16},{16,9},{17,8},{24,25},{25,24},{2,3},{3,2... | collective-permute-start | bytes 49160 | tf_op jit(solution)/shard_map/ppermute | solution.py:588
  72.3 5.3 %collective-permute-start.7 = (f32[32,128]{1,0:T(8,128)S(1)}, f32[32,128]{1,0:T(8,128)S(1)}, u32[]{:S(2)}, u32[]{:S(2)}) collective-permute-start(f32[32,128]{1,0:T(8,128)S(1)} %get-tuple-element.49), channel_id=1, source_target_pairs={{0,2},{2,0},{4,6},{6,4},{1,3},{3,1},{5,7},{7,5},{8,10},{10,8},{12,... | collective-permute-start | bytes 49160 | tf_op jit(solution)/shard_map/ppermute | solution.py:418
  73.8 3.7 %collective-permute-start.8 = (f32[32,128]{1,0:T(8,128)S(1)}, f32[32,128]{1,0:T(8,128)S(1)}, u32[]{:S(2)}, u32[]{:S(2)}) collective-permute-start(f32[32,128]{1,0:T(8,128)S(1)} %get-tuple-element.50), channel_id=1, source_target_pairs={{0,4},{2,6},{4,0},{6,2},{1,5},{3,7},{5,1},{7,3},{8,12},{10,14},{12... | collective-permute-start | bytes 49160 | tf_op jit(solution)/shard_map/ppermute | solution.py:418
  75.3 4.6 %collective-permute-start.9 = (f32[32,128]{1,0:T(8,128)S(1)}, f32[32,128]{1,0:T(8,128)S(1)}, u32[]{:S(2)}, u32[]{:S(2)}) collective-permute-start(f32[32,128]{1,0:T(8,128)S(1)} %get-tuple-element.51), channel_id=1, source_target_pairs={{0,6},{2,4},{4,2},{6,0},{1,7},{3,5},{5,3},{7,1},{8,14},{10,12},{12... | collective-permute-start | bytes 49160 | tf_op jit(solution)/shard_map/ppermute | solution.py:418

commit v5 on v4

--- a/solution.py
+++ b/solution.py
@@ -140,16 +140,16 @@
             jax.ShapeDtypeStruct((SUBLANES, src_rows), jnp.bfloat16),
             jax.ShapeDtypeStruct(image_rows.shape, jnp.bfloat16),
         ]
-        + [chunk] * req_count,
+        + [chunk],
         in_specs=[hbm] * 3,
-        out_specs=[vmem] * (3 + req_count),
+        out_specs=[vmem] * 4,
         scratch_shapes=[
             pltpu.VMEM((1, src_rows), jnp.int32),
             pltpu.VMEM((1, src_rows), jnp.int32),
             pltpu.SemaphoreType.DMA((2,)),
             pltpu.SemaphoreType.DMA((layers,)),
         ],
-        cost_estimate=cost(req_count),
+        cost_estimate=cost(1),
         compiler_params=pltpu.CompilerParams(vmem_limit_bytes=VMEM_LIMIT),
         name="group_first",
     )
@@ -159,11 +159,11 @@
         in_hbm(image_rows),
     )
     rest_call = pl.pallas_call(
-        functools.partial(rest_kernel, req_count, per),
-        out_shape=[chunk] * (groups - req_count),
+        functools.partial(rest_kernel, 1, per),
+        out_shape=[chunk] * (groups - 1),
         in_specs=[vmem] * 3,
-        out_specs=[vmem] * (groups - req_count),
-        cost_estimate=cost(groups - req_count),
+        out_specs=[vmem] * (groups - 1),
+        cost_estimate=cost(groups - 1),
         compiler_params=pltpu.CompilerParams(vmem_limit_bytes=VMEM_LIMIT),
         name="group_rest",
     )
@@ -415,9 +415,8 @@
 
 def seq_exchange(outs):
     arrived = [
-        lax.ppermute(out, "seq", [(s, s ^ k) for s in range(KV_HEADS)])
-        for k, out in enumerate(outs)
-        if k
+        lax.ppermute(outs[k], "seq", [(s, s ^ k) for s in range(KV_HEADS)])
+        for k in range(KV_HEADS - 1, 0, -1)
     ]
     return [outs[0], *arrived]
 

time: 81 us -> 80 us (0.988)
  waiting for transfers between devices: 21.6 us -> 20.6 us
    ppermute x6, waiting for transfers between devices: 8.94 us -> 7.98 us  [seq_exchange(): lax.ppermute(outs[k], 'seq', [(s, s ^ k) for s in range(KV_HEADS)])]
  transfers between devices with their start and end apart: 19 -> 19, of which waited for: 6 -> 7; matrix products, arithmetic and copies ran while one was open for 0% -> 0% of each run, Pallas kernels for 11% -> 11%
where the time goes in v5:
time: 80 us; the launch traced here: 79.7 us
  starting transfers between devices  45.5 us (57%)
  waiting for transfers between devices  20.6 us (26%)
  Pallas kernels  12.2 us (15%)
  between operations  1.46 us (2%)
    ppermute x13, starting transfers between devices, send(): return lax.ppermute(value, axes, some)  36.4 us
    ppermute x13, waiting for transfers between devices, send(): return lax.ppermute(value, axes, some)  12.6 us
    ppermute x6, starting transfers between devices, seq_exchange(): lax.ppermute(outs[k], 'seq', [(s, s ^ k) for s in range(KV_HEADS)])  9.08 us
    ppermute x6, waiting for transfers between devices, seq_exchange(): lax.ppermute(outs[k], 'seq', [(s, s ^ k) for s in range(KV_HEADS)])  7.98 us
    pallas_call x1, Pallas kernels, text_part(): pl.pallas_call(functools.partial(text_kernel, scale), out_shape=[jax.Shap...  4.64 us
    pallas_call x1, Pallas kernels, group_rows(): first_call(in_hbm(patch_map.reshape(1, src_rows)), in_hbm(image_places.re...  2.4 us
    pallas_call x1, Pallas kernels, place_rows(): pl.pallas_call(functools.partial(place_kernel, owners, outer), out_shape=...  1.68 us
  transfers between devices with their start and end apart: 19, of which 7 were waited for; matrix products, arithmetic and copies ran while one was open for 0% of the time, Pallas kernels for 11%

profile of v5, /device:TPU:0, one launch (start us, length us, event | category | flops | bytes accessed | tf_op | source)
XLA Modules:
  0.0 79.7 jit_solution(1559789852747143118)
XLA Ops:
  0.6 0.0 copy-start
  0.6 2.4 %group_first.1 = (bf16[256,256]{1,0:T(8,128)(2,1)S(1)}, bf16[8,256]{1,0:T(8,128)(2,1)S(1)}, bf16[4,256,1024]{2,1,0:T(8,128)(2,1)S(1)}, bf16[1032,128]{1,0:T(8,128)(2,1)S(1)}) custom-call(s32[1,256]{1,0:T(1,128)} %bitcast.11, s32[1,256]{1,0:T(1,128)} %bitcast.12, bf16[4,256,1024]{2,1,0:T(8,128)(2,1)} %rows_hbm.1), custom_call_target="tpu_custom_call" | custom-call | flops 67108864 | bytes 2359296 | tf_op jit(solution)/shard_map/group_first/pallas_call | solution.py:156
  3.0 4.1 %collective-permute-start = (bf16[1032,128]{1,0:T(8,128)(2,1)S(1)}, bf16[1032,128]{1,0:T(8,128)(2,1)S(1)}, u32[]{:S(2)}, u32[]{:S(2)}) collective-permute-start(bf16[1032,128]{1,0:T(8,128)(2,1)S(1)} %get-tuple-element.34), channel_id=1, source_target_pairs={{0,16},{1,17},{8,24},{9,25},{16,0},{17,1},{24,8},{25,9},{2,18},{3,... | collective-permute-start | bytes 792584 | tf_op jit(solution)/shard_map/ppermute | solution.py:587
  7.2 0.6 group_rest.1
  7.8 0.1 collective-permute-start.1
  7.9 1.6 %collective-permute-start.2 = (bf16[1032,128]{1,0:T(8,128)(2,1)S(1)}, bf16[1032,128]{1,0:T(8,128)(2,1)S(1)}, u32[]{:S(2)}, u32[]{:S(2)}) collective-permute-start(bf16[1032,128]{1,0:T(8,128)(2,1)S(1)} %get-tuple-element.39), channel_id=1, source_target_pairs={{0,8},{1,9},{8,0},{9,1},{16,24},{17,25},{24,16},{25,17},{2,10},{3,... | collective-permute-start | bytes 792584 | tf_op jit(solution)/shard_map/ppermute | solution.py:587
  9.5 0.1 collective-permute-start.3
  9.6 0.7 collective-permute-start.10
  10.3 0.0 collective-permute-done.10.refs_0_
  10.3 0.5 collective-permute-start.11
  10.8 0.9 %collective-permute-done.11.refs_1_ = bf16[4,3584]{1,0:T(4,128)(2,1)S(1)} collective-permute-done((bf16[4,3584]{1,0:T(4,128)(2,1)S(1)}, bf16[4,3584]{1,0:T(4,128)(2,1)S(1)}, u32[]{:S(2)}, u32[]{:S(2)}) %collective-permute-start.11) | collective-permute-done | bytes 28704 | tf_op jit(solution)/shard_map/ppermute | solution.py:587
  11.7 0.5 shard_map.78
  12.1 2.5 %collective-permute-start.12 = (f32[64,128]{1,0:T(8,128)S(1)}, f32[64,128]{1,0:T(8,128)S(1)}, u32[]{:S(2)}, u32[]{:S(2)}) collective-permute-start(f32[64,128]{1,0:T(8,128)S(1)} %get-tuple-element.53), channel_id=1, source_target_pairs={{0,6},{2,4},{4,2},{6,0},{1,7},{3,5},{5,3},{7,1},{8,14},{10,12},{12... | collective-permute-start | bytes 98312 | tf_op jit(solution)/shard_map/ppermute | solution.py:418
  14.6 2.4 %collective-permute-done.12.refs_1_ = f32[64,128]{1,0:T(8,128)S(1)} collective-permute-done((f32[64,128]{1,0:T(8,128)S(1)}, f32[64,128]{1,0:T(8,128)S(1)}, u32[]{:S(2)}, u32[]{:S(2)}) %collective-permute-start.12) | collective-permute-done | bytes 32800 | tf_op jit(solution)/shard_map/ppermute | solution.py:418
  17.0 1.5 %collective-permute-start.13 = (f32[64,128]{1,0:T(8,128)S(1)}, f32[64,128]{1,0:T(8,128)S(1)}, u32[]{:S(2)}, u32[]{:S(2)}) collective-permute-start(f32[64,128]{1,0:T(8,128)S(1)} %get-tuple-element.54), channel_id=1, source_target_pairs={{0,4},{2,6},{4,0},{6,2},{1,5},{3,7},{5,1},{7,3},{8,12},{10,14},{12... | collective-permute-start | bytes 98312 | tf_op jit(solution)/shard_map/ppermute | solution.py:418
  18.5 2.4 %collective-permute-done.13.refs_2_ = f32[64,128]{1,0:T(8,128)S(1)} collective-permute-done((f32[64,128]{1,0:T(8,128)S(1)}, f32[64,128]{1,0:T(8,128)S(1)}, u32[]{:S(2)}, u32[]{:S(2)}) %collective-permute-start.13) | collective-permute-done | bytes 32800 | tf_op jit(solution)/shard_map/ppermute | solution.py:418
  20.9 1.5 %collective-permute-start.14 = (f32[64,128]{1,0:T(8,128)S(1)}, f32[64,128]{1,0:T(8,128)S(1)}, u32[]{:S(2)}, u32[]{:S(2)}) collective-permute-start(f32[64,128]{1,0:T(8,128)S(1)} %get-tuple-element.55), channel_id=1, source_target_pairs={{0,2},{2,0},{4,6},{6,4},{1,3},{3,1},{5,7},{7,5},{8,10},{10,8},{12,... | collective-permute-start | bytes 98312 | tf_op jit(solution)/shard_map/ppermute | solution.py:418
  23.1 1.7 %collective-permute-done.14.refs_3_ = f32[64,128]{1,0:T(8,128)S(1)} collective-permute-done((f32[64,128]{1,0:T(8,128)S(1)}, f32[64,128]{1,0:T(8,128)S(1)}, u32[]{:S(2)}, u32[]{:S(2)}) %collective-permute-start.14) | collective-permute-done | bytes 32800 | tf_op jit(solution)/shard_map/ppermute | solution.py:418
  24.8 4.3 %collective-permute-start.4 = (bf16[1032,128]{1,0:T(8,128)(2,1)S(1)}, bf16[1032,128]{1,0:T(8,128)(2,1)S(1)}, u32[]{:S(2)}, u32[]{:S(2)}) collective-permute-start(bf16[1032,128]{1,0:T(8,128)(2,1)S(1)} %get-tuple-element.42.refs_2_), channel_id=1, source_target_pairs={{0,24},{1,25},{8,8},{9,9},{16,16},{17,17},{24,0},{25,1},{2,26},{3,... | collective-permute-start | bytes 792584 | tf_op jit(solution)/shard_map/ppermute | solution.py:587
  29.2 0.0 collective-permute-done.refs_0_
  29.2 0.1 collective-permute-start.5
  29.2 11.7 %collective-permute-done.1.refs_1_ = bf16[1032,128]{1,0:T(8,128)(2,1)S(1)} collective-permute-done((bf16[1032,128]{1,0:T(8,128)(2,1)S(1)}, bf16[1032,128]{1,0:T(8,128)(2,1)S(1)}, u32[]{:S(2)}, u32[]{:S(2)}) %collective-permute-start.1) | collective-permute-done | bytes 264224 | tf_op jit(solution)/shard_map/ppermute | solution.py:587
  41.0 0.7 collective-permute-start.17
  41.6 0.0 collective-permute-done.2.refs_2_.refs_6_
  41.7 1.0 %collective-permute-start.18 = (bf16[1032,128]{1,0:T(8,128)(2,1)S(1)}, bf16[1032,128]{1,0:T(8,128)(2,1)S(1)}, u32[]{:S(2)}, u32[]{:S(2)}) collective-permute-start(bf16[1032,128]{1,0:T(8,128)(2,1)S(1)} %get-tuple-element.43.refs_3_), channel_id=1, source_target_pairs={{0,1},{1,0},{8,17},{9,16},{16,9},{17,8},{24,25},{25,24},{2,3},{3,2... | collective-permute-start | bytes 792584 | tf_op jit(solution)/shard_map/ppermute | solution.py:587
  42.7 0.0 collective-permute-done.3.refs_3_.refs_9_
  42.7 22.2 %collective-permute-start.6 = (bf16[1032,128]{1,0:T(8,128)(2,1)S(1)}, bf16[1032,128]{1,0:T(8,128)(2,1)S(1)}, u32[]{:S(2)}, u32[]{:S(2)}) collective-permute-start(bf16[1032,128]{1,0:T(8,128)(2,1)S(1)} %get-tuple-element.47), channel_id=1, source_target_pairs={{0,9},{1,8},{8,1},{9,0},{16,25},{17,24},{24,17},{25,16},{2,11},{3,... | collective-permute-start | bytes 792584 | tf_op jit(solution)/shard_map/ppermute | solution.py:587
  64.9 4.6 %text_part.1 = (bf16[4,32,128]{2,1,0:T(8,128)(2,1)S(1)}, f32[4,32,128]{2,1,0:T(8,128)S(1)}, f32[4,32,128]{2,1,0:T(8,128)S(1)}, f32[4,32,128]{2,1,0:T(8,128)S(1)}) custom-call(s32[1]{0:T(128)S(6)} %copy.10.len_ref, bf16[4,1,3584]{2,1,0:T(2,128)(2,1)S(1)} %copy.8.query_ref, bf16[4,1,768,1024]{3,2,1,0:T(8,128)(2,1)} %text_ref.1), custom_call_target="tpu_custom_call" | custom-call | flops 25769803776 | bytes 6291456 | tf_op jit(solution)/shard_map/text_part/pallas_call | solution.py:245
  69.5 0.2 merge_far.1
  69.7 0.0 collective-permute-done.4.refs_5_.refs_3_
  69.7 0.7 collective-permute-start.15
  70.4 0.0 collective-permute-done.5.refs_6_.refs_5_
  70.4 0.4 collective-permute-start.16
  70.8 0.9 %here_part.1 = (f32[4,32,128]{2,1,0:T(8,128)S(1)}, f32[4,32,128]{2,1,0:T(8,128)S(1)}, f32[4,32,128]{2,1,0:T(8,128)S(1)}) custom-call(bf16[4,32,128]{2,1,0:T(8,128)(2,1)S(1)} %get-tuple-element.30.q_ref, f32[4,32,128]{2,1,0:T(8,128)S(1)} %get-tuple-element.31.top_in, f32[4,32,128]{2,1,0:T(8,128)S(1)} %get-tuple-element.32.total_in, ...), custom_call_target="tpu_custom_call" | custom-call | flops 59179008 | bytes 1849344 | tf_op jit(solution)/shard_map/here_part/pallas_call | solution.py:360
  71.7 0.0 collective-permute-done.6.refs_0_.refs_7_
  71.7 0.5 shard_map.77
  72.2 2.5 %collective-permute-start.7 = (f32[32,128]{1,0:T(8,128)S(1)}, f32[32,128]{1,0:T(8,128)S(1)}, u32[]{:S(2)}, u32[]{:S(2)}) collective-permute-start(f32[32,128]{1,0:T(8,128)S(1)} %get-tuple-element.49), channel_id=1, source_target_pairs={{0,6},{2,4},{4,2},{6,0},{1,7},{3,5},{5,3},{7,1},{8,14},{10,12},{12... | collective-permute-start | bytes 49160 | tf_op jit(solution)/shard_map/ppermute | solution.py:418
  74.7 0.0 collective-permute-done.17.refs_2_
  74.7 0.5 collective-permute-start.8
  75.3 0.0 collective-permute-done.18.refs_4_
  75.3 0.5 collective-permute-start.9
  75.8 1.7 %place_rows.1 = bf16[4,256,1024]{2,1,0:T(8,128)(2,1)} custom-call(bf16[1032,128]{1,0:T(8,128)(2,1)S(1)} %collective-permute-done.refs_0_, bf16[1032,128]{1,0:T(8,128)(2,1)S(1)} %collective-permute-done.1.refs_1_, bf16[1032,128]{1,0:T(8,128)(2,1)S(1)} %collective-permute-done.17.refs_2_, bf16[1032,128]{1,0:T(8,128)(2,1)S(1)} %collective-permute-done.4.refs_5_.refs_3_, ...), custom_call_target="tpu_custom_call" | custom-call | flops 536870912 | bytes 4194304 | tf_op jit(solution)/shard_map/place_rows/pallas_call | solution.py:502
  77.5 0.0 collective-permute-done.15.refs_4_
  77.5 0.0 collective-permute-done.16.refs_5_
  77.5 0.0 collective-permute-done.7.refs_1_
  77.5 1.0 %collective-permute-done.8.refs_2_ = f32[32,128]{1,0:T(8,128)S(1)} collective-permute-done((f32[32,128]{1,0:T(8,128)S(1)}, f32[32,128]{1,0:T(8,128)S(1)}, u32[]{:S(2)}, u32[]{:S(2)}) %collective-permute-start.8) | collective-permute-done | bytes 16416 | tf_op jit(solution)/shard_map/ppermute | solution.py:418
  78.5 0.5 collective-permute-done.9.refs_3_
  79.0 0.7 merge.1
  (2 shorter events, 0.0 us)
Async XLA Ops:
  0.6 9.0 %copy-start = (bf16[4,1,3584]{2,0,1:T(4,128)(2,1)S(1)}, bf16[4,1,3584]{2,0,1:T(4,128)(2,1)}, u32[]{:S(2)}) copy-start(bf16[4,1,3584]{2,0,1:T(4,128)(2,1)} %param.6) | copy-start | bytes 86020
  3.0 26.1 %collective-permute-start = (bf16[1032,128]{1,0:T(8,128)(2,1)S(1)}, bf16[1032,128]{1,0:T(8,128)(2,1)S(1)}, u32[]{:S(2)}, u32[]{:S(2)}) collective-permute-start(bf16[1032,128]{1,0:T(8,128)(2,1)S(1)} %get-tuple-element.34), channel_id=1, source_target_pairs={{0,16},{1,17},{8,24},{9,25},{16,0},{17,1},{24,8},{25,9},{2,18},{3,... | collective-permute-start | bytes 792584 | tf_op jit(solution)/shard_map/ppermute | solution.py:587
  7.8 33.1 %collective-permute-start.1 = (bf16[1032,128]{1,0:T(8,128)(2,1)S(1)}, bf16[1032,128]{1,0:T(8,128)(2,1)S(1)}, u32[]{:S(2)}, u32[]{:S(2)}) collective-permute-start(bf16[1032,128]{1,0:T(8,128)(2,1)S(1)} %get-tuple-element.38), channel_id=1, source_target_pairs={{0,17},{1,16},{8,25},{9,24},{16,1},{17,0},{24,9},{25,8},{2,19},{3,... | collective-permute-start | bytes 792584 | tf_op jit(solution)/shard_map/ppermute | solution.py:587
  7.9 33.7 %collective-permute-start.2 = (bf16[1032,128]{1,0:T(8,128)(2,1)S(1)}, bf16[1032,128]{1,0:T(8,128)(2,1)S(1)}, u32[]{:S(2)}, u32[]{:S(2)}) collective-permute-start(bf16[1032,128]{1,0:T(8,128)(2,1)S(1)} %get-tuple-element.39), channel_id=1, source_target_pairs={{0,8},{1,9},{8,0},{9,1},{16,24},{17,25},{24,16},{25,17},{2,10},{3,... | collective-permute-start | bytes 792584 | tf_op jit(solution)/shard_map/ppermute | solution.py:587
  9.5 33.2 %collective-permute-start.3 = (bf16[1032,128]{1,0:T(8,128)(2,1)S(1)}, bf16[1032,128]{1,0:T(8,128)(2,1)S(1)}, u32[]{:S(2)}, u32[]{:S(2)}) collective-permute-start(bf16[1032,128]{1,0:T(8,128)(2,1)S(1)} %get-tuple-element.40), channel_id=1, source_target_pairs={{0,1},{1,0},{8,9},{9,8},{16,17},{17,16},{24,25},{25,24},{2,3},{3,2... | collective-permute-start | bytes 792584 | tf_op jit(solution)/shard_map/ppermute | solution.py:587
  9.6 0.7 collective-permute-start.10
  10.3 1.3 %collective-permute-start.11 = (bf16[4,3584]{1,0:T(4,128)(2,1)S(1)}, bf16[4,3584]{1,0:T(4,128)(2,1)S(1)}, u32[]{:S(2)}, u32[]{:S(2)}) collective-permute-start(bf16[4,3584]{1,0:T(4,128)(2,1)S(1)} %bitcast.9), channel_id=1, source_target_pairs={{1,0},{0,1},{17,8},{16,9},{9,16},{8,17},{25,24},{24,25},{3,2},{2,3... | collective-permute-start | bytes 86024 | tf_op jit(solution)/shard_map/ppermute | solution.py:587
  12.1 4.9 %collective-permute-start.12 = (f32[64,128]{1,0:T(8,128)S(1)}, f32[64,128]{1,0:T(8,128)S(1)}, u32[]{:S(2)}, u32[]{:S(2)}) collective-permute-start(f32[64,128]{1,0:T(8,128)S(1)} %get-tuple-element.53), channel_id=1, source_target_pairs={{0,6},{2,4},{4,2},{6,0},{1,7},{3,5},{5,3},{7,1},{8,14},{10,12},{12... | collective-permute-start | bytes 98312 | tf_op jit(solution)/shard_map/ppermute | solution.py:418
  17.0 3.9 %collective-permute-start.13 = (f32[64,128]{1,0:T(8,128)S(1)}, f32[64,128]{1,0:T(8,128)S(1)}, u32[]{:S(2)}, u32[]{:S(2)}) collective-permute-start(f32[64,128]{1,0:T(8,128)S(1)} %get-tuple-element.54), channel_id=1, source_target_pairs={{0,4},{2,6},{4,0},{6,2},{1,5},{3,7},{5,1},{7,3},{8,12},{10,14},{12... | collective-permute-start | bytes 98312 | tf_op jit(solution)/shard_map/ppermute | solution.py:418
  20.9 3.9 %collective-permute-start.14 = (f32[64,128]{1,0:T(8,128)S(1)}, f32[64,128]{1,0:T(8,128)S(1)}, u32[]{:S(2)}, u32[]{:S(2)}) collective-permute-start(f32[64,128]{1,0:T(8,128)S(1)} %get-tuple-element.55), channel_id=1, source_target_pairs={{0,2},{2,0},{4,6},{6,4},{1,3},{3,1},{5,7},{7,5},{8,10},{10,8},{12,... | collective-permute-start | bytes 98312 | tf_op jit(solution)/shard_map/ppermute | solution.py:418
  24.8 44.9 %collective-permute-start.4 = (bf16[1032,128]{1,0:T(8,128)(2,1)S(1)}, bf16[1032,128]{1,0:T(8,128)(2,1)S(1)}, u32[]{:S(2)}, u32[]{:S(2)}) collective-permute-start(bf16[1032,128]{1,0:T(8,128)(2,1)S(1)} %get-tuple-element.42.refs_2_), channel_id=1, source_target_pairs={{0,24},{1,25},{8,8},{9,9},{16,16},{17,17},{24,0},{25,1},{2,26},{3,... | collective-permute-start | bytes 792584 | tf_op jit(solution)/shard_map/ppermute | solution.py:587
  29.2 41.2 %collective-permute-start.5 = (bf16[1032,128]{1,0:T(8,128)(2,1)S(1)}, bf16[1032,128]{1,0:T(8,128)(2,1)S(1)}, u32[]{:S(2)}, u32[]{:S(2)}) collective-permute-start(bf16[1032,128]{1,0:T(8,128)(2,1)S(1)} %get-tuple-element.43.refs_3_), channel_id=1, source_target_pairs={{0,25},{1,24},{8,9},{9,8},{16,17},{17,16},{24,1},{25,0},{2,27},{3,... | collective-permute-start | bytes 792584 | tf_op jit(solution)/shard_map/ppermute | solution.py:587
  41.0 33.8 %collective-permute-start.17 = (bf16[1032,128]{1,0:T(8,128)(2,1)S(1)}, bf16[1032,128]{1,0:T(8,128)(2,1)S(1)}, u32[]{:S(2)}, u32[]{:S(2)}) collective-permute-start(bf16[1032,128]{1,0:T(8,128)(2,1)S(1)} %get-tuple-element.42.refs_2_), channel_id=1, source_target_pairs={{0,0},{1,1},{8,16},{9,17},{16,8},{17,9},{24,24},{25,25},{2,2},{3,3... | collective-permute-start | bytes 792584 | tf_op jit(solution)/shard_map/ppermute | solution.py:587
  41.7 33.6 %collective-permute-start.18 = (bf16[1032,128]{1,0:T(8,128)(2,1)S(1)}, bf16[1032,128]{1,0:T(8,128)(2,1)S(1)}, u32[]{:S(2)}, u32[]{:S(2)}) collective-permute-start(bf16[1032,128]{1,0:T(8,128)(2,1)S(1)} %get-tuple-element.43.refs_3_), channel_id=1, source_target_pairs={{0,1},{1,0},{8,17},{9,16},{16,9},{17,8},{24,25},{25,24},{2,3},{3,2... | collective-permute-start | bytes 792584 | tf_op jit(solution)/shard_map/ppermute | solution.py:587
  42.7 29.0 %collective-permute-start.6 = (bf16[1032,128]{1,0:T(8,128)(2,1)S(1)}, bf16[1032,128]{1,0:T(8,128)(2,1)S(1)}, u32[]{:S(2)}, u32[]{:S(2)}) collective-permute-start(bf16[1032,128]{1,0:T(8,128)(2,1)S(1)} %get-tuple-element.47), channel_id=1, source_target_pairs={{0,9},{1,8},{8,1},{9,0},{16,25},{17,24},{24,17},{25,16},{2,11},{3,... | collective-permute-start | bytes 792584 | tf_op jit(solution)/shard_map/ppermute | solution.py:587
  69.7 7.8 %collective-permute-start.15 = (f32[32,128]{1,0:T(8,128)S(1)}, f32[32,128]{1,0:T(8,128)S(1)}, u32[]{:S(2)}, u32[]{:S(2)}) collective-permute-start(f32[32,128]{1,0:T(8,128)S(1)} %get-tuple-element.56), channel_id=1, source_target_pairs={{0,0},{1,1},{8,16},{9,17},{16,8},{17,9},{24,24},{25,25},{2,2},{3,3... | collective-permute-start | bytes 49160 | tf_op jit(solution)/shard_map/ppermute | solution.py:587
  70.4 7.1 %collective-permute-start.16 = (f32[32,128]{1,0:T(8,128)S(1)}, f32[32,128]{1,0:T(8,128)S(1)}, u32[]{:S(2)}, u32[]{:S(2)}) collective-permute-start(f32[32,128]{1,0:T(8,128)S(1)} %get-tuple-element.57), channel_id=1, source_target_pairs={{0,1},{1,0},{8,17},{9,16},{16,9},{17,8},{24,25},{25,24},{2,3},{3,2... | collective-permute-start | bytes 49160 | tf_op jit(solution)/shard_map/ppermute | solution.py:587
  72.2 5.3 %collective-permute-start.7 = (f32[32,128]{1,0:T(8,128)S(1)}, f32[32,128]{1,0:T(8,128)S(1)}, u32[]{:S(2)}, u32[]{:S(2)}) collective-permute-start(f32[32,128]{1,0:T(8,128)S(1)} %get-tuple-element.49), channel_id=1, source_target_pairs={{0,6},{2,4},{4,2},{6,0},{1,7},{3,5},{5,3},{7,1},{8,14},{10,12},{12... | collective-permute-start | bytes 49160 | tf_op jit(solution)/shard_map/ppermute | solution.py:418
  74.7 3.7 %collective-permute-start.8 = (f32[32,128]{1,0:T(8,128)S(1)}, f32[32,128]{1,0:T(8,128)S(1)}, u32[]{:S(2)}, u32[]{:S(2)}) collective-permute-start(f32[32,128]{1,0:T(8,128)S(1)} %get-tuple-element.50), channel_id=1, source_target_pairs={{0,4},{2,6},{4,0},{6,2},{1,5},{3,7},{5,1},{7,3},{8,12},{10,14},{12... | collective-permute-start | bytes 49160 | tf_op jit(solution)/shard_map/ppermute | solution.py:418
  75.3 3.7 %collective-permute-start.9 = (f32[32,128]{1,0:T(8,128)S(1)}, f32[32,128]{1,0:T(8,128)S(1)}, u32[]{:S(2)}, u32[]{:S(2)}) collective-permute-start(f32[32,128]{1,0:T(8,128)S(1)} %get-tuple-element.51), channel_id=1, source_target_pairs={{0,2},{2,0},{4,6},{6,4},{1,3},{3,1},{5,7},{7,5},{8,10},{10,8},{12,... | collective-permute-start | bytes 49160 | tf_op jit(solution)/shard_map/ppermute | solution.py:418
